TPU v7x, 32 devices: a 4x2x2 block of a 4x4x8 slice. The times are simulated.
32 devices in a mesh: dp: 4 (over y, z), tp: 8 (over x, core).
Axes of the slice: x: 4, y: 2, z: 2, core: 2. Of those that a mesh axis runs over, the one named last changes fastest.
The devices are a block of a 4x4x8 slice.
Arguments:
- x_in: bfloat16 [8192, 2048], P(('dp', 'tp')), parts along dimension 0
- grad_y: bfloat16 [8192, 2048], P(('dp', 'tp')), parts along dimension 0
- norm_gain: float32 [2, 2048], replicated
- w_qkv: bfloat16 [2, 2048, 6144], P(None, None, 'tp')
- w_out: bfloat16 [2, 2048, 2048], P(None, 'tp')
- w_gate: bfloat16 [2, 2048, 8192], P(None, None, 'tp')
- w_up: bfloat16 [2, 2048, 8192], P(None, None, 'tp')
- w_down: bfloat16 [2, 8192, 2048], P(None, 'tp')
Outputs:
- output 1: bfloat16 [8192, 2048], P(('dp', 'tp')), parts along dimension 0
- output 2: float32 [8, 2048], P('dp'), parts along dimension 0
- output 3: bfloat16 [8, 2048, 6144], P('dp', None, 'tp'), parts along dimension 0
- output 4: bfloat16 [8, 2048, 2048], P('dp', 'tp'), parts along dimension 0
- output 5: bfloat16 [8, 2048, 8192], P('dp', None, 'tp'), parts along dimension 0
- output 6: bfloat16 [8, 2048, 8192], P('dp', None, 'tp'), parts along dimension 0
- output 7: bfloat16 [8, 8192, 2048], P('dp', 'tp'), parts along dimension 0
There are 4 independent parts. A program takes and returns all parts, laid end to end along the dimension named above; an argument that names none is the same for every part.
All inputs are finite; a program needn't handle non-finite values.
Results may differ from a plain program's by a relative error of at most 0.0158804.
Values are sent between devices in bfloat16 or wider.
A program may use at most 768 MiB of HBM per device.

v0:
```python
import jax
import jax.numpy as jnp
from jax import lax
from jax.sharding import PartitionSpec as P

HEAD_DIM = 128
NORM_EPS = 1e-5
ROPE_BASE = 10000.0


def rope_tables(seq_len):
    half_dim = HEAD_DIM // 2
    freqs = ROPE_BASE ** (-2.0 * jnp.arange(half_dim, dtype=jnp.float32) / HEAD_DIM)
    angles = jnp.arange(seq_len, dtype=jnp.float32)[:, None] * freqs[None, :]
    return jnp.cos(angles)[:, None, None, :], jnp.sin(angles)[:, None, None, :]


def rotate(values, cos_tab, sin_tab):
    half_dim = values.shape[-1] // 2
    lower_half = values[..., :half_dim]
    upper_half = values[..., half_dim:]
    return jnp.concatenate([lower_half * cos_tab - upper_half * sin_tab, upper_half * cos_tab + lower_half * sin_tab], axis=-1)


def rms_scale(x_f32, gain_row):
    inv_rms = lax.rsqrt(jnp.mean(x_f32 * x_f32, axis=-1, keepdims=True) + NORM_EPS)
    return x_f32 * inv_rms * gain_row


def gated(gate_f32, up_f32):
    return jax.nn.silu(gate_f32) * up_f32


def causal_scores(query, keys_rot):
    seq_len = query.shape[0]
    causal = jnp.arange(seq_len)[:, None] >= jnp.arange(seq_len)[None, :]
    scores = jnp.einsum('skgd,tkd->kgst', query, keys_rot, preferred_element_type=jnp.float32) * HEAD_DIM ** -0.5
    return jnp.where(causal, scores, -1e30)


def block_forward(x_loc, gain_row, w_qkv_l, w_out_l, w_gate_l, w_up_l, w_down_l, cos_tab, sin_tab, with_output):
    seq_len = cos_tab.shape[0]
    heads_local = w_out_l.shape[0] // HEAD_DIM
    kv_local = (w_qkv_l.shape[1] // HEAD_DIM - heads_local) // 2
    group_size = heads_local // kv_local
    x_f32 = x_loc.astype(jnp.float32)
    u_loc = rms_scale(x_f32, gain_row).astype(jnp.bfloat16)
    u_full = lax.all_gather(u_loc, 'tp', axis=0, tiled=True)
    qkv_all = jnp.dot(u_full, w_qkv_l, preferred_element_type=jnp.float32).astype(jnp.bfloat16).reshape(seq_len, kv_local, group_size + 2, HEAD_DIM)
    rotated = rotate(qkv_all[:, :, :group_size + 1].astype(jnp.float32), cos_tab, sin_tab).astype(jnp.bfloat16)
    query = rotated[:, :, :group_size]
    keys_rot = rotated[:, :, group_size]
    values_v = qkv_all[:, :, group_size + 1]
    scores = causal_scores(query, keys_rot)
    row_max = jnp.max(scores, axis=-1, keepdims=True)
    log_norm = row_max + jnp.log(jnp.sum(jnp.exp(scores - row_max), axis=-1, keepdims=True))
    attn_prob = jnp.exp(scores - log_norm).astype(jnp.bfloat16)
    attn_out = jnp.einsum('kgst,tkd->skgd', attn_prob, values_v, preferred_element_type=jnp.float32).astype(jnp.bfloat16).reshape(seq_len, heads_local * HEAD_DIM)
    gate_act = jnp.dot(u_full, w_gate_l, preferred_element_type=jnp.float32).astype(jnp.bfloat16)
    up_act = jnp.dot(u_full, w_up_l, preferred_element_type=jnp.float32).astype(jnp.bfloat16)
    saved = {'x_loc': x_loc, 'u_loc': u_loc, 'query': query, 'keys_rot': keys_rot, 'values_v': values_v, 'attn_out': attn_out, 'log_norm': log_norm, 'gate_act': gate_act, 'up_act': up_act}
    if not with_output:
        return None, saved
    hidden = gated(gate_act.astype(jnp.float32), up_act.astype(jnp.float32)).astype(jnp.bfloat16)
    block_part = jnp.dot(attn_out, w_out_l, preferred_element_type=jnp.float32) + jnp.dot(hidden, w_down_l, preferred_element_type=jnp.float32)
    y_loc = (x_f32 + lax.psum_scatter(block_part, 'tp', scatter_dimension=0, tiled=True)).astype(jnp.bfloat16)
    return y_loc, saved


def block_backward(dy_loc, saved, gain_row, w_qkv_l, w_out_l, w_gate_l, w_up_l, w_down_l, cos_tab, sin_tab):
    saved, dy_loc = lax.optimization_barrier((saved, dy_loc))
    query = saved['query']
    keys_rot = saved['keys_rot']
    values_v = saved['values_v']
    seq_len, kv_local, group_size = query.shape[0], query.shape[1], query.shape[2]
    u_full = lax.all_gather(saved['u_loc'], 'tp', axis=0, tiled=True)
    dy_full = lax.all_gather(dy_loc, 'tp', axis=0, tiled=True)
    grad_out_l = jnp.einsum('sh,sd->hd', saved['attn_out'], dy_full, preferred_element_type=jnp.float32).astype(jnp.bfloat16)
    d_attn = jnp.einsum('sd,hd->sh', dy_full, w_out_l, preferred_element_type=jnp.float32).astype(jnp.bfloat16).reshape(seq_len, kv_local, group_size, HEAD_DIM)
    hidden_f32, gated_pull = jax.vjp(gated, saved['gate_act'].astype(jnp.float32), saved['up_act'].astype(jnp.float32))
    hidden = hidden_f32.astype(jnp.bfloat16)
    grad_down_l = jnp.einsum('sf,sd->fd', hidden, dy_full, preferred_element_type=jnp.float32).astype(jnp.bfloat16)
    d_hidden = jnp.einsum('sd,fd->sf', dy_full, w_down_l, preferred_element_type=jnp.float32).astype(jnp.bfloat16)
    d_gate_f32, d_up_f32 = gated_pull(d_hidden.astype(jnp.float32))
    d_gate = d_gate_f32.astype(jnp.bfloat16)
    d_up = d_up_f32.astype(jnp.bfloat16)
    grad_gate_l = jnp.einsum('sd,sf->df', u_full, d_gate, preferred_element_type=jnp.float32).astype(jnp.bfloat16)
    grad_up_l = jnp.einsum('sd,sf->df', u_full, d_up, preferred_element_type=jnp.float32).astype(jnp.bfloat16)
    attn_prob_f32 = jnp.exp(causal_scores(query, keys_rot) - saved['log_norm'])
    attn_prob = attn_prob_f32.astype(jnp.bfloat16)
    d_values = jnp.einsum('kgst,skgd->tkd', attn_prob, d_attn, preferred_element_type=jnp.float32).astype(jnp.bfloat16)
    d_prob = jnp.einsum('skgd,tkd->kgst', d_attn, values_v, preferred_element_type=jnp.float32).astype(jnp.bfloat16).astype(jnp.float32)
    d_scores = (attn_prob_f32 * (d_prob - jnp.sum(attn_prob_f32 * d_prob, axis=-1, keepdims=True)) * HEAD_DIM ** -0.5).astype(jnp.bfloat16)
    d_query = jnp.einsum('kgst,tkd->skgd', d_scores, keys_rot, preferred_element_type=jnp.float32).astype(jnp.bfloat16)
    d_keys = jnp.einsum('kgst,skgd->tkd', d_scores, query, preferred_element_type=jnp.float32).astype(jnp.bfloat16)
    d_rotated = jnp.concatenate([d_query, d_keys[:, :, None]], axis=2).astype(jnp.float32)
    d_unrotated = rotate(d_rotated, cos_tab, -sin_tab).astype(jnp.bfloat16)
    d_qkv = jnp.concatenate([d_unrotated, d_values[:, :, None]], axis=2).reshape(seq_len, w_qkv_l.shape[1])
    grad_qkv_l = jnp.einsum('sd,sc->dc', u_full, d_qkv, preferred_element_type=jnp.float32).astype(jnp.bfloat16)
    normed_part = jnp.einsum('sc,dc->sd', d_qkv, w_qkv_l, preferred_element_type=jnp.float32) + jnp.einsum('sf,df->sd', d_gate, w_gate_l, preferred_element_type=jnp.float32) + jnp.einsum('sf,df->sd', d_up, w_up_l, preferred_element_type=jnp.float32)
    d_normed = lax.psum_scatter(normed_part, 'tp', scatter_dimension=0, tiled=True).astype(jnp.bfloat16)
    norm_pull = jax.vjp(rms_scale, saved['x_loc'].astype(jnp.float32), gain_row)[1]
    d_x_norm, grad_gain_l = norm_pull(d_normed.astype(jnp.float32))
    grad_x_loc = (dy_loc.astype(jnp.float32) + d_x_norm).astype(jnp.bfloat16)
    return grad_x_loc, grad_gain_l, grad_qkv_l, grad_out_l, grad_gate_l, grad_up_l, grad_down_l


def solution(mesh):
    tp_size = mesh.shape['tp']
    row_spec = P(('dp', 'tp'), None)
    col_spec = P(None, None, 'tp')
    inner_spec = P(None, 'tp', None)

    def device_program(x_loc, dy_loc, norm_gain, w_qkv, w_out, w_gate, w_up, w_down):
        n_layers = w_qkv.shape[0]
        cos_tab, sin_tab = rope_tables(x_loc.shape[0] * tp_size)
        saved_all = []
        x_cur = x_loc
        for layer_idx in range(n_layers):
            x_cur, saved = block_forward(x_cur, norm_gain[layer_idx], w_qkv[layer_idx], w_out[layer_idx], w_gate[layer_idx], w_up[layer_idx], w_down[layer_idx], cos_tab, sin_tab, layer_idx < n_layers - 1)
            saved_all.append(saved)
        grad_cur = dy_loc
        layer_grads = []
        for layer_idx in reversed(range(n_layers)):
            results = block_backward(grad_cur, saved_all[layer_idx], norm_gain[layer_idx], w_qkv[layer_idx], w_out[layer_idx], w_gate[layer_idx], w_up[layer_idx], w_down[layer_idx], cos_tab, sin_tab)
            grad_cur = results[0]
            layer_grads.insert(0, results[1:])
        grad_gain = lax.psum(jnp.stack([item[0] for item in layer_grads]), 'tp')
        stacked = [jnp.stack([item[grad_idx] for item in layer_grads]) for grad_idx in range(1, 6)]
        return (grad_cur, grad_gain, stacked[0], stacked[1], stacked[2], stacked[3], stacked[4])

    return jax.shard_map(device_program, mesh=mesh, in_specs=(row_spec, row_spec, P(None, None), col_spec, inner_spec, col_spec, col_spec, inner_spec), out_specs=(row_spec, P('dp', None), P('dp', None, 'tp'), P('dp', 'tp', None), P('dp', None, 'tp'), P('dp', None, 'tp'), P('dp', 'tp', None)), check_vma=False)
```

profile of v0, /device:TPU:81, one launch (start us, length us, event | category | flops | bytes accessed | tf_op | source)
XLA Modules:
  0.0 1139.3 jit_solution(17428376420282775795)
XLA Ops:
  21.7 42.2 %all-gather.7.cloned.1.call-done = bf16[2048,2048]{1,0:T(8,128)(2,1)} async-done(((bf16[256,2048]{1,0:T(8,128)(2,1)}), bf16[2048,2048]{1,0:T(8,128)(2,1)}) %all-gather.7.cloned.1.call-update) | async-done | bytes 8388624 | tf_op jit(solution)/shard_map/all_gather | solution.py:48
  63.9 10.2 convolution_convert_fusion.3
  87.0 15.8 %fusion.16 = (f32[2,2048]{1,0:T(2,128)S(1)}, f32[2,2048,2048]{2,1,0:T(8,128)}) fusion(pred[2048,2048]{0,1:T(8,128)(4,1)S(1)} %copy-done, bf16[2048,2,128]{2,0,1:T(8,128)(2,1)} %get-tuple-element.36, bf16[2048,2,1,128]{3,0,1,2:T(8,128)(2,1)} %get-tuple-element.37), kind=kOutput, calls=%fused_computation.26 | convolution fusion | flops 2172645376 | bytes 39862272 | tf_op jit(solution)/shard_map/skgd,tkd->kgst/dot_general | solution.py:37
  102.8 14.9 %exponential_reduce_fusion.1 = f32[2,2048]{1,0:T(2,128)S(1)} fusion(f32[2,2048,2048]{2,1,0:T(8,128)} %get-tuple-element.71, f32[2,2048]{1,0:T(2,128)S(1)} %get-tuple-element.70, pred[2048,2048]{0,1:T(8,128)(4,1)S(1)} %copy-done), kind=kLoop, calls=%fused_computation.25 | loop fusion | flops 33550336 | bytes 37781504 | tf_op jit(solution)/shard_map/reduce_sum | solution.py:56
  117.7 17.9 %fusion.136 = bf16[2,128,2048]{2,1,0:T(8,128)(2,1)} fusion(f32[2,2048,2048]{2,1,0:T(8,128)} %get-tuple-element.71, f32[2,2048]{1,0:T(2,128)S(1)} %log_add_fusion.1, pred[2048,2048]{0,1:T(8,128)(4,1)} %iota_compare_fusion, bf16[2048,2,3,128]{0,3,2,1:T(8,128)(2,1)} %bitcast.358), kind=kOutput, calls=%fused_computation.184 | convolution fusion | flops 2181562368 | bytes 39862272 | tf_op jit(solution)/shard_map/kgst,tkd->skgd/dot_general | solution.py:58
  135.6 13.8 %fusion.90 = bf16[2048,1024]{1,0:T(8,128)(2,1)} fusion(bf16[2048,2048]{1,0:T(8,128)(2,1)} %all-gather.7.cloned.1.call-done, bf16[2,2048,1024]{2,1,0:T(8,128)(2,1)} %param.13), kind=kOutput, calls=%fused_computation.129 | convolution fusion | flops 8592031744 | bytes 16777216 | tf_op jit(solution)/shard_map/dot_general | solution.py:59
  149.4 13.8 %fusion.93 = bf16[2048,1024]{1,0:T(8,128)(2,1)} fusion(bf16[2048,2048]{1,0:T(8,128)(2,1)} %all-gather.7.cloned.1.call-done, bf16[2,2048,1024]{2,1,0:T(8,128)(2,1)} %param.14), kind=kOutput, calls=%fused_computation.130 | convolution fusion | flops 8592031744 | bytes 16777216 | tf_op jit(solution)/shard_map/dot_general | solution.py:60
  163.2 13.4 %fusion.59 = f32[2048,2048]{1,0:T(8,128)S(1)} fusion(bf16[2048,1024]{1,0:T(8,128)(2,1)} %fusion.93, bf16[2048,1024]{1,0:T(8,128)(2,1)} %fusion.90, bf16[2,1024,2048]{2,1,0:T(8,128)(2,1)} %param.15), kind=kOutput, calls=%fused_computation.91 | convolution fusion | flops 8606711808 | bytes 29360128 | tf_op jit(solution)/shard_map/dot_general | solution.py:65
  176.6 9.8 convolution_add_fusion
  186.6 88.2 %reduce-scatter.4.cloned.1.call-done = f32[256,2048]{1,0:T(8,128)} async-done(((f32[2048,2048]{1,0:T(8,128)}), f32[256,2048]{1,0:T(8,128)}) %reduce-scatter.4.cloned.1.call-update) | async-done | bytes 2097168 | tf_op jit(solution)/shard_map/reduce_scatter | solution.py:66
  279.2 47.0 %all-gather.9.cloned.1.call-done = bf16[2048,2048]{1,0:T(8,128)(2,1)} async-done(((bf16[256,2048]{1,0:T(8,128)(2,1)}), bf16[2048,2048]{1,0:T(8,128)(2,1)}) %all-gather.9.cloned.1.call-update) | async-done | bytes 8388624 | tf_op jit(solution)/shard_map/all_gather | solution.py:48
  326.1 10.3 convolution_convert_fusion.2
  348.5 13.4 %fusion.17 = (f32[2,2048]{1,0:T(2,128)S(1)}, f32[2,2048,2048]{2,1,0:T(8,128)}) fusion(pred[2048,2048]{0,1:T(8,128)(4,1)S(1)} %copy-done.1, bf16[2048,2,128]{2,0,1:T(8,128)(2,1)S(1)} %get-tuple-element.28, bf16[2048,2,1,128]{3,0,1,2:T(8,128)(2,1)S(1)} %get-tuple-element.29), kind=kOutput, calls=%fused_computation.27 | convolution fusion | flops 2172645376 | bytes 39862272 | tf_op jit(solution)/shard_map/skgd,tkd->kgst/dot_general | solution.py:37
  361.9 14.7 %exponential_reduce_fusion = f32[2,2048]{1,0:T(2,128)S(1)} fusion(f32[2,2048,2048]{2,1,0:T(8,128)} %get-tuple-element.73, f32[2,2048]{1,0:T(2,128)S(1)} %get-tuple-element.72, pred[2048,2048]{0,1:T(8,128)(4,1)S(1)} %copy-done.1), kind=kLoop, calls=%fused_computation.23 | loop fusion | flops 33550336 | bytes 37781504 | tf_op jit(solution)/shard_map/reduce_sum | solution.py:56
  376.7 18.1 %fusion.139 = bf16[2,128,2048]{2,1,0:T(8,128)(2,1)} fusion(f32[2,2048,2048]{2,1,0:T(8,128)} %get-tuple-element.73, f32[2,2048]{1,0:T(2,128)S(1)} %log_add_fusion, pred[2048,2048]{0,1:T(8,128)(4,1)} %iota_compare_fusion, bf16[2048,2,3,128]{0,3,2,1:T(8,128)(2,1)} %bitcast.362), kind=kOutput, calls=%fused_computation.185 | convolution fusion | flops 2181562368 | bytes 39862272 | tf_op jit(solution)/shard_map/kgst,tkd->skgd/dot_general | solution.py:58
  394.8 13.8 %fusion.99 = bf16[2048,1024]{1,0:T(8,128)(2,1)} fusion(bf16[2048,2048]{1,0:T(8,128)(2,1)} %all-gather.9.cloned.1.call-done, bf16[2,2048,1024]{2,1,0:T(8,128)(2,1)} %param.13), kind=kOutput, calls=%fused_computation.132 | convolution fusion | flops 8592031744 | bytes 16777216 | tf_op jit(solution)/shard_map/dot_general | solution.py:59
  408.6 13.8 %fusion.102 = bf16[2048,1024]{1,0:T(8,128)(2,1)} fusion(bf16[2048,2048]{1,0:T(8,128)(2,1)} %all-gather.9.cloned.1.call-done, bf16[2,2048,1024]{2,1,0:T(8,128)(2,1)} %param.14), kind=kOutput, calls=%fused_computation.133 | convolution fusion | flops 8592031744 | bytes 16777216 | tf_op jit(solution)/shard_map/dot_general | solution.py:60
  422.9 46.3 %all-gather.11.cloned.1.call-done = bf16[2048,2048]{1,0:T(8,128)(2,1)} async-done(((bf16[256,2048]{1,0:T(8,128)(2,1)}), bf16[2048,2048]{1,0:T(8,128)(2,1)}) %all-gather.11.cloned.1.call-update) | async-done | bytes 8388624 | tf_op jit(solution)/shard_map/all_gather | solution.py:77
  483.4 23.4 %fusion.12 = (f32[2,2048]{1,0:T(2,128)S(1)}, f32[2,2048,2048]{2,1,0:T(8,128)}) fusion(bf16[2,2048,2048]{2,1,0:T(8,128)(2,1)} %convolution_convert_fusion.1, f32[2,2048]{1,0:T(2,128)S(1)} %log_add_fusion, pred[2048,2048]{0,1:T(8,128)(4,1)} %iota_compare_fusion, bf16[2048,2,128]{2,0,1:T(8,128)(2,1)S(1)} %get-tuple-element.28, ...), kind=kOutput, calls=%fused_computation.18 | convolution fusion | flops 2197811200 | bytes 56655872 | tf_op jit(solution)/shard_map/skgd,tkd->kgst/dot_general | solution.py:37
  506.8 15.2 %fusion.150 = bf16[2048,2,1,128]{3,0,1,2:T(8,128)(2,1)} fusion(bf16[2048,2,128]{0,2,1:T(8,128)(2,1)S(1)} %bitcast.366, f32[2,2048,2048]{2,1,0:T(8,128)} %get-tuple-element.75, f32[2,2048]{1,0:T(2,128)S(1)} %log_add_fusion, pred[2048,2048]{0,1:T(8,128)(4,1)S(1)} %copy-done.2), kind=kOutput, calls=%fused_computation.202 | convolution fusion | flops 2181562368 | bytes 39862272 | tf_op jit(solution)/shard_map/kgst,skgd->tkd/dot_general | solution.py:91
  522.0 25.4 %fusion.24 = bf16[2,2048,2048]{1,2,0:T(8,128)(2,1)} fusion(f32[2,2048,2048]{2,1,0:T(8,128)} %get-tuple-element.75, bf16[2,2048,2048]{2,1,0:T(8,128)(2,1)} %convolution_convert_fusion.1, f32[2,2048]{1,0:T(2,128)S(1)} %get-tuple-element.74, f32[2,2048]{1,0:T(2,128)S(1)} %log_add_fusion, pred[2048,2048]{0,1:T(8,128)(4,1)S(1)} %copy-done.2), kind=kLoop, calls=%fused_computation.34 | loop fusion | flops 67108864 | bytes 71335936 | tf_op jit(solution)/shard_map/reshape.30
  547.4 9.3 fusion.148
  556.7 11.4 fusion.146
  575.6 13.2 %fusion.118 = f32[2048,2048]{1,0:T(8,128)} fusion(bf16[2048,768]{0,1:T(8,128)(2,1)} %bitcast.353, bf16[2,2048,768]{2,1,0:T(8,128)(2,1)} %param.11), kind=kOutput, calls=%fused_computation.159 | convolution fusion | flops 6442450944 | bytes 23068672 | tf_op jit(solution)/shard_map/sc,dc->sd/dot_general | solution.py:100
  588.9 14.0 %fusion.105 = bf16[2048,1024]{1,0:T(8,128)(2,1)} fusion(bf16[2048,2048]{1,0:T(8,128)(2,1)} %all-gather.11.cloned.1.call-done, bf16[2,1024,2048]{2,1,0:T(8,128)(2,1)} %param.15), kind=kOutput, calls=%fused_computation.134 | convolution fusion | flops 8592031744 | bytes 16777216 | tf_op jit(solution)/shard_map/sd,fd->sf/dot_general | solution.py:83
  602.9 16.7 %fusion.70 = f32[2048,2048]{1,0:T(8,128)} fusion(bf16[2,2048,1024]{2,1,0:T(8,128)(2,1)S(1)} %bitcast.376, bf16[2048,1024]{1,0:T(8,128)(2,1)S(1)} %copy-done.40, bf16[2048,1024]{1,0:T(8,128)(2,1)} %fusion.102, bf16[2048,1024]{1,0:T(8,128)(2,1)} %fusion.105), kind=kOutput, calls=%fused_computation.99 | convolution fusion | flops 8619294720 | bytes 33554432 | tf_op jit(solution)/shard_map/sf,df->sd/dot_general | solution.py:100
  619.6 24.5 %add_add_fusion.1 = f32[2048,2048]{1,0:T(8,128)} fusion(f32[2048,2048]{1,0:T(8,128)} %fusion.118, f32[2048,2048]{1,0:T(8,128)} %fusion.70, bf16[2,2048,1024]{2,1,0:T(8,128)(2,1)} %param.14, bf16[2048,1024]{1,0:T(8,128)(2,1)} %fusion.105, bf16[2048,1024]{1,0:T(8,128)(2,1)} %fusion.99), kind=kOutput, calls=%fused_computation.37 | convolution fusion | flops 8615100416 | bytes 62914560 | tf_op jit(solution)/shard_map/sf,df->sd/dot_general | solution.py:100
  646.3 86.2 %reduce-scatter.6.cloned.1.call-done = f32[256,2048]{1,0:T(8,128)} async-done(((f32[2048,2048]{1,0:T(8,128)}), f32[256,2048]{1,0:T(8,128)}) %reduce-scatter.6.cloned.1.call-update) | async-done | bytes 2097168 | tf_op jit(solution)/shard_map/reduce_scatter | solution.py:101
  740.4 45.4 %all-gather.13.cloned.1.call-done = bf16[2048,2048]{1,0:T(8,128)(2,1)} async-done(((bf16[256,2048]{1,0:T(8,128)(2,1)}), bf16[2048,2048]{1,0:T(8,128)(2,1)}) %all-gather.13.cloned.1.call-update) | async-done | bytes 8388624 | tf_op jit(solution)/shard_map/all_gather | solution.py:77
  792.7 9.4 convolution_convert_fusion
  802.1 23.4 %fusion.6 = (f32[2,2048]{1,0:T(2,128)S(1)}, f32[2,2048,2048]{2,1,0:T(8,128)}) fusion(bf16[2,2048,2048]{2,1,0:T(8,128)(2,1)} %convolution_convert_fusion, f32[2,2048]{1,0:T(2,128)S(1)} %copy-done.35, pred[2048,2048]{0,1:T(8,128)(4,1)} %iota_compare_fusion, bf16[2048,2,128]{2,0,1:T(8,128)(2,1)S(1)} %copy-done.15, bf16[2048,2,1,128]{3,0,1,2:T(8,128)(2,1)} %get-tuple-element.37), kind=kOutput, calls=%fused_computation.11 | convolution fusion | flops 2197811200 | bytes 56655872 | tf_op jit(solution)/shard_map/skgd,tkd->kgst/dot_general | solution.py:37
  825.6 25.3 %fusion.25 = bf16[2,2048,2048]{1,2,0:T(8,128)(2,1)} fusion(f32[2,2048,2048]{2,1,0:T(8,128)} %get-tuple-element.77, bf16[2,2048,2048]{2,1,0:T(8,128)(2,1)} %convolution_convert_fusion, f32[2,2048]{1,0:T(2,128)S(1)} %get-tuple-element.76, f32[2,2048]{1,0:T(2,128)S(1)} %copy-done.35, pred[2048,2048]{0,1:T(8,128)(4,1)S(1)} %copy-done.3), kind=kLoop, calls=%fused_computation.35 | loop fusion | flops 67108864 | bytes 71335936 | tf_op jit(solution)/shard_map/reshape.50
  850.9 10.7 fusion.147
  861.6 10.7 fusion.149
  876.6 15.2 %fusion.153 = bf16[2048,2,1,128]{3,0,1,2:T(8,128)(2,1)} fusion(bf16[2048,2,128]{0,2,1:T(8,128)(2,1)S(1)} %bitcast.364, f32[2,2048,2048]{2,1,0:T(8,128)} %get-tuple-element.77, f32[2,2048]{1,0:T(2,128)S(1)} %copy-done.35, pred[2048,2048]{0,1:T(8,128)(4,1)S(1)} %copy-done.4), kind=kOutput, calls=%fused_computation.203 | convolution fusion | flops 2181562368 | bytes 39862272 | tf_op jit(solution)/shard_map/kgst,skgd->tkd/dot_general | solution.py:91
  898.2 13.0 %fusion.121 = f32[2048,2048]{1,0:T(8,128)} fusion(bf16[2048,768]{0,1:T(8,128)(2,1)} %bitcast.355, bf16[2,2048,768]{2,1,0:T(8,128)(2,1)} %param.11), kind=kOutput, calls=%fused_computation.162 | convolution fusion | flops 6442450944 | bytes 23068672 | tf_op jit(solution)/shard_map/sc,dc->sd/dot_general | solution.py:100
  911.3 14.0 %fusion.96 = bf16[2048,1024]{1,0:T(8,128)(2,1)} fusion(bf16[2048,2048]{1,0:T(8,128)(2,1)} %all-gather.13.cloned.1.call-done, bf16[2,1024,2048]{2,1,0:T(8,128)(2,1)} %param.15), kind=kOutput, calls=%fused_computation.131 | convolution fusion | flops 8592031744 | bytes 16777216 | tf_op jit(solution)/shard_map/sd,fd->sf/dot_general | solution.py:83
  925.3 16.7 %fusion.80 = f32[2048,2048]{1,0:T(8,128)} fusion(bf16[2,2048,1024]{2,1,0:T(8,128)(2,1)S(1)} %bitcast.378, bf16[2048,1024]{1,0:T(8,128)(2,1)S(1)} %copy-done.37, bf16[2048,1024]{1,0:T(8,128)(2,1)} %fusion.93, bf16[2048,1024]{1,0:T(8,128)(2,1)} %fusion.96), kind=kOutput, calls=%fused_computation.109 | convolution fusion | flops 8619294720 | bytes 33554432 | tf_op jit(solution)/shard_map/sf,df->sd/dot_general | solution.py:100
  942.0 24.8 %add_add_fusion = f32[2048,2048]{1,0:T(8,128)} fusion(f32[2048,2048]{1,0:T(8,128)} %fusion.121, f32[2048,2048]{1,0:T(8,128)} %fusion.80, bf16[2,2048,1024]{2,1,0:T(8,128)(2,1)} %param.14, bf16[2048,1024]{1,0:T(8,128)(2,1)} %fusion.96, bf16[2048,1024]{1,0:T(8,128)(2,1)} %fusion.90), kind=kOutput, calls=%fused_computation.36 | convolution fusion | flops 8615100416 | bytes 62914560 | tf_op jit(solution)/shard_map/sf,df->sd/dot_general | solution.py:100
  974.1 10.5 fusion.125
  984.6 15.1 %convert_bitcast_fusion.2 = bf16[1,1024,2048]{2,1,0:T(8,128)(2,1)} fusion(bf16[2048,2048]{1,0:T(8,128)(2,1)} %all-gather.11.cloned.1.call-done, bf16[2048,1024]{1,0:T(8,128)(2,1)S(1)} %copy-done.44, bf16[2048,1024]{1,0:T(8,128)(2,1)S(1)} %copy-done.41), kind=kOutput, calls=%fused_computation.113 | convolution fusion | flops 8608808960 | bytes 20971520 | tf_op jit(solution)/shard_map/sf,sd->fd/dot_general | solution.py:82
  999.7 14.1 %convert_bitcast_fusion.6 = bf16[1,2048,1024]{2,1,0:T(8,128)(2,1)} fusion(bf16[2048,2048]{1,0:T(8,128)(2,1)S(1)} %bitcast.382, bf16[2048,1024]{1,0:T(8,128)(2,1)S(1)} %copy-done.42, bf16[2048,1024]{1,0:T(8,128)(2,1)} %fusion.102, bf16[2048,1024]{1,0:T(8,128)(2,1)} %fusion.105), kind=kOutput, calls=%fused_computation.117 | convolution fusion | flops 8621391872 | bytes 25165824 | tf_op jit(solution)/shard_map/sd,sf->df/dot_general | solution.py:87
  1013.8 13.8 %convert_bitcast_fusion.4 = bf16[1,2048,1024]{2,1,0:T(8,128)(2,1)} fusion(bf16[2048,2048]{1,0:T(8,128)(2,1)S(1)} %bitcast.382, bf16[2048,1024]{1,0:T(8,128)(2,1)} %fusion.105, bf16[2048,1024]{1,0:T(8,128)(2,1)} %fusion.99), kind=kOutput, calls=%fused_computation.115 | convolution fusion | flops 8608808960 | bytes 20971520 | tf_op jit(solution)/shard_map/sd,sf->df/dot_general | solution.py:88
  1031.9 10.3 fusion.124
  1048.0 14.8 %convert_bitcast_fusion.3 = bf16[1,1024,2048]{2,1,0:T(8,128)(2,1)} fusion(bf16[2048,2048]{1,0:T(8,128)(2,1)} %all-gather.13.cloned.1.call-done, bf16[2048,1024]{1,0:T(8,128)(2,1)S(1)} %copy-done.43, bf16[2048,1024]{1,0:T(8,128)(2,1)S(1)} %copy-done.38), kind=kOutput, calls=%fused_computation.114 | convolution fusion | flops 8608808960 | bytes 20971520 | tf_op jit(solution)/shard_map/sf,sd->fd/dot_general | solution.py:82
  1070.5 15.7 %convert_bitcast_fusion.7 = bf16[1,2048,1024]{2,1,0:T(8,128)(2,1)S(1)} fusion(bf16[2048,2048]{1,0:T(8,128)(2,1)} %all-gather.15.cloned.1.call-done, bf16[2048,1024]{1,0:T(8,128)(2,1)} %fusion.90, bf16[2048,1024]{1,0:T(8,128)(2,1)} %fusion.93, bf16[2048,1024]{1,0:T(8,128)(2,1)} %fusion.96), kind=kOutput, calls=%fused_computation.118 | convolution fusion | flops 8621391872 | bytes 25165824 | tf_op jit(solution)/shard_map/sd,sf->df/dot_general | solution.py:87
  1086.2 13.5 %convert_bitcast_fusion.5 = bf16[1,2048,1024]{2,1,0:T(8,128)(2,1)S(1)} fusion(bf16[2048,2048]{1,0:T(8,128)(2,1)} %all-gather.15.cloned.1.call-done, bf16[2048,1024]{1,0:T(8,128)(2,1)} %fusion.96, bf16[2048,1024]{1,0:T(8,128)(2,1)S(1)} %copy-done.39), kind=kOutput, calls=%fused_computation.116 | convolution fusion | flops 8608808960 | bytes 20971520 | tf_op jit(solution)/shard_map/sd,sf->df/dot_general | solution.py:88
  1108.2 20.9 %psum.7 = f32[2,2048]{1,0:T(2,128)} all-reduce(f32[2,2048]{1,0:T(2,128)S(1)} %pad_maximum_fusion.9), channel_id=1, replica_groups=mesh['dp'=4,'tp'=8] {'tp'}, use_global_device_ids=true, to_apply=%region_17.18 | all-reduce | flops 4096 | bytes 32768 | tf_op jit(solution)/shard_map/psum | solution.py:128
  (183 shorter events, 130.3 us)
Async XLA Ops:
  7.2 56.7 %all-gather.7.cloned.1.call-start = ((), (), s32[]{:S(2)}) async-start(), calls=%async_computation.3 | async-start | bytes 9437184 | tf_op jit(solution)/shard_map/all_gather | solution.py:48
  12.8 262.0 %reduce-scatter.4.cloned.1.call-start = ((), (), s32[]{:S(2)}) async-start(), calls=%async_computation.4 | async-start | bytes 18874368 | tf_op jit(solution)/shard_map/reduce_scatter | solution.py:66
  17.6 328.2 %copy-start.7 = (f32[2048,64]{1,0:T(8,128)}, f32[2048,64]{1,0:T(8,128)S(1)}, u32[]{:S(2)}) copy-start(f32[2048,64]{1,0:T(8,128)S(1)} %get-tuple-element.69) | copy-start | bytes 1572868
  117.7 17.9 %copy-start.34 = (f32[2,2048]{1,0:T(2,128)}, f32[2,2048]{1,0:T(2,128)S(1)}, u32[]{:S(2)}) copy-start(f32[2,2048]{1,0:T(2,128)S(1)} %log_add_fusion.1) | copy-start | bytes 49156
  186.4 88.4 %copy-start.5 = (bf16[256,2048]{1,0:T(8,128)(2,1)S(1)}, bf16[256,2048]{1,0:T(8,128)(2,1)}, u32[]{:S(2)}) copy-start(bf16[256,2048]{1,0:T(8,128)(2,1)} %param.8) | copy-start | bytes 3145732
  186.4 91.3 %copy-start.32 = (f32[1,2048]{1,0:T(1,128)S(1)}, f32[1,2048]{1,0:T(1,128)}, u32[]{:S(2)}) copy-start(f32[1,2048]{1,0:T(1,128)} %get-tuple-element.65) | copy-start | bytes 24580
  186.5 139.7 %all-gather.9.cloned.1.call-start = ((), (), s32[]{:S(2)}) async-start(), calls=%async_computation.5 | async-start | bytes 9437184 | tf_op jit(solution)/shard_map/all_gather | solution.py:48
  279.1 190.2 %all-gather.11.cloned.1.call-start = ((), (), s32[]{:S(2)}) async-start(), calls=%async_computation.6 | async-start | bytes 9437184 | tf_op jit(solution)/shard_map/all_gather | solution.py:77
  348.5 13.5 %copy-start.26 = (bf16[2048,2,1,128]{3,0,1,2:T(8,128)(2,1)}, bf16[2048,2,1,128]{3,0,1,2:T(8,128)(2,1)S(1)}, u32[]{:S(2)}) copy-start(bf16[2048,2,1,128]{3,0,1,2:T(8,128)(2,1)S(1)} %get-tuple-element.29) | copy-start | bytes 3145732
  422.5 52.8 %copy-start.17 = (bf16[2048,2,128]{0,2,1:T(8,128)(2,1)S(1)}, bf16[2048,2,128]{0,2,1:T(8,128)(2,1)}, u32[]{:S(2)}) copy-start(bf16[2048,2,128]{0,2,1:T(8,128)(2,1)} %slice_bitcast_fusion) | copy-start | bytes 3145732
  422.5 310.0 %reduce-scatter.6.cloned.1.call-start = ((), (), s32[]{:S(2)}) async-start(), calls=%async_computation.7 | async-start | bytes 18874368 | tf_op jit(solution)/shard_map/reduce_scatter | solution.py:101
  483.4 23.4 %copy-start.2 = (pred[2048,2048]{0,1:T(8,128)(4,1)S(1)}, pred[2048,2048]{0,1:T(8,128)(4,1)}, u32[]{:S(2)}) copy-start(pred[2048,2048]{0,1:T(8,128)(4,1)} %iota_compare_fusion) | copy-start | bytes 12582916
  522.0 25.4 %copy-start.27 = (bf16[2048,2,1,128]{3,0,1,2:T(8,128)(2,1)S(1)}, bf16[2048,2,1,128]{3,0,1,2:T(8,128)(2,1)}, u32[]{:S(2)}) copy-start(bf16[2048,2,1,128]{3,0,1,2:T(8,128)(2,1)} %copy-done.26) | copy-start | bytes 3145732
  556.7 13.2 %copy-start.8 = (f32[2048,64]{1,0:T(8,128)S(1)}, f32[2048,64]{1,0:T(8,128)}, u32[]{:S(2)}) copy-start(f32[2048,64]{1,0:T(8,128)} %copy-done.7) | copy-start | bytes 1572868
  556.7 13.2 %copy-start.12 = (f32[2048,64]{1,0:T(8,128)S(1)}, f32[2048,64]{1,0:T(8,128)}, u32[]{:S(2)}) copy-start(f32[2048,64]{1,0:T(8,128)} %get-tuple-element.67) | copy-start | bytes 1572868
  575.6 27.3 %slice-start = ((s8[8388608]{0:T(1024)(128)(4,1)}), s8[4194304]{0:T(1024)(128)(4,1)S(1)}, s32[]{:S(2)}) async-start(s8[8388608]{0:T(1024)(128)(4,1)} %bitcast.375), calls=%async_computation.12 | async-start | bytes 8388608
  588.9 14.0 %slice-start.1 = ((s8[8388608]{0:T(1024)(128)(4,1)}), s8[4194304]{0:T(1024)(128)(4,1)S(1)}, s32[]{:S(2)}) async-start(s8[8388608]{0:T(1024)(128)(4,1)} %bitcast.375), calls=%async_computation.13 | async-start | bytes 8388608
  588.9 14.0 %copy-start.40 = (bf16[2048,1024]{1,0:T(8,128)(2,1)S(1)}, bf16[2048,1024]{1,0:T(8,128)(2,1)}, u32[]{:S(2)}) copy-start(bf16[2048,1024]{1,0:T(8,128)(2,1)} %fusion.99) | copy-start | bytes 12582916
  644.2 88.3 %copy-start.33 = (f32[1,2048]{1,0:T(1,128)S(1)}, f32[1,2048]{1,0:T(1,128)}, u32[]{:S(2)}) copy-start(f32[1,2048]{1,0:T(1,128)} %get-tuple-element.65) | copy-start | bytes 24580
  644.2 91.2 %copy-start.16 = (bf16[256,2048]{1,0:T(8,128)(2,1)S(1)}, bf16[256,2048]{1,0:T(8,128)(2,1)}, u32[]{:S(2)}) copy-start(bf16[256,2048]{1,0:T(8,128)(2,1)} %param.9) | copy-start | bytes 3145732
  644.2 141.5 %all-gather.13.cloned.1.call-start = ((), (), s32[]{:S(2)}) async-start(), calls=%async_computation.8 | async-start | bytes 9437184 | tf_op jit(solution)/shard_map/all_gather | solution.py:77
  738.7 235.4 %all-gather.17.cloned.1.call-start = ((), (), s32[]{:S(2)}) async-start(), calls=%async_computation.11 | async-start | bytes 9437184 | tf_op jit(solution)/shard_map/all_gather | solution.py:76
  739.5 292.4 %all-gather.15.cloned.1.call-start = ((), (), s32[]{:S(2)}) async-start(), calls=%async_computation.10 | async-start | bytes 9437184 | tf_op jit(solution)/shard_map/all_gather | solution.py:76
  740.3 365.6 %reduce-scatter.8.cloned.1.call-start = ((), (), s32[]{:S(2)}) async-start(), calls=%async_computation.9 | async-start | bytes 18874368 | tf_op jit(solution)/shard_map/reduce_scatter | solution.py:101
  792.7 9.4 copy-start.15
  792.7 9.4 copy-start.35
  802.1 23.4 %copy-start.3 = (pred[2048,2048]{0,1:T(8,128)(4,1)S(1)}, pred[2048,2048]{0,1:T(8,128)(4,1)}, u32[]{:S(2)}) copy-start(pred[2048,2048]{0,1:T(8,128)(4,1)} %iota_compare_fusion) | copy-start | bytes 12582916
  861.6 11.0 copy-start.9
  861.6 11.0 copy-start.13
  898.2 27.1 %slice-start.2 = ((s8[8388608]{0:T(1024)(128)(4,1)}), s8[4194304]{0:T(1024)(128)(4,1)S(1)}, s32[]{:S(2)}) async-start(s8[8388608]{0:T(1024)(128)(4,1)} %bitcast.377), calls=%async_computation.14 | async-start | bytes 8388608
  911.3 14.0 %slice-start.3 = ((s8[8388608]{0:T(1024)(128)(4,1)}), s8[4194304]{0:T(1024)(128)(4,1)S(1)}, s32[]{:S(2)}) async-start(s8[8388608]{0:T(1024)(128)(4,1)} %bitcast.377), calls=%async_computation.15 | async-start | bytes 8388608
  911.3 14.0 %copy-start.37 = (bf16[2048,1024]{1,0:T(8,128)(2,1)S(1)}, bf16[2048,1024]{1,0:T(8,128)(2,1)}, u32[]{:S(2)}) copy-start(bf16[2048,1024]{1,0:T(8,128)(2,1)} %fusion.90) | copy-start | bytes 12582916
  966.9 7.2 copy-start.21
  974.0 10.5 copy-start.41
  974.0 10.5 copy-start.44
  974.0 25.6 %slice-start.6 = ((s8[8388608]{0:T(1024)(128)(4,1)}), s8[4194304]{0:T(1024)(128)(4,1)S(1)}, s32[]{:S(2)}) async-start(s8[8388608]{0:T(1024)(128)(4,1)} %bitcast.381), calls=%async_computation.18 | async-start | bytes 8388608
  984.6 15.1 %slice-start.7 = ((s8[8388608]{0:T(1024)(128)(4,1)}), s8[4194304]{0:T(1024)(128)(4,1)S(1)}, s32[]{:S(2)}) async-start(s8[8388608]{0:T(1024)(128)(4,1)} %bitcast.381), calls=%async_computation.19 | async-start | bytes 8388608
  984.6 15.1 %copy-start.42 = (bf16[2048,1024]{1,0:T(8,128)(2,1)S(1)}, bf16[2048,1024]{1,0:T(8,128)(2,1)}, u32[]{:S(2)}) copy-start(bf16[2048,1024]{1,0:T(8,128)(2,1)} %fusion.99) | copy-start | bytes 12582916
  984.6 43.3 %slice-start.4 = ((s8[8388608]{0:T(1024)(128)(4,1)}), s8[4194304]{0:T(1024)(128)(4,1)S(1)}, s32[]{:S(2)}) async-start(s8[8388608]{0:T(1024)(128)(4,1)} %bitcast.379), calls=%async_computation.16 | async-start | bytes 8388608
  999.7 28.2 %slice-start.5 = ((s8[8388608]{0:T(1024)(128)(4,1)}), s8[4194304]{0:T(1024)(128)(4,1)S(1)}, s32[]{:S(2)}) async-start(s8[8388608]{0:T(1024)(128)(4,1)} %bitcast.379), calls=%async_computation.17 | async-start | bytes 8388608
  1013.8 13.8 %copy-start.6 = (bf16[256,2048]{1,0:T(8,128)(2,1)S(1)}, bf16[256,2048]{1,0:T(8,128)(2,1)}, u32[]{:S(2)}) copy-start(bf16[256,2048]{1,0:T(8,128)(2,1)} %param.8) | copy-start | bytes 3145732
  1013.8 14.1 %copy-start.20 = (bf16[2,128,2048]{2,1,0:T(8,128)(2,1)S(1)}, bf16[2,128,2048]{2,1,0:T(8,128)(2,1)}, u32[]{:S(2)}) copy-start(bf16[2,128,2048]{2,1,0:T(8,128)(2,1)} %fusion.136) | copy-start | bytes 3145732
  1031.9 10.3 copy-start.24
  1070.5 15.7 %copy-start.39 = (bf16[2048,1024]{1,0:T(8,128)(2,1)S(1)}, bf16[2048,1024]{1,0:T(8,128)(2,1)}, u32[]{:S(2)}) copy-start(bf16[2048,1024]{1,0:T(8,128)(2,1)} %fusion.90) | copy-start | bytes 12582916
  1086.1 13.5 %copy-start.18 = (bf16[1,2048,1024]{2,1,0:T(8,128)(2,1)S(1)}, bf16[1,2048,1024]{2,1,0:T(8,128)(2,1)}, u32[]{:S(2)}) copy-start(bf16[1,2048,1024]{2,1,0:T(8,128)(2,1)} %convert_bitcast_fusion.6) | copy-start | bytes 12582916
  1086.1 13.5 %copy-start.19 = (bf16[1,2048,1024]{2,1,0:T(8,128)(2,1)S(1)}, bf16[1,2048,1024]{2,1,0:T(8,128)(2,1)}, u32[]{:S(2)}) copy-start(bf16[1,2048,1024]{2,1,0:T(8,128)(2,1)} %convert_bitcast_fusion.4) | copy-start | bytes 12582916
  1099.7 8.5 copy-start.36
  1099.7 29.4 %copy-start.14 = (bf16[256,2048]{1,0:T(8,128)(2,1)S(1)}, bf16[256,2048]{1,0:T(8,128)(2,1)}, u32[]{:S(2)}) copy-start(bf16[256,2048]{1,0:T(8,128)(2,1)} %fusion.166) | copy-start | bytes 3145732
  (14 other events, 42.4 us)
Sparse Core Ops, SparseCore 0:
  12.9 50.9 all-gather.6
  186.6 88.1 reduce-scatter.3
  279.2 46.8 all-gather.8
  422.6 46.6 all-gather.10
  644.4 88.0 reduce-scatter.5
  738.8 46.8 all-gather.12
  787.3 46.6 all-gather.16
  836.2 46.6 all-gather.14
  967.0 88.0 reduce-scatter.7
where the time goes:
time: 1150 us; the launch traced here: 1140 us
  matrix products  568 us (49%)
  waiting for transfers between devices  357 us (31%)
  other arithmetic  150 us (13%)
  local copies, waits for them, and re-layouts  27.1 us (2%)
  blocking collectives  20.9 us (2%)
  between operations  15 us (1%)
    all_gather x2, waiting for transfers between devices, block_backward(): dy_full = lax.all_gather(dy_loc, 'tp', axis=0, tiled=True)  91.7 us
    all_gather x2, waiting for transfers between devices, block_forward(): u_full = lax.all_gather(u_loc, 'tp', axis=0, tiled=True)  89.2 us
    reduce_scatter x1, waiting for transfers between devices, block_forward(): lax.psum_scatter(block_part, 'tp', scatter_dimension=0, tiled=True)  88.2 us
    reduce_scatter x2, waiting for transfers between devices, block_backward(): lax.psum_scatter(normed_part, 'tp', scatter_dimension=0, tiled=True)  86.2 us
    dot_general x4, matrix products, causal_scores(): jnp.einsum('skgd,tkd->kgst', query, keys_rot, preferred_element_type=jnp....  76 us
    another operation x6, other arithmetic  58.3 us
    dot_general x2, matrix products, block_backward(): jnp.einsum('sf,df->sd', d_up, w_up_l, preferred_element_type=jnp.float32)  49.3 us
    dot_general x2, matrix products, block_forward(): jnp.einsum('kgst,tkd->skgd', attn_prob, values_v, preferred_element_type=...  36.1 us
  transfers between devices with their start and end apart: 9, of which 6 were waited for; matrix products, arithmetic and copies ran while one was open for 29% of the time, Pallas kernels for 0%

commit v1 on v0

v1 whole, which is shorter than its diff:
```python
import functools

import jax
import jax.numpy as jnp
import numpy as np
from jax import lax
from jax.experimental import pallas as pl
from jax.experimental.pallas import tpu as pltpu
from jax.sharding import PartitionSpec as P

HEAD_DIM = 128
NORM_EPS = 1e-5
ROPE_BASE = 10000.0
SCALE = HEAD_DIM ** -0.5
LOG2E = 1.4426950408889634
VMEM_LIMIT = 64000 * 1024
N_CHIPS = 4
SUBS = 4
BF16 = jnp.bfloat16
F32 = jnp.float32
ANY = pl.BlockSpec(memory_space=pl.ANY)
VMEM = pl.BlockSpec(memory_space=pltpu.VMEM)
NT = (((1,), (1,)), ((), ()))
TN = (((0,), (0,)), ((), ()))


def dot(lhs, rhs):
    return jnp.dot(lhs, rhs, preferred_element_type=F32)


def dot_nt(lhs, rhs):
    return lax.dot_general(lhs, rhs, NT, preferred_element_type=F32)


def dot_tn(lhs, rhs):
    return lax.dot_general(lhs, rhs, TN, preferred_element_type=F32)


def params(collective_id=None, semantics=None):
    if collective_id is None:
        return pltpu.CompilerParams(vmem_limit_bytes=VMEM_LIMIT, dimension_semantics=semantics)
    return pltpu.CompilerParams(vmem_limit_bytes=VMEM_LIMIT, collective_id=collective_id, has_side_effects=True)


def cost(flops, bytes_accessed, transcendentals=0):
    return pl.CostEstimate(flops=flops, bytes_accessed=bytes_accessed, transcendentals=transcendentals)


def rope_tables(seq_len):
    half_dim = HEAD_DIM // 2
    freqs = np.float32(ROPE_BASE) ** (np.float32(-2.0) * np.arange(half_dim, dtype=np.float32) / np.float32(HEAD_DIM))
    angles = np.arange(seq_len, dtype=np.float32)[:, None] * freqs[None, :].astype(np.float32)
    cos_half, sin_half = np.cos(angles).astype(np.float32), np.sin(angles).astype(np.float32)
    return np.concatenate([cos_half, cos_half], axis=1), np.concatenate([-sin_half, sin_half], axis=1)


def rotate(values, cos_tab, sin_tab):
    return values * cos_tab + pltpu.roll(values, HEAD_DIM // 2, 1) * sin_tab


def rms_scale(x_f32, gain_row):
    inv_rms = lax.rsqrt(jnp.mean(x_f32 * x_f32, axis=-1, keepdims=True) + NORM_EPS)
    return x_f32 * inv_rms * gain_row


def ring_place():
    me = lax.axis_index('tp')
    chip = me // 2
    core = me % 2
    return me, chip, core


def device_at(chip, core):
    return ((chip + N_CHIPS) % N_CHIPS) * 2 + core


def remote_copy(src, dst, send_sem, recv_sem, peer):
    return pltpu.make_async_remote_copy(
        src_ref=src, dst_ref=dst, send_sem=send_sem, recv_sem=recv_sem, device_id={'tp': peer}, device_id_type=pl.DeviceIdType.MESH
    )


def meet(peers):
    barrier = pltpu.get_barrier_semaphore()
    for peer in peers:
        pl.semaphore_signal(barrier, inc=1, device_id={'tp': peer}, device_id_type=pl.DeviceIdType.MESH)
    pl.semaphore_wait(barrier, len(peers))


def gather_shards(local_hbm, full, send_sems, recv_sems, local_sem, before, compute):
    me, chip, core = ring_place()
    turn = 1 - 2 * core
    partner = device_at(chip, 1 - core)
    ahead = device_at(chip + turn, core)
    behind = device_at(chip - turn, core)
    rows = full.shape[1] // SUBS

    def piece(kind, shard, sub, peer):
        part = full.at[shard, pl.ds(sub * rows, rows)]
        return remote_copy(part, part, send_sems.at[kind, sub], recv_sems.at[shard, sub], peer)

    def send(kind, shard, peer):
        for sub in range(SUBS):
            piece(kind, shard, sub, peer).start()

    def sent(kind, shard, peer, subs):
        for sub in subs:
            piece(kind, shard, sub, peer).wait_send()

    def arrived(shard, pass_on=None):
        for sub in range(SUBS):
            piece(0, shard, sub, partner).wait_recv()
            if pass_on is not None:
                piece(pass_on, shard, sub, partner).start()

    first = device_at(chip - turn, core)
    second = device_at(chip + turn, core)
    third = device_at(chip + 2, core)
    own = pltpu.make_async_copy(local_hbm, full.at[me], local_sem)
    own.start()
    meet((partner, ahead, behind))
    own.wait()
    send(1, me, ahead)
    send(0, me, partner)
    before()

    def step_body(step, carry):
        pair = step // 2
        odd = step % 2
        side = turn * (1 - 2 * odd)
        hop = (3 * pair + (pair // 2) * (2 * pair - 5)) % N_CHIPS
        shard = device_at((chip + side * hop + 2 * N_CHIPS) % N_CHIPS, (core + odd) % 2)

        @pl.when(step == 1)
        def _():
            arrived(partner)

        @pl.when(step == 2)
        def _():
            sent(1, me, ahead, range(SUBS - 1))
            send(2, me, behind)
            arrived(first, 3)

        @pl.when(step == 3)
        def _():
            arrived(device_at(chip + turn, 1 - core))

        @pl.when(step == 4)
        def _():
            sent(2, me, behind, range(SUBS - 1))
            send(4, first, ahead)
            arrived(second, 5)

        @pl.when(step == 5)
        def _():
            arrived(device_at(chip - turn, 1 - core))

        @pl.when(step == 6)
        def _():
            arrived(third, 6)

        @pl.when(step == 7)
        def _():
            arrived(device_at(chip + 2, 1 - core))

        compute(step, shard)
        return carry

    lax.fori_loop(0, 2 * N_CHIPS, step_body, 0)
    sent(0, me, partner, range(SUBS))
    sent(1, me, ahead, (SUBS - 1,))
    sent(2, me, behind, (SUBS - 1,))
    sent(3, first, partner, range(SUBS))
    sent(4, first, ahead, range(SUBS))
    sent(5, second, partner, range(SUBS))
    sent(6, third, partner, range(SUBS))


def gather_scratch(tp_size, rows, width):
    return [
        pltpu.VMEM((tp_size, rows, width), BF16),
        pltpu.SemaphoreType.DMA((7, SUBS)),
        pltpu.SemaphoreType.DMA((tp_size, SUBS)),
        pltpu.SemaphoreType.DMA,
    ]


class RowWriter:
    def __init__(self, stages, outs, sems, rows):
        self.stages, self.outs, self.sems, self.rows = stages, outs, sems, rows

    def copy(self, idx, slot, shard):
        start = pl.multiple_of(shard * self.rows, self.rows)
        return pltpu.make_async_copy(self.stages[idx].at[slot], self.outs[idx].at[pl.ds(start, self.rows)], self.sems.at[idx, slot])

    def reuse(self, step, shard):
        @pl.when(step >= 2)
        def _():
            for idx in range(len(self.outs)):
                self.copy(idx, step % 2, shard).wait()

    def start(self, step, shard):
        for idx in range(len(self.outs)):
            self.copy(idx, step % 2, shard).start()

    def finish(self):
        for idx in range(len(self.outs)):
            for slot in range(2):
                self.copy(idx, slot, 0).wait()


def project_kernel(layer, with_hidden, u_hbm, w_qkv_hbm, w_gate_hbm, w_up_hbm, cos_ref, sin_ref, *rest):
    n_out = 4 if with_hidden else 3
    outs, rest = rest[:n_out], rest[n_out:]
    stages, rest = rest[:n_out], rest[n_out:]
    w_qkv, w_gate, w_up, full, send_sems, recv_sems, local_sem, w_sems, out_sems = rest
    rows = full.shape[1]
    loads = [
        pltpu.make_async_copy(src.at[layer], dst, w_sems.at[idx])
        for idx, (src, dst) in enumerate(((w_qkv_hbm, w_qkv), (w_gate_hbm, w_gate), (w_up_hbm, w_up)))
    ]
    for load in loads:
        load.start()
    writer = RowWriter(stages, outs, out_sems, rows)

    def before():
        for load in loads:
            load.wait()

    def compute(step, shard):
        slot = step % 2
        writer.reuse(step, shard)
        u_rows = full[shard]
        table = pl.ds(pl.multiple_of(shard * rows, rows), rows)
        cos_tab, sin_tab = cos_ref[table], sin_ref[table]
        qkv = dot(u_rows, w_qkv[...]).astype(BF16)
        for head in range(w_qkv.shape[1] // HEAD_DIM):
            cols = slice(head * HEAD_DIM, (head + 1) * HEAD_DIM)
            part = qkv[:, cols]
            if head % 3 != 2:
                part = rotate(part.astype(F32), cos_tab, sin_tab).astype(BF16)
            stages[0][slot, :, cols] = part
        gate = dot(u_rows, w_gate[...]).astype(BF16)
        up = dot(u_rows, w_up[...]).astype(BF16)
        stages[1][slot] = gate
        stages[2][slot] = up
        if with_hidden:
            stages[3][slot] = (jax.nn.silu(gate.astype(F32)) * up.astype(F32)).astype(BF16)
        writer.start(step, shard)

    gather_shards(u_hbm, full, send_sems, recv_sems, local_sem, before, compute)
    writer.finish()


def project(u_loc, w_qkv, w_gate, w_up, tables, layer, tp_size, with_hidden):
    rows, width = u_loc.shape
    seq_len = rows * tp_size
    qkv_cols, ff_cols = w_qkv.shape[2], w_gate.shape[2]
    out_cols = [qkv_cols, ff_cols, ff_cols] + ([ff_cols] if with_hidden else [])
    outs = [jax.ShapeDtypeStruct((seq_len, cols), BF16) for cols in out_cols]
    scratch = [pltpu.VMEM((2, rows, cols), BF16) for cols in out_cols]
    scratch += [pltpu.VMEM((width, cols), BF16) for cols in (qkv_cols, ff_cols, ff_cols)]
    scratch += gather_scratch(tp_size, rows, width)
    scratch += [pltpu.SemaphoreType.DMA((3,)), pltpu.SemaphoreType.DMA((len(outs), 2))]
    total = qkv_cols + 2 * ff_cols
    return pl.pallas_call(
        functools.partial(project_kernel, layer, with_hidden),
        out_shape=outs,
        in_specs=[ANY] * 4 + [VMEM] * 2,
        out_specs=[ANY] * len(outs),
        scratch_shapes=scratch,
        compiler_params=params(collective_id=1 + layer),
        cost_estimate=cost(2 * seq_len * width * total, 2 * (width * total + seq_len * total)),
        name=f'project_{layer}',
    )(u_loc, w_qkv, w_gate, w_up, *tables)


def down_kernel(layer, dy_hbm, w_out_hbm, w_down_hbm, gate_hbm, up_hbm, *rest):
    outs, rest = rest[:5], rest[5:]
    stages, rest = rest[:4], rest[4:]
    gate_in, up_in, w_out, w_down, full, send_sems, recv_sems, local_sem, w_sems, out_sems, in_sems, full_sems = rest
    rows = full.shape[1]
    loads = [
        pltpu.make_async_copy(src.at[layer], dst, w_sems.at[idx])
        for idx, (src, dst) in enumerate(((w_out_hbm, w_out), (w_down_hbm, w_down)))
    ]
    for load in loads:
        load.start()
    writer = RowWriter(stages, outs[:4], out_sems, rows)
    dy_full = outs[4]

    def before():
        for load in loads:
            load.wait()

    def keep(shard):
        return pltpu.make_async_copy(full.at[shard], dy_full.at[pl.ds(pl.multiple_of(shard * rows, rows), rows)], full_sems.at[shard])

    def compute(step, shard):
        slot = step % 2
        here = pl.ds(pl.multiple_of(shard * rows, rows), rows)
        fetch = [pltpu.make_async_copy(src.at[here], dst, in_sems.at[idx]) for idx, (src, dst) in enumerate(((gate_hbm, gate_in), (up_hbm, up_in)))]
        for item in fetch:
            item.start()
        keep(shard).start()
        writer.reuse(step, shard)
        dy_rows = full[shard]
        stages[0][slot] = dot_nt(dy_rows, w_out[...]).astype(BF16)
        d_hidden = dot_nt(dy_rows, w_down[...]).astype(BF16).astype(F32)
        for item in fetch:
            item.wait()
        gate, up = gate_in[...].astype(F32), up_in[...].astype(F32)
        sig = jax.nn.sigmoid(gate)
        act = gate * sig
        stages[1][slot] = (act * up).astype(BF16)
        stages[2][slot] = (d_hidden * up * (sig + act * (1.0 - sig))).astype(BF16)
        stages[3][slot] = (d_hidden * act).astype(BF16)
        writer.start(step, shard)

    gather_shards(dy_hbm, full, send_sems, recv_sems, local_sem, before, compute)
    writer.finish()
    for shard in range(full.shape[0]):
        keep(shard).wait()


def down_backward(dy_loc, w_out, w_down, gate_act, up_act, layer, tp_size):
    rows, width = dy_loc.shape
    seq_len = rows * tp_size
    head_cols, ff_cols = w_out.shape[1], w_down.shape[1]
    out_cols = [head_cols, ff_cols, ff_cols, ff_cols]
    outs = [jax.ShapeDtypeStruct((seq_len, cols), BF16) for cols in out_cols + [width]]
    scratch = [pltpu.VMEM((2, rows, cols), BF16) for cols in out_cols]
    scratch += [pltpu.VMEM((rows, ff_cols), BF16)] * 2
    scratch += [pltpu.VMEM((cols, width), BF16) for cols in (head_cols, ff_cols)]
    scratch += gather_scratch(tp_size, rows, width)
    scratch += [pltpu.SemaphoreType.DMA((2,)), pltpu.SemaphoreType.DMA((4, 2)), pltpu.SemaphoreType.DMA((2,)), pltpu.SemaphoreType.DMA((tp_size,))]
    total = head_cols + ff_cols
    return pl.pallas_call(
        functools.partial(down_kernel, layer),
        out_shape=outs,
        in_specs=[ANY] * 5,
        out_specs=[ANY] * 5,
        scratch_shapes=scratch,
        compiler_params=params(collective_id=3 + layer),
        cost_estimate=cost(2 * seq_len * width * total, 2 * (width * total + 3 * seq_len * total)),
        name=f'down_backward_{layer}',
    )(dy_loc, w_out, w_down, gate_act, up_act)


def scatter_blocks(blocks_each, load_block, product, tmp, acc, ring, pair_send, pair_recv, ring_send, ring_recv):
    me, chip, core = ring_place()
    partner = device_at(chip, 1 - core)
    right, left = device_at(chip + 1, core), device_at(chip - 1, core)
    per_step = 2 * blocks_each
    n_blocks = N_CHIPS * per_step
    slots = tmp.shape[0]
    meet((partner, right, left))

    def place(block):
        step = block // per_step
        way = block % 2
        dest = (chip + (1 + step) * (2 * way - 1) + 2 * N_CHIPS) % N_CHIPS
        cols = way * blocks_each + (block % per_step) // 2
        return step, way, dest, cols

    def to_partner(block):
        return remote_copy(tmp.at[block % slots, 1 - core], acc.at[block], pair_send.at[block % slots], pair_recv.at[block], partner)

    def to_next(block):
        way = block % 2
        peer = device_at(chip + 1 - 2 * way, core)
        return remote_copy(acc.at[block], ring.at[block], ring_send.at[block], ring_recv.at[block], peer)

    def body(block, carry):
        @pl.when(block < n_blocks)
        def _():
            step, way, dest, cols = place(block)
            load_block(block)

            @pl.when(block >= slots)
            def _():
                to_partner(block - slots).wait_send()

            product(dest, cols, tmp.at[block % slots])
            to_partner(block).start()

        @pl.when(block >= 1)
        def _():
            last = block - 1
            to_partner(last).wait_recv()

            @pl.when(last < per_step)
            def _():
                acc[last] = acc[last] + tmp[last % slots, core]

            @pl.when(last >= per_step)
            def _():
                to_next(last - per_step).wait_recv()
                acc[last] = (acc[last] + tmp[last % slots, core]) + ring[last - per_step]

            @pl.when(last < n_blocks - per_step)
            def _():
                to_next(last).start()

        return carry

    lax.fori_loop(0, n_blocks + 1, body, 0)
    for block in range(n_blocks - slots, n_blocks):
        to_partner(block).wait_send()
    for block in range(n_blocks - per_step):
        to_next(block).wait_send()
    return lambda cols: acc.at[n_blocks - per_step + 2 * (cols % blocks_each) + cols // blocks_each]


def scatter_scratch(blocks_each, rows, width):
    per_step = 2 * blocks_each
    n_blocks = N_CHIPS * per_step
    cols = width // per_step
    return [
        pltpu.VMEM((3, 2, rows, cols), F32),
        pltpu.VMEM((n_blocks, rows, cols), F32),
        pltpu.VMEM((n_blocks - per_step, rows, cols), F32),
        pltpu.SemaphoreType.DMA((3,)),
        pltpu.SemaphoreType.DMA((n_blocks,)),
        pltpu.SemaphoreType.DMA((n_blocks - per_step,)),
        pltpu.SemaphoreType.DMA((n_blocks - per_step,)),
    ]


BLOCKS_EACH = 2
ROWS_AT_ONCE = 32


def row_loads(pairs, sems, rows, chip):
    def load(order, hop):
        span = pl.ds(pl.multiple_of(((chip + hop) % N_CHIPS) * rows, rows), rows)
        return [pltpu.make_async_copy(src.at[span], dst.at[span], sems.at[idx, order]) for idx, (src, dst) in enumerate(pairs)]

    return [load(order, hop) for order, hop in enumerate((3, 1, 2, 0))]


def forward_kernel(layer, next_gain, o_hbm, m_hbm, w_out_hbm, w_down_hbm, x_ref, gain_ref, y_ref, u_ref, o_all, m_all, w_out, w_down, row_sems, w_sems, *scatter):
    me, chip, core = ring_place()
    per_step = 2 * BLOCKS_EACH
    rows = x_ref.shape[0]
    width = x_ref.shape[1]
    block_cols = width // per_step
    loads = row_loads(((o_hbm, o_all), (m_hbm, m_all)), row_sems, 2 * rows, chip)

    def w_load(cols):
        span = pl.ds(cols * block_cols, block_cols)
        return [
            pltpu.make_async_copy(src.at[layer, :, span], dst.at[cols], w_sems.at[idx, cols])
            for idx, (src, dst) in enumerate(((w_out_hbm, w_out), (w_down_hbm, w_down)))
        ]

    order = [way * BLOCKS_EACH + j for j in range(BLOCKS_EACH) for way in range(2)]
    for block, cols in enumerate(order):
        for item in w_load(cols):
            item.start()
        if block < 2:
            for item in loads[block]:
                item.start()
    for block in range(2, 4):
        for item in loads[block]:
            item.start()

    def load_block(block):
        for idx, cols in enumerate(order):
            @pl.when(block == idx)
            def _():
                for item in w_load(cols):
                    item.wait()

        for idx, at in enumerate((0, 1, per_step, 3 * per_step)):
            @pl.when(block == at)
            def _():
                for item in loads[idx]:
                    item.wait()

    def product(dest, cols, out):
        span = pl.ds(pl.multiple_of(dest * 2 * rows, 2 * rows), 2 * rows)
        total = dot(o_all[span], w_out[cols]) + dot(m_all[span], w_down[cols])
        out[0] = total[:rows]
        out[1] = total[rows:]

    result = scatter_blocks(BLOCKS_EACH, load_block, product, *scatter)

    def finish(idx, carry):
        span = pl.ds(pl.multiple_of(idx * ROWS_AT_ONCE, ROWS_AT_ONCE), ROWS_AT_ONCE)
        summed = jnp.concatenate([result(cols)[span] for cols in range(per_step)], axis=1)
        y = (x_ref[span].astype(F32) + summed).astype(BF16)
        y_ref[span] = y
        u_ref[span] = rms_scale(y.astype(F32), gain_ref[next_gain:next_gain + 1]).astype(BF16)
        return carry

    lax.fori_loop(0, rows // ROWS_AT_ONCE, finish, 0)


def block_output(attn_out, hidden, w_out, w_down, x_loc, norm_gain, layer):
    rows, width = x_loc.shape
    seq_len = attn_out.shape[0]
    head_cols, ff_cols = w_out.shape[1], w_down.shape[1]
    per_step = 2 * BLOCKS_EACH
    cols = width // per_step
    shard = jax.ShapeDtypeStruct((rows, width), BF16)
    return pl.pallas_call(
        functools.partial(forward_kernel, layer, layer + 1),
        out_shape=[shard, shard],
        in_specs=[ANY] * 4 + [VMEM] * 2,
        out_specs=[VMEM] * 2,
        scratch_shapes=[
            pltpu.VMEM((seq_len, head_cols), BF16),
            pltpu.VMEM((seq_len, ff_cols), BF16),
            pltpu.VMEM((per_step, head_cols, cols), BF16),
            pltpu.VMEM((per_step, ff_cols, cols), BF16),
            pltpu.SemaphoreType.DMA((2, 4)),
            pltpu.SemaphoreType.DMA((2, per_step)),
        ] + scatter_scratch(BLOCKS_EACH, rows, width),
        compiler_params=params(collective_id=5 + layer),
        cost_estimate=cost(2 * seq_len * width * (head_cols + ff_cols), 4 * seq_len * (head_cols + ff_cols)),
        name=f'block_output_{layer}',
    )(attn_out, hidden, w_out, w_down, x_loc, norm_gain)


def backward_kernel(layer, dqkv_hbm, dgate_hbm, dup_hbm, w_qkv_hbm, w_gate_hbm, w_up_hbm, x_ref, dy_ref, gain_ref, dx_ref, dgain_ref, *rest):
    acts, rest = rest[:3], rest[3:]
    weights, rest = rest[:3], rest[3:]
    row_sems, w_sems, *scatter = rest
    me, chip, core = ring_place()
    per_step = 2 * BLOCKS_EACH
    rows, width = x_ref.shape
    block_cols = width // per_step
    loads = row_loads(list(zip((dqkv_hbm, dgate_hbm, dup_hbm), acts)), row_sems, 2 * rows, chip)

    def w_load(cols):
        span = pl.ds(cols * block_cols, block_cols)
        return [
            pltpu.make_async_copy(src.at[layer, span], dst.at[span], w_sems.at[idx, cols])
            for idx, (src, dst) in enumerate(zip((w_qkv_hbm, w_gate_hbm, w_up_hbm), weights))
        ]

    order = [way * BLOCKS_EACH + j for j in range(BLOCKS_EACH) for way in range(2)]
    for block, cols in enumerate(order):
        for item in w_load(cols):
            item.start()
        if block < 2:
            for item in loads[block]:
                item.start()
    for block in range(2, 4):
        for item in loads[block]:
            item.start()

    def load_block(block):
        for idx, cols in enumerate(order):
            @pl.when(block == idx)
            def _():
                for item in w_load(cols):
                    item.wait()

        for idx, at in enumerate((0, 1, per_step, 3 * per_step)):
            @pl.when(block == at)
            def _():
                for item in loads[idx]:
                    item.wait()

    def product(dest, cols, out):
        span = pl.ds(pl.multiple_of(dest * 2 * rows, 2 * rows), 2 * rows)
        w_span = pl.ds(pl.multiple_of(cols * block_cols, block_cols), block_cols)
        total = dot_nt(acts[0][span], weights[0][w_span]) + dot_nt(acts[1][span], weights[1][w_span]) + dot_nt(acts[2][span], weights[2][w_span])
        out[0] = total[:rows]
        out[1] = total[rows:]

    result = scatter_blocks(BLOCKS_EACH, load_block, product, *scatter)
    gain_row = gain_ref[layer:layer + 1]
    dgain_ref[...] = jnp.zeros_like(dgain_ref)

    def finish(idx, carry):
        span = pl.ds(pl.multiple_of(idx * ROWS_AT_ONCE, ROWS_AT_ONCE), ROWS_AT_ONCE)
        summed = jnp.concatenate([result(cols)[span] for cols in range(per_step)], axis=1)
        d_normed = summed.astype(BF16).astype(F32)
        x_f32 = x_ref[span].astype(F32)
        inv_rms = lax.rsqrt(jnp.mean(x_f32 * x_f32, axis=-1, keepdims=True) + NORM_EPS)
        scaled = d_normed * gain_row
        dgain_ref[...] += jnp.sum(d_normed * (x_f32 * inv_rms), axis=0, keepdims=True)
        mix = jnp.mean(scaled * x_f32, axis=-1, keepdims=True) * (inv_rms * inv_rms * inv_rms)
        dx_ref[span] = (dy_ref[span].astype(F32) + (scaled * inv_rms - x_f32 * mix)).astype(BF16)
        return carry

    lax.fori_loop(0, rows // ROWS_AT_ONCE, finish, 0)


def block_input_backward(d_qkv, d_gate, d_up, w_qkv, w_gate, w_up, x_loc, dy_loc, norm_gain, layer):
    rows, width = x_loc.shape
    seq_len = d_qkv.shape[0]
    all_cols = (w_qkv.shape[2], w_gate.shape[2], w_up.shape[2])
    per_step = 2 * BLOCKS_EACH
    return pl.pallas_call(
        functools.partial(backward_kernel, layer),
        out_shape=[jax.ShapeDtypeStruct((rows, width), BF16), jax.ShapeDtypeStruct((1, width), F32)],
        in_specs=[ANY] * 6 + [VMEM] * 3,
        out_specs=[VMEM] * 2,
        scratch_shapes=[pltpu.VMEM((seq_len, cols), BF16) for cols in all_cols]
        + [pltpu.VMEM((width, cols), BF16) for cols in all_cols]
        + [pltpu.SemaphoreType.DMA((3, 4)), pltpu.SemaphoreType.DMA((3, per_step))]
        + scatter_scratch(BLOCKS_EACH, rows, width),
        compiler_params=params(collective_id=7 + layer),
        cost_estimate=cost(2 * seq_len * width * sum(all_cols), 4 * seq_len * sum(all_cols)),
        name=f'block_input_backward_{layer}',
    )(d_qkv, d_gate, d_up, w_qkv, w_gate, w_up, x_loc, dy_loc, norm_gain)


Q_ROWS = 256


def causal_tile(size):
    return lax.broadcasted_iota(jnp.int32, (size, size), 0) >= lax.broadcasted_iota(jnp.int32, (size, size), 1)


def masked_scores(query, keys, q_start):
    size = query.shape[0]
    scores = dot_nt(query, keys[:q_start + size])
    diagonal = jnp.where(causal_tile(size), scores[:, q_start:], -1e30)
    return diagonal if q_start == 0 else jnp.concatenate([scores[:, :q_start], diagonal], axis=1)


def attention_kernel(qkv_ref, o_ref, lse_ref):
    seq_len = qkv_ref.shape[0]
    keys = qkv_ref[:, HEAD_DIM:2 * HEAD_DIM]
    values = qkv_ref[:, 2 * HEAD_DIM:]
    for q_start in range(0, seq_len, Q_ROWS):
        span = slice(q_start, q_start + Q_ROWS)
        scores = masked_scores(qkv_ref[span, :HEAD_DIM], keys, q_start) * (SCALE * LOG2E)
        row_max = jnp.max(scores, axis=-1, keepdims=True)
        prob = jnp.exp2(scores - row_max)
        norm = jnp.sum(prob, axis=-1, keepdims=True)
        prob = (prob * (1.0 / norm)).astype(BF16)
        o_ref[span] = dot(prob, values[:q_start + Q_ROWS]).astype(BF16)
        lse_ref[span] = jnp.broadcast_to(row_max + jnp.log2(norm), (Q_ROWS, HEAD_DIM))


def attention(qkv):
    seq_len, cols = qkv.shape
    heads = cols // (3 * HEAD_DIM)
    work = heads * seq_len * seq_len
    return pl.pallas_call(
        attention_kernel,
        grid=(heads,),
        out_shape=[jax.ShapeDtypeStruct((seq_len, heads * HEAD_DIM), BF16), jax.ShapeDtypeStruct((seq_len, heads * HEAD_DIM), F32)],
        in_specs=[pl.BlockSpec((seq_len, 3 * HEAD_DIM), lambda h: (0, h))],
        out_specs=[pl.BlockSpec((seq_len, HEAD_DIM), lambda h: (0, h))] * 2,
        compiler_params=params(semantics=('arbitrary',)),
        cost_estimate=cost(8 * work * HEAD_DIM // 2, 2 * seq_len * cols, work // 2),
        name='attention',
    )(qkv)


def attention_backward_kernel(qkv_ref, lse_ref, do_ref, cos_ref, sin_ref, dqkv_ref, dk_acc, dv_acc):
    seq_len = qkv_ref.shape[0]
    keys = qkv_ref[:, HEAD_DIM:2 * HEAD_DIM]
    values = qkv_ref[:, 2 * HEAD_DIM:]
    dk_acc[...] = jnp.zeros_like(dk_acc)
    dv_acc[...] = jnp.zeros_like(dv_acc)

    def unrotate(cotangent, span):
        return rotate(cotangent.astype(BF16).astype(F32), cos_ref[span], -sin_ref[span]).astype(BF16)

    for q_start in range(0, seq_len, Q_ROWS):
        span = slice(q_start, q_start + Q_ROWS)
        seen = slice(0, q_start + Q_ROWS)
        query = qkv_ref[span, :HEAD_DIM]
        d_out = do_ref[span]
        scores = masked_scores(query, keys, q_start) * (SCALE * LOG2E)
        prob = jnp.exp2(scores - lse_ref[span, :1])
        d_prob = dot_nt(d_out, values[seen]).astype(BF16).astype(F32)
        dv_acc[seen] += dot_tn(prob.astype(BF16), d_out)
        inner = jnp.sum(prob * d_prob, axis=-1, keepdims=True)
        d_scores = (prob * (d_prob - inner) * SCALE).astype(BF16)
        dqkv_ref[span, :HEAD_DIM] = unrotate(dot(d_scores, keys[seen]), span)
        dk_acc[seen] += dot_tn(d_scores, query)
    everything = slice(0, seq_len)
    dqkv_ref[:, HEAD_DIM:2 * HEAD_DIM] = unrotate(dk_acc[...], everything)
    dqkv_ref[:, 2 * HEAD_DIM:] = dv_acc[...].astype(BF16)


def attention_backward(qkv, lse, d_attn, tables):
    seq_len, cols = qkv.shape
    heads = cols // (3 * HEAD_DIM)
    work = heads * seq_len * seq_len
    head_block = pl.BlockSpec((seq_len, HEAD_DIM), lambda h: (0, h))
    table_block = pl.BlockSpec((seq_len, HEAD_DIM), lambda h: (0, 0))
    qkv_block = pl.BlockSpec((seq_len, 3 * HEAD_DIM), lambda h: (0, h))
    return pl.pallas_call(
        attention_backward_kernel,
        grid=(heads,),
        out_shape=jax.ShapeDtypeStruct((seq_len, cols), BF16),
        in_specs=[qkv_block, head_block, head_block, table_block, table_block],
        out_specs=qkv_block,
        scratch_shapes=[pltpu.VMEM((seq_len, HEAD_DIM), F32)] * 2,
        compiler_params=params(semantics=('arbitrary',)),
        cost_estimate=cost(20 * work * HEAD_DIM // 2, 6 * seq_len * cols, work // 2),
        name='attention_backward',
    )(qkv, lse, d_attn, *tables)


def weight_grad_kernel(n_pairs, n_held, lhs_refs_first, *refs):
    ins, outs = refs[:n_pairs + 1 + n_held], refs[n_pairs + 1 + n_held:]
    shared, others = ins[0], ins[1:1 + n_pairs]
    for other, out in zip(others, outs):
        lhs, rhs = (shared, other) if lhs_refs_first else (other, shared)
        out[0] = dot_tn(lhs[...], rhs[...]).astype(BF16)


def weight_grads(shared, others, held, layer, n_layers, shared_is_lhs, block):
    seq_len, width = shared.shape
    n_pairs = len(others)
    n_held = len(held)
    shapes = [(width, item.shape[1]) if shared_is_lhs else (item.shape[1], width) for item in others]
    if shared_is_lhs:
        out_specs = [pl.BlockSpec((1, block, item.shape[1]), lambda i: (layer, i, 0)) for item in others]
    else:
        out_specs = [pl.BlockSpec((1, item.shape[1], block), lambda i: (layer, 0, i)) for item in others]
    total = sum(item.shape[1] for item in others)
    return pl.pallas_call(
        functools.partial(weight_grad_kernel, n_pairs, n_held, shared_is_lhs),
        grid=(width // block,),
        out_shape=[jax.ShapeDtypeStruct((n_layers,) + shape, BF16) for shape in shapes],
        in_specs=[pl.BlockSpec((seq_len, block), lambda i: (0, i))]
        + [pl.BlockSpec(item.shape, lambda i: (0, 0), pipeline_mode=pl.Buffered(1)) for item in others]
        + [ANY] * n_held,
        out_specs=out_specs,
        input_output_aliases={1 + n_pairs + idx: idx for idx in range(n_held)},
        compiler_params=params(semantics=('arbitrary',)),
        cost_estimate=cost(2 * seq_len * width * total, 2 * (seq_len * (width + total) + width * total)),
        name=f'weight_grads_{layer}',
    )(shared, *others, *held)


def solution(mesh):
    tp_size = mesh.shape['tp']
    assert tp_size == 2 * N_CHIPS
    row_spec = P(('dp', 'tp'), None)
    col_spec = P(None, None, 'tp')
    inner_spec = P(None, 'tp', None)

    def device_program(x_loc, dy_loc, norm_gain, w_qkv, w_out, w_gate, w_up, w_down):
        n_layers = w_qkv.shape[0]
        seq_len = x_loc.shape[0] * tp_size
        tables = tuple(jnp.asarray(table) for table in rope_tables(seq_len))
        x_cur = x_loc
        u_loc = rms_scale(x_loc.astype(F32), norm_gain[0]).astype(BF16)
        saved = []
        for layer in range(n_layers):
            last = layer == n_layers - 1
            projected = project(u_loc, w_qkv, w_gate, w_up, tables, layer, tp_size, not last)
            qkv, gate_act, up_act = projected[:3]
            attn_out, lse = attention(qkv)
            saved.append((x_cur, u_loc, qkv, gate_act, up_act, attn_out, lse))
            if not last:
                x_cur, u_loc = block_output(attn_out, projected[3], w_out, w_down, x_cur, norm_gain, layer)
        grad_cur = dy_loc
        grads_in, grads_out, gains = (), (), [None] * n_layers
        for layer in reversed(range(n_layers)):
            x_cur, u_loc, qkv, gate_act, up_act, attn_out, lse = saved[layer]
            d_attn, hidden, d_gate, d_up, dy_full = down_backward(grad_cur, w_out, w_down, gate_act, up_act, layer, tp_size)
            u_loc, d_attn = lax.optimization_barrier((u_loc, d_attn))
            u_full = lax.all_gather(u_loc, 'tp', axis=0, tiled=True)
            d_qkv = attention_backward(qkv, lse, d_attn, tables)
            grad_cur, gains[layer] = block_input_backward(d_qkv, d_gate, d_up, w_qkv, w_gate, w_up, x_cur, grad_cur, norm_gain, layer)
            grads_out = weight_grads(dy_full, (attn_out, hidden), grads_out, layer, n_layers, False, 512)
            grads_in = weight_grads(u_full, (d_qkv, d_gate, d_up), grads_in, layer, n_layers, True, 512)
        grad_gain = lax.psum(jnp.concatenate(gains, axis=0), 'tp')
        return (grad_cur, grad_gain, grads_in[0], grads_out[0], grads_in[1], grads_in[2], grads_out[1])

    return jax.shard_map(
        device_program,
        mesh=mesh,
        in_specs=(row_spec, row_spec, P(None, None), col_spec, inner_spec, col_spec, col_spec, inner_spec),
        out_specs=(row_spec, P('dp', None), P('dp', None, 'tp'), P('dp', 'tp', None), P('dp', None, 'tp'), P('dp', None, 'tp'), P('dp', 'tp', None)),
        check_vma=False,
    )
```

time: 1150 us -> 672 us (0.58)
  Pallas kernels: 0 us -> 619 us
  matrix products: 568 us -> 0 us
  waiting for transfers between devices: 357 us -> 0.11 us
  other arithmetic: 150 us -> 4.74 us
  local copies, waits for them, and re-layouts: 27.1 us -> 1.71 us
    pallas_call x0 -> x15, Pallas kernels: none -> 619 us  [the longest x2 181 us: block_input_backward(): pl.pallas_call(functools.partial(backward_kernel, layer), out_shape=[jax....]
    dot_general x42 -> x0, matrix products: 568 us -> none  [the longest x4 76 us: causal_scores(): jnp.einsum('skgd,tkd->kgst', query, keys_rot, preferred_element_type=jnp....]
    all_gather x6 -> x2, waiting for transfers between devices: 181 us -> 0.01 us  [device_program(): u_full = lax.all_gather(u_loc, 'tp', axis=0, tiled=True)]
    reduce_scatter x3 -> x0, waiting for transfers between devices: 174 us -> none  [the longest x1 88.2 us: block_forward(): lax.psum_scatter(block_part, 'tp', scatter_dimension=0, tiled=True)]
    another operation x11 -> x0, other arithmetic: 77.4 us -> none
    reduce_sum x4 -> x0, other arithmetic: 34.7 us -> none  [the longest x2 29.6 us: block_forward(): jnp.sum(jnp.exp(scores - row_max), axis=-1, keepdims=True)]
    unnamed x108 -> x5, local copies, waits for them, and re-layouts: 14.5 us -> 0.98 us
    convert_element_type x8 -> x1, other arithmetic: 16.1 us -> 2.5 us  [device_program(): u_loc = rms_scale(x_loc.astype(F32), norm_gain[0]).astype(BF16)]
  transfers between devices with their start and end apart: 9 -> 2, of which waited for: 6 -> 0; matrix products, arithmetic and copies ran while one was open for 29% -> 0% of each run, Pallas kernels for 0% -> 52%
where the time goes in v1:
time: 672 us; the launch traced here: 661 us
  Pallas kernels  619 us (92%)
  blocking collectives  20.8 us (3%)
  between operations  14.6 us (2%)
    pallas_call x2, Pallas kernels, block_input_backward(): pl.pallas_call(functools.partial(backward_kernel, layer), out_shape=[jax....  181 us
    pallas_call x2, Pallas kernels, project(): pl.pallas_call(functools.partial(project_kernel, layer, with_hidden), out...  102 us
    pallas_call x4, Pallas kernels, weight_grads(): pl.pallas_call(functools.partial(weight_grad_kernel, n_pairs, n_held, sha...  93.3 us
    pallas_call x2, Pallas kernels, down_backward(): pl.pallas_call(functools.partial(down_kernel, layer), out_shape=outs, in_...  92.7 us
    pallas_call x1, Pallas kernels, block_output(): pl.pallas_call(functools.partial(forward_kernel, layer, layer + 1), out_s...  80.7 us
    pallas_call x2, Pallas kernels, attention_backward(): pl.pallas_call(attention_backward_kernel, grid=(heads,), out_shape=jax.Sh...  41.8 us
    pallas_call x2, Pallas kernels, attention(): pl.pallas_call(attention_kernel, grid=(heads,), out_shape=[jax.ShapeDtype...  28.3 us
    psum x1, blocking collectives, device_program(): grad_gain = lax.psum(jnp.concatenate(gains, axis=0), 'tp')  20.8 us
  transfers between devices with their start and end apart: 2, of which 0 were waited for; matrix products, arithmetic and copies ran while one was open for 0% of the time, Pallas kernels for 52%

profile of v1, /device:TPU:81, one launch (start us, length us, event | category | flops | bytes accessed | tf_op | source)
XLA Modules:
  0.0 661.3 jit_solution(15012304440371005055)
XLA Ops:
  7.2 0.1 all-gather.5.cloned.1.call-start
  7.2 1.5 fusion
  8.8 0.7 slice.3
  9.5 2.5 fusion.2.u_hbm
  12.0 52.4 %project_0.1 = (bf16[2048,768]{1,0:T(8,128)(2,1)}, bf16[2048,1024]{1,0:T(8,128)(2,1)}, bf16[2048,1024]{1,0:T(8,128)(2,1)}, bf16[2048,1024]{1,0:T(8,128)(2,1)}) custom-call(bf16[256,2048]{1,0:T(8,128)(2,1)} %fusion.2.u_hbm, bf16[2,2048,768]{2,1,0:T(8,128)(2,1)} %w_qkv_hbm.7, bf16[2,2048,1024]{2,1,0:T(8,128)(2,1)} %w_gate_hbm.7, ...), custom_call_target="tpu_custom_call" | custom-call | flops 23622320128 | bytes 23068672 | tf_op jit(solution)/shard_map/project_0/pallas_call | solution.py:266
  64.4 14.2 %attention.2 = (bf16[2048,256]{1,0:T(8,128)(2,1)}, f32[2048,256]{1,0:T(8,128)}) custom-call(bf16[2048,768]{1,0:T(8,128)(2,1)} %get-tuple-element.48.qkv_ref), custom_call_target="tpu_custom_call" | custom-call | flops 4294967296 | bytes 3145728 | tf_op jit(solution)/shard_map/attention/pallas_call | solution.py:646
  78.5 80.7 %block_output_0.1 = (bf16[256,2048]{1,0:T(8,128)(2,1)}, bf16[256,2048]{1,0:T(8,128)(2,1)}) custom-call(bf16[2048,256]{1,0:T(8,128)(2,1)} %get-tuple-element.50.o_hbm.refs_1_, bf16[2048,1024]{1,0:T(8,128)(2,1)} %get-tuple-element.51.m_hbm, bf16[2,256,2048]{2,1,0:T(8,128)(2,1)} %w_out_hbm.5, bf16[2,1024,2048]{2,1,0:T(8,128)(2,1)} %w_down_hbm.5, ...), custom_call_target="tpu_custom_call" | custom-call | flops 10737418240 | bytes 10485760 | tf_op jit(solution)/shard_map/block_output_0/pallas_call | solution.py:507
  159.3 49.5 %project_1.1 = (bf16[2048,768]{1,0:T(8,128)(2,1)}, bf16[2048,1024]{1,0:T(8,128)(2,1)}, bf16[2048,1024]{1,0:T(8,128)(2,1)}) custom-call(bf16[256,2048]{1,0:T(8,128)(2,1)} %get-tuple-element.73.u_hbm, bf16[2,2048,768]{2,1,0:T(8,128)(2,1)} %w_qkv_hbm.7, bf16[2,2048,1024]{2,1,0:T(8,128)(2,1)} %w_gate_hbm.7, bf16[2,2048,1024]{2,1,0:T(8,128)(2,1)} %w_up_hbm.7, ...), custom_call_target="tpu_custom_call" | custom-call | flops 23622320128 | bytes 23068672 | tf_op jit(solution)/shard_map/project_1/pallas_call | solution.py:266
  208.7 47.6 %down_backward_1.1 = (bf16[2048,256]{1,0:T(8,128)(2,1)}, bf16[2048,1024]{1,0:T(8,128)(2,1)}, bf16[2048,1024]{1,0:T(8,128)(2,1)}, bf16[2048,1024]{1,0:T(8,128)(2,1)}, bf16[2048,2048]{1,0:T(8,128)(2,1)}) custom-call(bf16[256,2048]{1,0:T(8,128)(2,1)} %dy_ref.1, bf16[2,256,2048]{2,1,0:T(8,128)(2,1)} %w_out_hbm.5, bf16[2,1024,2048]{2,1,0:T(8,128)(2,1)} %w_down_hbm.5, ...), custom_call_target="tpu_custom_call" | custom-call | flops 10737418240 | bytes 20971520 | tf_op jit(solution)/shard_map/down_backward_1/pallas_call | solution.py:338
  256.3 0.1 all-gather.5.cloned.1.call-update
  256.4 0.1 all-gather.3.cloned.1.call-start
  256.4 14.2 %attention.3 = (bf16[2048,256]{1,0:T(8,128)(2,1)}, f32[2048,256]{1,0:T(8,128)}) custom-call(bf16[2048,768]{1,0:T(8,128)(2,1)} %get-tuple-element.53.qkv_ref), custom_call_target="tpu_custom_call" | custom-call | flops 4294967296 | bytes 3145728 | tf_op jit(solution)/shard_map/attention/pallas_call | solution.py:646
  270.6 21.1 %attention_backward.2.dqkv_hbm.refs_1_ = bf16[2048,768]{1,0:T(8,128)(2,1)} custom-call(bf16[2048,768]{1,0:T(8,128)(2,1)} %get-tuple-element.53.qkv_ref, f32[2048,256]{1,0:T(8,128)} %get-tuple-element.54.lse_ref, bf16[2048,256]{1,0:T(8,128)(2,1)} %get-tuple-element.58.do_ref, f32[2048,128]{1,0:T(8,128)} %constant.11.clone.cos_ref, ...), custom_call_target="tpu_custom_call" | custom-call | flops 10737418240 | bytes 9437184 | tf_op jit(solution)/shard_map/attention_backward/pallas_call | solution.py:693
  291.7 82.9 %block_input_backward_1.1 = (bf16[256,2048]{1,0:T(8,128)(2,1)}, f32[1,2048]{1,0:T(1,128)}) custom-call(bf16[2048,768]{1,0:T(8,128)(2,1)} %attention_backward.2.dqkv_hbm.refs_1_, bf16[2048,1024]{1,0:T(8,128)(2,1)} %get-tuple-element.59.dgate_hbm.refs_2_, bf16[2048,1024]{1,0:T(8,128)(2,1)} %get-tuple-element.60.dup_hbm.refs_3_, ...), custom_call_target="tpu_custom_call" | custom-call | flops 23622320128 | bytes 23068672 | tf_op jit(solution)/shard_map/block_input_backward_1/pallas_call | solution.py:598
  374.7 45.1 %down_backward_0.1 = (bf16[2048,256]{1,0:T(8,128)(2,1)}, bf16[2048,1024]{1,0:T(8,128)(2,1)}, bf16[2048,1024]{1,0:T(8,128)(2,1)}, bf16[2048,1024]{1,0:T(8,128)(2,1)}, bf16[2048,2048]{1,0:T(8,128)(2,1)}) custom-call(bf16[256,2048]{1,0:T(8,128)(2,1)} %get-tuple-element.62.dy_hbm.dy_ref, bf16[2,256,2048]{2,1,0:T(8,128)(2,1)} %w_out_hbm.5, ...), custom_call_target="tpu_custom_call" | custom-call | flops 10737418240 | bytes 20971520 | tf_op jit(solution)/shard_map/down_backward_0/pallas_call | solution.py:338
  419.8 0.1 all-gather.3.cloned.1.call-update
  419.8 20.7 %attention_backward.3.dqkv_hbm.refs_1_ = bf16[2048,768]{1,0:T(8,128)(2,1)} custom-call(bf16[2048,768]{1,0:T(8,128)(2,1)} %get-tuple-element.48.qkv_ref, f32[2048,256]{1,0:T(8,128)} %get-tuple-element.49.lse_ref, bf16[2048,256]{1,0:T(8,128)(2,1)} %get-tuple-element.66.do_ref, f32[2048,128]{1,0:T(8,128)} %constant.11.clone.cos_ref, ...), custom_call_target="tpu_custom_call" | custom-call | flops 10737418240 | bytes 9437184 | tf_op jit(solution)/shard_map/attention_backward/pallas_call | solution.py:693
  440.5 0.0 copy-start.1
  440.5 97.6 %block_input_backward_0.1 = (bf16[256,2048]{1,0:T(8,128)(2,1)}, f32[1,2048]{1,0:T(1,128)}) custom-call(bf16[2048,768]{1,0:T(8,128)(2,1)} %attention_backward.3.dqkv_hbm.refs_1_, bf16[2048,1024]{1,0:T(8,128)(2,1)} %get-tuple-element.67.dgate_hbm.refs_2_, bf16[2048,1024]{1,0:T(8,128)(2,1)} %get-tuple-element.68.dup_hbm.refs_3_, ...), custom_call_target="tpu_custom_call" | custom-call | flops 23622320128 | bytes 23068672 | tf_op jit(solution)/shard_map/block_input_backward_0/pallas_call | solution.py:598
  538.1 0.0 copy-done.1
  538.1 0.7 pad_maximum_fusion
  538.9 20.8 %psum.7 = f32[2,2048]{1,0:T(2,128)} all-reduce(f32[2,2048]{1,0:T(2,128)S(1)} %pad_maximum_fusion), channel_id=1, replica_groups=mesh['dp'=4,'tp'=8] {'tp'}, use_global_device_ids=true, to_apply=%region_1.0 | all-reduce | flops 4096 | bytes 32768 | tf_op jit(solution)/shard_map/psum | solution.py:772
  559.7 15.8 %weight_grads_1.3 = (bf16[2,256,2048]{2,1,0:T(8,128)(2,1)}, bf16[2,1024,2048]{2,1,0:T(8,128)(2,1)}) custom-call(bf16[2048,2048]{1,0:T(8,128)(2,1)} %get-tuple-element.80.refs_0_, bf16[2048,256]{1,0:T(8,128)(2,1)} %get-tuple-element.81.refs_1_, bf16[2048,1024]{1,0:T(8,128)(2,1)} %get-tuple-element.82.refs_2_), custom_call_target="tpu_custom_call" | custom-call | flops 10737418240 | bytes 18874368 | tf_op jit(solution)/shard_map/weight_grads_1/pallas_call | solution.py:724
  575.5 15.8 %weight_grads_0.3 = (bf16[2,256,2048]{2,1,0:T(8,128)(2,1)}, bf16[2,1024,2048]{2,1,0:T(8,128)(2,1)}) custom-call(bf16[2048,2048]{1,0:T(8,128)(2,1)} %get-tuple-element.78.refs_0_, bf16[2048,256]{1,0:T(8,128)(2,1)} %get-tuple-element.50.o_hbm.refs_1_, bf16[2048,1024]{1,0:T(8,128)(2,1)} %get-tuple-element.79.refs_2_, ...), custom_call_target="tpu_custom_call", output_to_operand_aliasing={{0}: (3, {}), {1}: (4, {})} | custom-call | flops 10737418240 | bytes 18874368 | tf_op jit(solution)/shard_map/weight_grads_0/pallas_call | solution.py:724
  591.3 0.0 all-gather.5.cloned.1.call-done.refs_0_
  591.3 30.7 %weight_grads_1.2 = (bf16[2,2048,768]{2,1,0:T(8,128)(2,1)}, bf16[2,2048,1024]{2,1,0:T(8,128)(2,1)}, bf16[2,2048,1024]{2,1,0:T(8,128)(2,1)}) custom-call(bf16[2048,2048]{1,0:T(8,128)(2,1)} %all-gather.5.cloned.1.call-done.refs_0_, bf16[2048,768]{1,0:T(8,128)(2,1)} %attention_backward.2.dqkv_hbm.refs_1_, ...), custom_call_target="tpu_custom_call" | custom-call | flops 23622320128 | bytes 31457280 | tf_op jit(solution)/shard_map/weight_grads_1/pallas_call | solution.py:724
  622.0 0.0 all-gather.3.cloned.1.call-done.refs_0_
  622.0 0.0 copy-start
  622.0 31.0 %weight_grads_0.2 = (bf16[2,2048,768]{2,1,0:T(8,128)(2,1)}, bf16[2,2048,1024]{2,1,0:T(8,128)(2,1)}, bf16[2,2048,1024]{2,1,0:T(8,128)(2,1)}) custom-call(bf16[2048,2048]{1,0:T(8,128)(2,1)} %all-gather.3.cloned.1.call-done.refs_0_, bf16[2048,768]{1,0:T(8,128)(2,1)} %attention_backward.3.dqkv_hbm.refs_1_, ...), custom_call_target="tpu_custom_call", output_to_operand_aliasing={{0}: (4, {}), {1}: (5, {}), {2}: (6, {})} | custom-call | flops 23622320128 | bytes 31457280 | tf_op jit(solution)/shard_map/weight_grads_0/pallas_call | solution.py:724
  653.0 0.0 copy-done
  653.0 1.0 copy.28
  (1 shorter events, 0.0 us)
Async XLA Ops:
  7.2 584.1 %all-gather.5.cloned.1.call-start = ((), (), s32[]{:S(2)}) async-start(), calls=%async_computation.1 | async-start | bytes 9437184 | tf_op jit(solution)/shard_map/all_gather | solution.py:767
  256.4 365.7 %all-gather.3.cloned.1.call-start = ((), (), s32[]{:S(2)}) async-start(), calls=%async_computation | async-start | bytes 9437184 | tf_op jit(solution)/shard_map/all_gather | solution.py:767
  440.5 97.6 %copy-start.1 = (f32[1,2048]{1,0:T(1,128)S(1)}, f32[1,2048]{1,0:T(1,128)}, u32[]{:S(2)}) copy-start(f32[1,2048]{1,0:T(1,128)} %get-tuple-element.71) | copy-start | bytes 24580
  622.0 31.0 %copy-start = (bf16[256,2048]{1,0:T(8,128)(2,1)S(1)}, bf16[256,2048]{1,0:T(8,128)(2,1)}, u32[]{:S(2)}) copy-start(bf16[256,2048]{1,0:T(8,128)(2,1)} %get-tuple-element.96) | copy-start | bytes 3145732
Sparse Core Ops, SparseCore 0:
  256.5 50.5 all-gather.4
  420.0 64.5 all-gather.2

commit v2 on v1

v2 whole, which is shorter than its diff:
```python
import functools

import jax
import jax.numpy as jnp
import numpy as np
from jax import lax
from jax.experimental import pallas as pl
from jax.experimental.pallas import tpu as pltpu
from jax.sharding import PartitionSpec as P

HEAD_DIM = 128
NORM_EPS = 1e-5
ROPE_BASE = 10000.0
SCALE = HEAD_DIM ** -0.5
LOG2E = 1.4426950408889634
VMEM_LIMIT = 64000 * 1024
N_CHIPS = 4
SUBS = 4
Q_ROWS = 256
ROWS_AT_ONCE = 32
BF16 = jnp.bfloat16
F32 = jnp.float32
ANY = pl.BlockSpec(memory_space=pl.ANY)
VMEM = pl.BlockSpec(memory_space=pltpu.VMEM)
NT = (((1,), (1,)), ((), ()))
TN = (((0,), (0,)), ((), ()))


def dot(lhs, rhs):
    return jnp.dot(lhs, rhs, preferred_element_type=F32)


def dot_nt(lhs, rhs):
    return lax.dot_general(lhs, rhs, NT, preferred_element_type=F32)


def dot_tn(lhs, rhs):
    return lax.dot_general(lhs, rhs, TN, preferred_element_type=F32)


def params(collective_id=None, semantics=None):
    if collective_id is None:
        return pltpu.CompilerParams(vmem_limit_bytes=VMEM_LIMIT, dimension_semantics=semantics)
    return pltpu.CompilerParams(vmem_limit_bytes=VMEM_LIMIT, collective_id=collective_id, has_side_effects=True)


def cost(flops, bytes_accessed, transcendentals=0):
    return pl.CostEstimate(flops=flops, bytes_accessed=bytes_accessed, transcendentals=transcendentals)


def rope_tables(seq_len):
    half_dim = HEAD_DIM // 2
    freqs = np.float32(ROPE_BASE) ** (np.float32(-2.0) * np.arange(half_dim, dtype=np.float32) / np.float32(HEAD_DIM))
    angles = np.arange(seq_len, dtype=np.float32)[:, None] * freqs[None, :].astype(np.float32)
    cos_half, sin_half = np.cos(angles).astype(np.float32), np.sin(angles).astype(np.float32)
    return np.concatenate([cos_half, cos_half], axis=1), np.concatenate([-sin_half, sin_half], axis=1)


def rotate(values, cos_tab, sin_tab):
    return values * cos_tab + pltpu.roll(values, HEAD_DIM // 2, 1) * sin_tab


def rms_scale(x_f32, gain_row):
    inv_rms = lax.rsqrt(jnp.mean(x_f32 * x_f32, axis=-1, keepdims=True) + NORM_EPS)
    return x_f32 * inv_rms * gain_row


def ring_place():
    me = lax.axis_index('tp')
    chip = me // 2
    core = me % 2
    return me, chip, core


def device_at(chip, core):
    return ((chip + N_CHIPS) % N_CHIPS) * 2 + core


def remote_copy(src, dst, send_sem, recv_sem, peer):
    return pltpu.make_async_remote_copy(
        src_ref=src, dst_ref=dst, send_sem=send_sem, recv_sem=recv_sem, device_id={'tp': peer}, device_id_type=pl.DeviceIdType.MESH
    )


def meet(peers):
    barrier = pltpu.get_barrier_semaphore()
    for peer in peers:
        pl.semaphore_signal(barrier, inc=1, device_id={'tp': peer}, device_id_type=pl.DeviceIdType.MESH)
    pl.semaphore_wait(barrier, len(peers))


class Gather:
    EVERY, EARLY, LATE = range(SUBS), range(SUBS // 2), range(SUBS // 2, SUBS)

    def __init__(self, full, send_sems, recv_sems):
        self.full, self.send_sems, self.recv_sems = full, send_sems, recv_sems
        self.me, chip, core = ring_place()
        turn = 1 - 2 * core
        self.chip, self.core, self.turn = chip, core, turn
        self.partner = device_at(chip, 1 - core)
        self.ahead = device_at(chip + turn, core)
        self.behind = device_at(chip - turn, core)
        self.first = device_at(chip - turn, core)
        self.first_other = device_at(chip + turn, 1 - core)
        self.second = device_at(chip + turn, core)
        self.second_other = device_at(chip - turn, 1 - core)
        self.third = device_at(chip + 2, core)
        self.third_other = device_at(chip + 2, 1 - core)

    def peers(self):
        return self.partner, self.ahead, self.behind

    def piece(self, kind, shard, sub, peer):
        rows = self.full.shape[1] // SUBS
        part = self.full.at[shard, pl.ds(sub * rows, rows)]
        return remote_copy(part, part, self.send_sems.at[kind, sub], self.recv_sems.at[shard, sub], peer)

    def send(self, kind, shard, peer):
        for sub in self.EVERY:
            self.piece(kind, shard, sub, peer).start()

    def sent(self, kind, shard, peer, subs=EVERY):
        for sub in subs:
            self.piece(kind, shard, sub, peer).wait_send()

    def arrived(self, shard, subs=EVERY, pass_on=None):
        for sub in subs:
            self.piece(0, shard, sub, self.partner).wait_recv()
            if pass_on is not None:
                self.piece(pass_on, shard, sub, self.partner).start()

    def launch(self):
        self.send(1, self.me, self.ahead)
        self.send(0, self.me, self.partner)

    def turn_back(self):
        self.sent(1, self.me, self.ahead, range(SUBS - 1))
        self.send(2, self.me, self.behind)

    def pass_ahead(self):
        self.sent(2, self.me, self.behind, range(SUBS - 1))
        self.send(4, self.first, self.ahead)

    def events(self):
        return (
            lambda: None,
            lambda: (self.turn_back(), self.arrived(self.partner)),
            lambda: self.arrived(self.first, pass_on=3),
            lambda: self.arrived(self.first_other),
            lambda: (self.pass_ahead(), self.arrived(self.second, pass_on=5)),
            lambda: self.arrived(self.second_other),
            lambda: (self.arrived(self.third, self.EARLY, 6), self.arrived(self.third_other, self.EARLY)),
            lambda: (self.arrived(self.third, self.LATE, 6), self.arrived(self.third_other, self.LATE)),
        )

    def places(self, step):
        half = self.full.shape[1] // 2
        pair = step // 2
        odd = step % 2
        side = self.turn * (1 - 2 * odd)
        hop = (3 * pair + (pair // 2) * (2 * pair - 5)) % N_CHIPS
        shard = device_at((self.chip + side * hop + 2 * N_CHIPS) % N_CHIPS, (self.core + odd) % 2)
        last = step // (2 * N_CHIPS - 2)
        upper = (1 - last) * shard + last * self.third
        lower = (1 - last) * shard + last * self.third_other
        return (upper, last * odd * half), (lower, (1 - last) * half + last * odd * half)

    def finish(self):
        self.sent(0, self.me, self.partner)
        self.sent(1, self.me, self.ahead, (SUBS - 1,))
        self.sent(2, self.me, self.behind, (SUBS - 1,))
        self.sent(3, self.first, self.partner)
        self.sent(4, self.first, self.ahead)
        self.sent(5, self.second, self.partner)
        self.sent(6, self.third, self.partner)


def run_at(step, actions):
    for idx, action in enumerate(actions):
        @pl.when(step == idx)
        def _():
            action()


def gather_scratch(tp_size, rows, width):
    return [
        pltpu.VMEM((tp_size, rows, width), BF16),
        pltpu.SemaphoreType.DMA((7, SUBS)),
        pltpu.SemaphoreType.DMA((tp_size, SUBS)),
    ]


def half_rows(ref, place, half):
    return ref[place[0], pl.ds(pl.multiple_of(place[1], half), half)]


def both_halves(ref, places, half):
    return jnp.concatenate([half_rows(ref, place, half) for place in places], axis=0)


def table_rows(ref, places, half, rows):
    parts = [ref[pl.ds(pl.multiple_of(shard * rows + row, half), half)] for shard, row in places]
    return jnp.concatenate(parts, axis=0)


class RowWriter:
    def __init__(self, stages, outs, sems, rows):
        self.stages, self.outs, self.sems, self.rows = stages, outs, sems, rows

    def copies(self, slot, places):
        half = self.rows // 2
        items = []
        for idx in range(len(self.outs)):
            for part, (shard, row) in enumerate(places):
                start = pl.multiple_of(shard * self.rows + row, half)
                src = self.stages[idx].at[slot, pl.ds(part * half, half)]
                items.append(pltpu.make_async_copy(src, self.outs[idx].at[pl.ds(start, half)], self.sems.at[idx, slot, part]))
        return items

    def reuse(self, step):
        @pl.when(step >= 2)
        def _():
            for item in self.copies(step % 2, ((0, 0), (0, 0))):
                item.wait()

    def start(self, step, places):
        for item in self.copies(step % 2, places):
            item.start()

    def finish(self):
        for slot in range(2):
            for item in self.copies(slot, ((0, 0), (0, 0))):
                item.wait()


def project_kernel(layer, first, x_ref, gain_ref, w_qkv_hbm, w_gate_hbm, w_up_hbm, cos_hbm, sin_hbm, *rest):
    n_out = 4 if first else 3
    outs, rest = rest[:n_out], rest[n_out:]
    if first:
        u_ref, *rest = rest
    stages, rest = rest[:n_out], rest[n_out:]
    cos_ref, sin_ref, weights, full, send_sems, recv_sems, w_sems, out_sems = rest
    rows = full.shape[1]
    half = rows // 2
    gather = Gather(full, send_sems, recv_sems)
    loads, spans, start = [], [], 0
    for idx, src in enumerate((w_qkv_hbm, w_gate_hbm, w_up_hbm)):
        spans.append(slice(start, start + src.shape[2]))
        start += src.shape[2]
        loads.append(pltpu.make_async_copy(src.at[layer], weights.at[:, spans[-1]], w_sems.at[idx]))
    loads += [pltpu.make_async_copy(cos_hbm, cos_ref, w_sems.at[3]), pltpu.make_async_copy(sin_hbm, sin_ref, w_sems.at[4])]
    writer = RowWriter(stages, outs, out_sems, rows)
    if first:
        def norm(idx, carry):
            span = pl.ds(pl.multiple_of(idx * ROWS_AT_ONCE, ROWS_AT_ONCE), ROWS_AT_ONCE)
            normed = rms_scale(x_ref[span].astype(F32), gain_ref[layer:layer + 1]).astype(BF16)
            full[gather.me, span] = normed
            u_ref[span] = normed
            return carry

        lax.fori_loop(0, rows // ROWS_AT_ONCE, norm, 0)
        meet(gather.peers())
    else:
        own = pltpu.make_async_copy(x_ref, full.at[gather.me], w_sems.at[5])
        own.start()
        meet(gather.peers())
        own.wait()
    gather.launch()
    for load in loads:
        load.start()
    for load in loads:
        load.wait()

    def step_body(step, carry):
        run_at(step, gather.events())
        places = gather.places(step)
        slot = step % 2
        writer.reuse(step)
        cos_tab, sin_tab = table_rows(cos_ref, places, half, rows), table_rows(sin_ref, places, half, rows)
        product = dot(both_halves(full, places, half), weights[...]).astype(BF16)
        qkv, gate, up = (product[:, span] for span in spans)
        for head in range(qkv.shape[1] // HEAD_DIM):
            cols = slice(head * HEAD_DIM, (head + 1) * HEAD_DIM)
            part = qkv[:, cols]
            if head % 3 != 2:
                part = rotate(part.astype(F32), cos_tab, sin_tab).astype(BF16)
            stages[0][slot, :, cols] = part
        stages[1][slot] = gate
        stages[2][slot] = up
        if first:
            stages[3][slot] = (jax.nn.silu(gate.astype(F32)) * up.astype(F32)).astype(BF16)
        writer.start(step, places)
        return carry

    lax.fori_loop(0, 2 * N_CHIPS, step_body, 0)
    gather.finish()
    writer.finish()


def project(source, norm_gain, w_qkv, w_gate, w_up, tables, layer, tp_size, first):
    rows, width = source.shape
    seq_len = rows * tp_size
    qkv_cols, ff_cols = w_qkv.shape[2], w_gate.shape[2]
    out_cols = [qkv_cols, ff_cols, ff_cols] + ([ff_cols] if first else [])
    total = qkv_cols + 2 * ff_cols
    outs = [jax.ShapeDtypeStruct((seq_len, cols), BF16) for cols in out_cols]
    out_specs = [ANY] * len(outs)
    if first:
        outs.append(jax.ShapeDtypeStruct((rows, width), BF16))
        out_specs.append(VMEM)
    scratch = [pltpu.VMEM((2, rows, cols), BF16) for cols in out_cols]
    scratch += [pltpu.VMEM(table.shape, F32) for table in tables]
    scratch += [pltpu.VMEM((width, total), BF16)]
    scratch += gather_scratch(tp_size, rows, width)
    scratch += [pltpu.SemaphoreType.DMA((6,)), pltpu.SemaphoreType.DMA((len(out_cols), 2, 2))]
    return pl.pallas_call(
        functools.partial(project_kernel, layer, first),
        out_shape=outs,
        in_specs=[VMEM if first else ANY, VMEM] + [ANY] * 5,
        out_specs=out_specs,
        scratch_shapes=scratch,
        compiler_params=params(collective_id=1 + layer),
        cost_estimate=cost(2 * seq_len * width * total, 2 * (width * total + seq_len * total)),
        name=f'project_{layer}',
    )(source, norm_gain, w_qkv, w_gate, w_up, *tables)


def scatter_blocks(blocks_each, peers, load_block, product, beside, tmp, acc, ring, pair_send, pair_recv, ring_send, ring_recv):
    me, chip, core = ring_place()
    partner = device_at(chip, 1 - core)
    right, left = device_at(chip + 1, core), device_at(chip - 1, core)
    per_step = 2 * blocks_each
    n_blocks = N_CHIPS * per_step
    slots = tmp.shape[0]
    meet(peers or (partner, right, left))

    def place(block):
        step = block // per_step
        way = block % 2
        dest = (chip + (1 + step) * (2 * way - 1) + 2 * N_CHIPS) % N_CHIPS
        cols = way * blocks_each + (block % per_step) // 2
        return step, way, dest, cols

    def to_partner(block):
        return remote_copy(tmp.at[block % slots, 1 - core], acc.at[block], pair_send.at[block % slots], pair_recv.at[block], partner)

    def to_next(block):
        way = block % 2
        peer = device_at(chip + 1 - 2 * way, core)
        return remote_copy(acc.at[block], ring.at[block], ring_send.at[block], ring_recv.at[block], peer)

    def body(block, carry):
        @pl.when(block < n_blocks)
        def _():
            step, way, dest, cols = place(block)
            load_block(block)

            @pl.when(block >= slots)
            def _():
                to_partner(block - slots).wait_send()

            product(dest, cols, tmp.at[block % slots])
            to_partner(block).start()
            beside(block)

        @pl.when(block >= 1)
        def _():
            last = block - 1
            to_partner(last).wait_recv()

            @pl.when(last < per_step)
            def _():
                acc[last] = acc[last] + tmp[last % slots, core]

            @pl.when(last >= per_step)
            def _():
                to_next(last - per_step).wait_recv()
                acc[last] = (acc[last] + tmp[last % slots, core]) + ring[last - per_step]

            @pl.when(last < n_blocks - per_step)
            def _():
                to_next(last).start()

        return carry

    lax.fori_loop(0, n_blocks + 1, body, 0)
    for block in range(n_blocks - slots, n_blocks):
        to_partner(block).wait_send()
    for block in range(n_blocks - per_step):
        to_next(block).wait_send()
    return lambda cols: acc.at[n_blocks - per_step + 2 * (cols % blocks_each) + cols // blocks_each]


def scatter_scratch(blocks_each, rows, width):
    per_step = 2 * blocks_each
    n_blocks = N_CHIPS * per_step
    cols = width // per_step
    return [
        pltpu.VMEM((3, 2, rows, cols), F32),
        pltpu.VMEM((n_blocks, rows, cols), F32),
        pltpu.VMEM((n_blocks - per_step, rows, cols), F32),
        pltpu.SemaphoreType.DMA((3,)),
        pltpu.SemaphoreType.DMA((n_blocks,)),
        pltpu.SemaphoreType.DMA((n_blocks - per_step,)),
        pltpu.SemaphoreType.DMA((n_blocks - per_step,)),
    ]


BLOCKS_EACH = 2


def row_loads(pairs, sems, rows, chip):
    def load(order, hop):
        span = pl.ds(pl.multiple_of(((chip + hop) % N_CHIPS) * rows, rows), rows)
        return [pltpu.make_async_copy(src.at[span], dst.at[span], sems.at[idx, order]) for idx, (src, dst) in enumerate(pairs)]

    return [load(order, hop) for order, hop in enumerate((3, 1, 2, 0))]


def forward_kernel(layer, next_gain, o_hbm, m_hbm, w_out_hbm, w_down_hbm, x_ref, gain_ref, y_ref, u_ref, o_all, m_all, w_out, w_down, row_sems, w_sems, *scatter):
    me, chip, core = ring_place()
    per_step = 2 * BLOCKS_EACH
    rows = x_ref.shape[0]
    width = x_ref.shape[1]
    block_cols = width // per_step
    loads = row_loads(((o_hbm, o_all), (m_hbm, m_all)), row_sems, 2 * rows, chip)

    def w_load(cols):
        span = pl.ds(cols * block_cols, block_cols)
        return [
            pltpu.make_async_copy(src.at[layer, :, span], dst.at[cols], w_sems.at[idx, cols])
            for idx, (src, dst) in enumerate(((w_out_hbm, w_out), (w_down_hbm, w_down)))
        ]

    order = [way * BLOCKS_EACH + j for j in range(BLOCKS_EACH) for way in range(2)]
    for block, cols in enumerate(order):
        for item in w_load(cols):
            item.start()
        if block < 2:
            for item in loads[block]:
                item.start()
    for block in range(2, 4):
        for item in loads[block]:
            item.start()

    def load_block(block):
        for idx, cols in enumerate(order):
            @pl.when(block == idx)
            def _():
                for item in w_load(cols):
                    item.wait()

        for idx, at in enumerate((0, 1, per_step, 3 * per_step)):
            @pl.when(block == at)
            def _():
                for item in loads[idx]:
                    item.wait()

    def product(dest, cols, out):
        span = pl.ds(pl.multiple_of(dest * 2 * rows, 2 * rows), 2 * rows)
        total = dot(o_all[span], w_out[cols]) + dot(m_all[span], w_down[cols])
        out[0] = total[:rows]
        out[1] = total[rows:]

    result = scatter_blocks(BLOCKS_EACH, None, load_block, product, lambda block: None, *scatter)

    def finish(idx, carry):
        span = pl.ds(pl.multiple_of(idx * ROWS_AT_ONCE, ROWS_AT_ONCE), ROWS_AT_ONCE)
        summed = jnp.concatenate([result(cols)[span] for cols in range(per_step)], axis=1)
        y = (x_ref[span].astype(F32) + summed).astype(BF16)
        y_ref[span] = y
        u_ref[span] = rms_scale(y.astype(F32), gain_ref[next_gain:next_gain + 1]).astype(BF16)
        return carry

    lax.fori_loop(0, rows // ROWS_AT_ONCE, finish, 0)


def block_output(attn_out, hidden, w_out, w_down, x_loc, norm_gain, layer):
    rows, width = x_loc.shape
    seq_len = attn_out.shape[0]
    head_cols, ff_cols = w_out.shape[1], w_down.shape[1]
    per_step = 2 * BLOCKS_EACH
    cols = width // per_step
    shard = jax.ShapeDtypeStruct((rows, width), BF16)
    return pl.pallas_call(
        functools.partial(forward_kernel, layer, layer + 1),
        out_shape=[shard, shard],
        in_specs=[ANY] * 4 + [VMEM] * 2,
        out_specs=[VMEM] * 2,
        scratch_shapes=[
            pltpu.VMEM((seq_len, head_cols), BF16),
            pltpu.VMEM((seq_len, ff_cols), BF16),
            pltpu.VMEM((per_step, head_cols, cols), BF16),
            pltpu.VMEM((per_step, ff_cols, cols), BF16),
            pltpu.SemaphoreType.DMA((2, 4)),
            pltpu.SemaphoreType.DMA((2, per_step)),
        ] + scatter_scratch(BLOCKS_EACH, rows, width),
        compiler_params=params(collective_id=5 + layer),
        cost_estimate=cost(2 * seq_len * width * (head_cols + ff_cols), 4 * seq_len * (head_cols + ff_cols)),
        name=f'block_output_{layer}',
    )(attn_out, hidden, w_out, w_down, x_loc, norm_gain)


GRAD_ROWS = 4


def backward_kernel(layer, dqkv_hbm, dgate_hbm, dup_hbm, w_qkv_hbm, w_gate_hbm, w_up_hbm, u_hbm, x_ref, dy_ref, gain_ref, *rest):
    first_layer = layer == 0
    if first_layer:
        later_gains_ref, *rest = rest
    dx_ref, dgain_ref, *rest = rest
    grads, rest = rest[:3], rest[3:]
    acts, rest = rest[:3], rest[3:]
    weights, rest = rest[:3], rest[3:]
    u_all, stage, row_sems, w_sems, u_sem, stage_sems, *rest = rest
    if first_layer:
        gain_parts, gain_send, gain_recv, *rest = rest
    scatter = rest
    me, chip, core = ring_place()
    per_step = 2 * BLOCKS_EACH
    rows, width = x_ref.shape
    block_cols = width // per_step
    loads = row_loads(list(zip((dqkv_hbm, dgate_hbm, dup_hbm), acts)), row_sems, 2 * rows, chip)
    u_load = pltpu.make_async_copy(u_hbm, u_all, u_sem)

    def w_load(cols):
        span = pl.ds(cols * block_cols, block_cols)
        return [
            pltpu.make_async_copy(src.at[layer, span], dst.at[span], w_sems.at[idx, cols])
            for idx, (src, dst) in enumerate(zip((w_qkv_hbm, w_gate_hbm, w_up_hbm), weights))
        ]

    order = [way * BLOCKS_EACH + j for j in range(BLOCKS_EACH) for way in range(2)]
    for block, cols in enumerate(order):
        for item in w_load(cols):
            item.start()
        if block < 2:
            for item in loads[block]:
                item.start()
    for block in range(2, 4):
        for item in loads[block]:
            item.start()
    u_load.start()

    def load_block(block):
        for idx, cols in enumerate(order):
            @pl.when(block == idx)
            def _():
                for item in w_load(cols):
                    item.wait()

        for idx, at in enumerate((0, 1, per_step)):
            @pl.when(block == at)
            def _():
                for item in loads[idx]:
                    item.wait()

        @pl.when(block == per_step)
        def _():
            for item in loads[3]:
                item.wait()
            u_load.wait()

    def product(dest, cols, out):
        span = pl.ds(pl.multiple_of(dest * 2 * rows, 2 * rows), 2 * rows)
        w_span = pl.ds(pl.multiple_of(cols * block_cols, block_cols), block_cols)
        total = dot_nt(acts[0][span], weights[0][w_span]) + dot_nt(acts[1][span], weights[1][w_span]) + dot_nt(acts[2][span], weights[2][w_span])
        out[0] = total[:rows]
        out[1] = total[rows:]

    grad_rows = width // GRAD_ROWS

    def grad_out(which, part):
        slot = which % 2
        src = stage.at[slot, :, :grads[which].shape[1]]
        return pltpu.make_async_copy(src, grads[which].at[pl.ds(pl.multiple_of(part * grad_rows, grad_rows), grad_rows)], stage_sems.at[slot])

    def beside(block):
        task = block - per_step
        part = task // 3
        cols = pl.ds(pl.multiple_of(part * grad_rows, grad_rows), grad_rows)
        for turn, which in enumerate((2, 1, 0)):
            @pl.when((task >= 0) & (task % 3 == turn))
            def _():
                if which == 2:
                    @pl.when(part > 0)
                    def _():
                        grad_out(0, part - 1).wait()
                elif which == 0:
                    grad_out(2, part).wait()
                else:
                    @pl.when(part > 0)
                    def _():
                        grad_out(1, part - 1).wait()
                stage[which % 2, :, :grads[which].shape[1]] = dot_tn(u_all[:, cols], acts[which][...]).astype(BF16)
                grad_out(which, part).start()

    peers = [(me + 1 + idx) % (2 * N_CHIPS) for idx in range(2 * N_CHIPS - 1)] if first_layer else None
    result = scatter_blocks(BLOCKS_EACH, peers, load_block, product, beside, *scatter)
    gain_row = gain_ref[layer:layer + 1]
    dgain = gain_parts.at[me, layer:layer + 1] if first_layer else dgain_ref
    dgain[...] = jnp.zeros_like(dgain)

    def finish(idx, carry):
        span = pl.ds(pl.multiple_of(idx * ROWS_AT_ONCE, ROWS_AT_ONCE), ROWS_AT_ONCE)
        summed = jnp.concatenate([result(cols)[span] for cols in range(per_step)], axis=1)
        d_normed = summed.astype(BF16).astype(F32)
        x_f32 = x_ref[span].astype(F32)
        inv_rms = lax.rsqrt(jnp.mean(x_f32 * x_f32, axis=-1, keepdims=True) + NORM_EPS)
        scaled = d_normed * gain_row
        dgain[...] += jnp.sum(d_normed * (x_f32 * inv_rms), axis=0, keepdims=True)
        mix = jnp.mean(scaled * x_f32, axis=-1, keepdims=True) * (inv_rms * inv_rms * inv_rms)
        dx_ref[span] = (dy_ref[span].astype(F32) + (scaled * inv_rms - x_f32 * mix)).astype(BF16)
        return carry

    lax.fori_loop(0, rows // ROWS_AT_ONCE, finish, 0)
    if first_layer:
        gain_parts[me, 1:] = later_gains_ref[...]
        copies = [remote_copy(gain_parts.at[me], gain_parts.at[me], gain_send.at[idx], gain_recv.at[me], peer) for idx, peer in enumerate(peers)]
        for item in copies:
            item.start()
        for idx, peer in enumerate(peers):
            remote_copy(gain_parts.at[peer], gain_parts.at[peer], gain_send.at[idx], gain_recv.at[peer], peer).wait_recv()
        total = gain_parts[0]
        for idx in range(1, 2 * N_CHIPS):
            total = total + gain_parts[idx]
        dgain_ref[...] = total
        for item in copies:
            item.wait_send()
    grad_out(0, GRAD_ROWS - 1).wait()
    grad_out(1, GRAD_ROWS - 1).wait()


def block_input_backward(d_qkv, d_gate, d_up, w_qkv, w_gate, w_up, u_full, x_loc, dy_loc, norm_gain, later_gains, layer):
    rows, width = x_loc.shape
    seq_len = d_qkv.shape[0]
    n_layers = norm_gain.shape[0]
    all_cols = (w_qkv.shape[2], w_gate.shape[2], w_up.shape[2])
    per_step = 2 * BLOCKS_EACH
    first_layer = layer == 0
    out_shape = [jax.ShapeDtypeStruct((rows, width), BF16), jax.ShapeDtypeStruct((n_layers if first_layer else 1, width), F32)]
    out_shape += [jax.ShapeDtypeStruct((width, cols), BF16) for cols in all_cols]
    scratch = [pltpu.VMEM((seq_len, cols), BF16) for cols in all_cols]
    scratch += [pltpu.VMEM((width, cols), BF16) for cols in all_cols]
    scratch += [pltpu.VMEM((seq_len, width), BF16), pltpu.VMEM((2, width // GRAD_ROWS, max(all_cols)), BF16)]
    scratch += [pltpu.SemaphoreType.DMA((3, 4)), pltpu.SemaphoreType.DMA((3, per_step)), pltpu.SemaphoreType.DMA, pltpu.SemaphoreType.DMA((2,))]
    if first_layer:
        scratch += [pltpu.VMEM((2 * N_CHIPS, n_layers, width), F32), pltpu.SemaphoreType.DMA((2 * N_CHIPS - 1,)), pltpu.SemaphoreType.DMA((2 * N_CHIPS,))]
    flops = 2 * seq_len * width * sum(all_cols)
    return pl.pallas_call(
        functools.partial(backward_kernel, layer),
        out_shape=out_shape,
        in_specs=[ANY] * 7 + [VMEM] * (4 if first_layer else 3),
        out_specs=[VMEM] * 2 + [ANY] * 3,
        scratch_shapes=scratch + scatter_scratch(BLOCKS_EACH, rows, width),
        compiler_params=params(collective_id=7 + layer),
        cost_estimate=cost(2 * flops, 4 * seq_len * sum(all_cols)),
        name=f'block_input_backward_{layer}',
    )(d_qkv, d_gate, d_up, w_qkv, w_gate, w_up, u_full, x_loc, dy_loc, norm_gain, *((later_gains,) if first_layer else ()))


def stack_kernel(n_arrays, *refs):
    ins, outs = refs[:-n_arrays], refs[-n_arrays:]
    per_array = len(ins) // n_arrays
    for idx, out in enumerate(outs):
        for layer in range(per_array):
            out[layer] = ins[idx * per_array + layer][...]


def stack_layers(arrays, steps):
    flat = [item for layers in arrays for item in layers]
    n_layers = len(arrays[0])
    return pl.pallas_call(
        functools.partial(stack_kernel, len(arrays)),
        grid=(steps,),
        out_shape=[jax.ShapeDtypeStruct((n_layers,) + layers[0].shape, BF16) for layers in arrays],
        in_specs=[pl.BlockSpec((item.shape[0] // steps, item.shape[1]), lambda i: (i, 0)) for item in flat],
        out_specs=[pl.BlockSpec((n_layers, layers[0].shape[0] // steps, layers[0].shape[1]), lambda i: (0, i, 0)) for layers in arrays],
        compiler_params=params(semantics=('arbitrary',)),
        cost_estimate=cost(0, 4 * sum(item.size for item in flat)),
        name='stack_layers',
    )(*flat)


def causal_tile(size):
    return lax.broadcasted_iota(jnp.int32, (size, size), 0) >= lax.broadcasted_iota(jnp.int32, (size, size), 1)


def masked_scores(query, keys):
    size = query.shape[0]
    q_start = keys.shape[0] - size
    scores = dot_nt(query, keys)
    diagonal = jnp.where(causal_tile(size), scores[:, q_start:], -1e30)
    scores = diagonal if q_start == 0 else jnp.concatenate([scores[:, :q_start], diagonal], axis=1)
    return scores * (SCALE * LOG2E)


def head_cols(head, part, parts):
    return pl.ds(pl.multiple_of((head * parts + part) * HEAD_DIM, HEAD_DIM), HEAD_DIM)


def attend_rows(q_start, head, qkv_ref, o_ref, lse_ref):
    span, seen = slice(q_start, q_start + Q_ROWS), slice(0, q_start + Q_ROWS)
    scores = masked_scores(qkv_ref[span, head_cols(head, 0, 3)], qkv_ref[seen, head_cols(head, 1, 3)])
    row_max = jnp.max(scores, axis=-1, keepdims=True)
    prob = jnp.exp2(scores - row_max)
    norm = jnp.sum(prob, axis=-1, keepdims=True)
    prob = (prob * (1.0 / norm)).astype(BF16)
    o_ref[span, head_cols(head, 0, 1)] = dot(prob, qkv_ref[seen, head_cols(head, 2, 3)]).astype(BF16)
    lse_ref[span, head_cols(head, 0, 1)] = jnp.broadcast_to(row_max + jnp.log2(norm), (Q_ROWS, HEAD_DIM))


def attend_rows_backward(q_start, head, qkv_ref, lse_ref, do_ref, dq_ref, dk_acc, dv_acc):
    span, seen = slice(q_start, q_start + Q_ROWS), slice(0, q_start + Q_ROWS)
    query = qkv_ref[span, head_cols(head, 0, 3)]
    keys = qkv_ref[seen, head_cols(head, 1, 3)]
    d_out = do_ref[span, head_cols(head, 0, 1)]
    scores = masked_scores(query, keys)
    prob = jnp.exp2(scores - lse_ref[span, head_cols(head, 0, 1)][:, :1])
    d_prob = dot_nt(d_out, qkv_ref[seen, head_cols(head, 2, 3)]).astype(BF16).astype(F32)
    dv_acc[head, seen] += dot_tn(prob.astype(BF16), d_out)
    inner = jnp.sum(prob * d_prob, axis=-1, keepdims=True)
    d_scores = (prob * (d_prob - inner) * SCALE).astype(BF16)
    dq_ref[span, head_cols(head, 0, 3)] = dot(d_scores, keys).astype(BF16)
    dk_acc[head, seen] += dot_tn(d_scores, query)


def attention_kernel(qkv_ref, o_ref, lse_ref):
    for q_start in range(0, qkv_ref.shape[0], Q_ROWS):
        attend_rows(q_start, 0, qkv_ref, o_ref, lse_ref)


def attention(qkv):
    seq_len, cols = qkv.shape
    heads = cols // (3 * HEAD_DIM)
    work = heads * seq_len * seq_len
    return pl.pallas_call(
        attention_kernel,
        grid=(heads,),
        out_shape=[jax.ShapeDtypeStruct((seq_len, heads * HEAD_DIM), BF16), jax.ShapeDtypeStruct((seq_len, heads * HEAD_DIM), F32)],
        in_specs=[pl.BlockSpec((seq_len, 3 * HEAD_DIM), lambda h: (0, h))],
        out_specs=[pl.BlockSpec((seq_len, HEAD_DIM), lambda h: (0, h))] * 2,
        compiler_params=params(semantics=('arbitrary',)),
        cost_estimate=cost(8 * work * HEAD_DIM // 2, 2 * seq_len * cols, work // 2),
        name='attention',
    )(qkv)


def middle_kernel(layer, with_forward, dy_hbm, u_hbm, w_out_hbm, w_down_hbm, gate_hbm, up_hbm, cos_hbm, sin_hbm, qkv_hbm, *rest):
    if not with_forward:
        (o_hbm, lse_hbm), rest = rest[:2], rest[2:]
    (dgate_hbm, dup_hbm, dqkv_hbm, u_full_hbm, g_out_hbm, g_down_hbm), rest = rest[:6], rest[6:]
    (dgate_stage, dup_stage, gate_in, up_in, weights, qkv, o_all, lse, hidden, d_attn, dqkv, dk_acc, dv_acc, grad_stage, cos_ref, sin_ref), rest = rest[:16], rest[16:]
    dy_full, dy_send, dy_recv, u_full, u_send, u_recv, load_sems, out_sems, in_sems, u_sems, grad_sems = rest
    rows = dy_full.shape[1]
    half = rows // 2
    seq_len = qkv.shape[0]
    n_heads = o_all.shape[1] // HEAD_DIM
    o_cols = o_all.shape[1]
    gather = Gather(dy_full, dy_send, dy_recv)
    u_gather = Gather(u_full, u_send, u_recv)
    me = gather.me
    own_dy = pltpu.make_async_copy(dy_hbm, dy_full.at[me], load_sems.at[0])
    own_u = pltpu.make_async_copy(u_hbm, u_full.at[me], load_sems.at[1])
    w_loads = [
        pltpu.make_async_copy(w_out_hbm.at[layer], weights.at[:o_cols], load_sems.at[2]),
        pltpu.make_async_copy(w_down_hbm.at[layer], weights.at[o_cols:], load_sems.at[3]),
    ]
    loads = [
        pltpu.make_async_copy(src, dst, load_sems.at[4 + idx])
        for idx, (src, dst) in enumerate([(qkv_hbm, qkv), (cos_hbm, cos_ref), (sin_hbm, sin_ref)] + ([] if with_forward else [(o_hbm, o_all), (lse_hbm, lse)]))
    ]
    writer = RowWriter((dgate_stage, dup_stage), (dgate_hbm, dup_hbm), out_sems, rows)
    own_dy.start()
    meet(gather.peers())
    own_dy.wait()
    gather.launch()
    for item in w_loads + loads + [own_u]:
        item.start()
    dk_acc[...] = jnp.zeros_like(dk_acc)
    dv_acc[...] = jnp.zeros_like(dv_acc)
    for item in w_loads + loads + [own_u]:
        item.wait()

    def both_heads(function, *args):
        def body(head, carry):
            function(*args[:1], head, *args[1:])
            return carry

        lax.fori_loop(0, n_heads, body, 0)

    def dy_step(step, carry):
        run_at(step, gather.events())

        @pl.when(step == 2 * N_CHIPS - 2)
        def _():
            u_gather.launch()

        places = gather.places(step)
        slot = step % 2
        fetch = []
        for idx, (src, dst) in enumerate(((gate_hbm, gate_in), (up_hbm, up_in))):
            for part, (shard, row) in enumerate(places):
                here = pl.ds(pl.multiple_of(shard * rows + row, half), half)
                fetch.append(pltpu.make_async_copy(src.at[here], dst.at[pl.ds(part * half, half)], in_sems.at[idx, part]))
        for item in fetch:
            item.start()
        writer.reuse(step)
        product = dot_nt(both_halves(dy_full, places, half), weights[...]).astype(BF16)
        d_hidden = product[:, o_cols:].astype(F32)
        for item in fetch:
            item.wait()
        gate, up = gate_in[...].astype(F32), up_in[...].astype(F32)
        sig = jax.nn.sigmoid(gate)
        act = gate * sig
        hidden_rows = (act * up).astype(BF16)
        for part, (shard, row) in enumerate(places):
            here = pl.ds(pl.multiple_of(shard * rows + row, half), half)
            d_attn[here] = product[part * half:(part + 1) * half, :o_cols]
            hidden[here] = hidden_rows[part * half:(part + 1) * half]
        dgate_stage[slot] = (d_hidden * up * (sig + act * (1.0 - sig))).astype(BF16)
        dup_stage[slot] = (d_hidden * act).astype(BF16)
        writer.start(step, places)
        if with_forward:
            run_at(step, [functools.partial(both_heads, attend_rows, q_start, qkv, o_all, lse) for q_start in range(0, seq_len, Q_ROWS)])
        return carry

    lax.fori_loop(0, 2 * N_CHIPS, dy_step, 0)

    def grad_copies(step):
        slot = step % 2
        cols = pl.ds(pl.multiple_of(step * grad_cols, grad_cols), grad_cols)
        return (
            pltpu.make_async_copy(grad_stage.at[slot, :o_cols], g_out_hbm.at[:, cols], grad_sems.at[slot, 0]),
            pltpu.make_async_copy(grad_stage.at[slot, o_cols:], g_down_hbm.at[:, cols], grad_sems.at[slot, 1]),
        )

    grad_cols = dy_full.shape[2] // (2 * N_CHIPS)
    u_events = (
        lambda: u_gather.turn_back(),
        lambda: u_gather.arrived(u_gather.partner),
        lambda: u_gather.arrived(u_gather.first, pass_on=3),
        lambda: u_gather.arrived(u_gather.first_other),
        lambda: (u_gather.pass_ahead(), u_gather.arrived(u_gather.second, pass_on=5)),
        lambda: u_gather.arrived(u_gather.second_other),
        lambda: u_gather.arrived(u_gather.third, u_gather.EARLY, 6),
        lambda: None,
    )

    def u_step(step, carry):
        run_at(step, u_events)

        @pl.when(step >= 2)
        def _():
            for item in grad_copies(step - 2):
                item.wait()

        cols = pl.ds(pl.multiple_of(step * grad_cols, grad_cols), grad_cols)
        dy_cols = dy_full[:, :, cols].reshape(seq_len, grad_cols)
        slot = step % 2
        grad_stage[slot, :o_cols] = dot_tn(o_all[...], dy_cols).astype(BF16)
        grad_stage[slot, o_cols:] = dot_tn(hidden[...], dy_cols).astype(BF16)
        for item in grad_copies(step):
            item.start()
        run_at(step, [functools.partial(both_heads, attend_rows_backward, q_start, qkv, lse, d_attn, dqkv, dk_acc, dv_acc) for q_start in range(0, seq_len, Q_ROWS)])
        return carry

    lax.fori_loop(0, 2 * N_CHIPS, u_step, 0)
    u_gather.arrived(u_gather.third, u_gather.LATE, 6)
    u_gather.arrived(u_gather.third_other)
    keep_u = pltpu.make_async_copy(u_full, u_full_hbm, u_sems.at[0])
    keep_u.start()

    def finish(idx, carry):
        span = pl.ds(pl.multiple_of(idx * Q_ROWS, Q_ROWS), Q_ROWS)
        cos_tab, sin_tab = cos_ref[span], -sin_ref[span]
        for head in range(n_heads):
            for part, value in enumerate((dqkv[span, head_cols(head, 0, 3)], dk_acc[head, span].astype(BF16))):
                dqkv[span, head_cols(head, part, 3)] = rotate(value.astype(F32), cos_tab, sin_tab).astype(BF16)
            dqkv[span, head_cols(head, 2, 3)] = dv_acc[head, span].astype(BF16)
        return carry

    lax.fori_loop(0, seq_len // Q_ROWS, finish, 0)
    keep_dqkv = pltpu.make_async_copy(dqkv, dqkv_hbm, u_sems.at[1])
    keep_dqkv.start()
    for step in (2 * N_CHIPS - 2, 2 * N_CHIPS - 1):
        for item in grad_copies(step):
            item.wait()
    gather.finish()
    u_gather.finish()
    writer.finish()
    keep_u.wait()
    keep_dqkv.wait()


def middle(dy_loc, u_loc, w_out, w_down, gate_act, up_act, tables, qkv, attended, layer, tp_size):
    rows, width = dy_loc.shape
    seq_len = rows * tp_size
    o_cols, ff_cols, qkv_cols = w_out.shape[1], w_down.shape[1], qkv.shape[1]
    n_heads = o_cols // HEAD_DIM
    total = o_cols + ff_cols
    outs = [(seq_len, ff_cols), (seq_len, ff_cols), (seq_len, qkv_cols), (tp_size, rows, width), (o_cols, width), (ff_cols, width)]
    scratch = [pltpu.VMEM((2, rows, ff_cols), BF16)] * 2
    scratch += [pltpu.VMEM((rows, ff_cols), BF16)] * 2
    scratch += [
        pltpu.VMEM((total, width), BF16),
        pltpu.VMEM((seq_len, qkv_cols), BF16),
        pltpu.VMEM((seq_len, o_cols), BF16),
        pltpu.VMEM((seq_len, o_cols), F32),
        pltpu.VMEM((seq_len, ff_cols), BF16),
        pltpu.VMEM((seq_len, o_cols), BF16),
        pltpu.VMEM((seq_len, qkv_cols), BF16),
        pltpu.VMEM((n_heads, seq_len, HEAD_DIM), F32),
        pltpu.VMEM((n_heads, seq_len, HEAD_DIM), F32),
        pltpu.VMEM((2, total, width // (2 * N_CHIPS)), BF16),
    ]
    scratch += [pltpu.VMEM(table.shape, F32) for table in tables]
    scratch += gather_scratch(tp_size, rows, width) + gather_scratch(tp_size, rows, width)
    scratch += [
        pltpu.SemaphoreType.DMA((9,)),
        pltpu.SemaphoreType.DMA((2, 2, 2)),
        pltpu.SemaphoreType.DMA((2, 2)),
        pltpu.SemaphoreType.DMA((2,)),
        pltpu.SemaphoreType.DMA((2, 2)),
    ]
    work = n_heads * seq_len * seq_len * HEAD_DIM
    return pl.pallas_call(
        functools.partial(middle_kernel, layer, not attended),
        out_shape=[jax.ShapeDtypeStruct(shape, BF16) for shape in outs],
        in_specs=[ANY] * (9 + len(attended)),
        out_specs=[ANY] * len(outs),
        scratch_shapes=scratch,
        compiler_params=params(collective_id=3 + layer),
        cost_estimate=cost(4 * seq_len * width * total + 10 * work, 2 * (width * total + 3 * seq_len * total)),
        name=f'middle_{layer}',
    )(dy_loc, u_loc, w_out, w_down, gate_act, up_act, *tables, qkv, *attended)


def solution(mesh):
    tp_size = mesh.shape['tp']
    assert tp_size == 2 * N_CHIPS
    row_spec = P(('dp', 'tp'), None)
    col_spec = P(None, None, 'tp')
    inner_spec = P(None, 'tp', None)

    def device_program(x_loc, dy_loc, norm_gain, w_qkv, w_out, w_gate, w_up, w_down):
        n_layers = w_qkv.shape[0]
        seq_len = x_loc.shape[0] * tp_size
        tables = tuple(jnp.asarray(table) for table in rope_tables(seq_len))
        x_cur, source = x_loc, x_loc
        saved = []
        for layer in range(n_layers):
            first, last = layer == 0, layer == n_layers - 1
            qkv, gate_act, up_act, *more = project(source, norm_gain, w_qkv, w_gate, w_up, tables, layer, tp_size, first)
            u_loc = more[1] if first else source
            if last:
                saved.append((x_cur, u_loc, qkv, gate_act, up_act, ()))
            else:
                attended = attention(qkv)
                saved.append((x_cur, u_loc, qkv, gate_act, up_act, tuple(attended)))
                x_cur, source = block_output(attended[0], more[0], w_out, w_down, x_cur, norm_gain, layer)
        grad_cur = dy_loc
        grads, gains = [None] * n_layers, ()
        for layer in reversed(range(n_layers)):
            x_cur, u_loc, qkv, gate_act, up_act, attended = saved[layer]
            d_gate, d_up, d_qkv, u_full, g_out, g_down = middle(grad_cur, u_loc, w_out, w_down, gate_act, up_act, tables, qkv, attended, layer, tp_size)
            u_full = u_full.reshape(seq_len, u_full.shape[2])
            later_gains = jnp.concatenate(gains, axis=0) if gains else None
            grad_cur, gain_grad, g_qkv, g_gate, g_up = block_input_backward(
                d_qkv, d_gate, d_up, w_qkv, w_gate, w_up, u_full, x_cur, grad_cur, norm_gain, later_gains, layer
            )
            grads[layer] = (g_qkv, g_gate, g_up, g_out, g_down)
            gains = (gain_grad,) + gains
        g_qkv, g_gate, g_up, g_out, g_down = stack_layers(list(zip(*grads)), 8)
        return (grad_cur, gains[0], g_qkv, g_out, g_gate, g_up, g_down)

    return jax.shard_map(
        device_program,
        mesh=mesh,
        in_specs=(row_spec, row_spec, P(None, None), col_spec, inner_spec, col_spec, col_spec, inner_spec),
        out_specs=(row_spec, P('dp', None), P('dp', None, 'tp'), P('dp', 'tp', None), P('dp', None, 'tp'), P('dp', None, 'tp'), P('dp', 'tp', None)),
        check_vma=False,
    )
```

time: 672 us -> 567 us (0.84)
  Pallas kernels: 619 us -> 556 us
  blocking collectives: 20.8 us -> 0 us
  between operations: 14.6 us -> 1.16 us
    pallas_call x12 -> x7, Pallas kernels: 510 us -> 465 us  [the longest x2 174 us: middle(): pl.pallas_call(functools.partial(middle_kernel, layer, not attended), out...]
    psum x1 -> x0, blocking collectives: 20.8 us -> none  [device_program(): grad_gain = lax.psum(jnp.concatenate(gains, axis=0), 'tp')]
    pallas_call x2 -> x1, Pallas kernels: 28.3 us -> 14.1 us  [attention(): pl.pallas_call(attention_kernel, grid=(heads,), out_shape=[jax.ShapeDtype...]
  transfers between devices with their start and end apart: 2 -> 0, of which waited for: 0 -> 0; matrix products, arithmetic and copies ran while one was open for 0% -> 0% of each run, Pallas kernels for 52% -> 0%
where the time goes in v2:
time: 567 us; the launch traced here: 559 us
  Pallas kernels  556 us (98%)
    pallas_call x2, Pallas kernels, middle(): pl.pallas_call(functools.partial(middle_kernel, layer, not attended), out...  174 us
    pallas_call x2, Pallas kernels, block_input_backward(): pl.pallas_call(functools.partial(backward_kernel, layer), out_shape=out_s...  169 us
    pallas_call x2, Pallas kernels, project(): pl.pallas_call(functools.partial(project_kernel, layer, first), out_shape...  99 us
    pallas_call x1, Pallas kernels, block_output(): pl.pallas_call(functools.partial(forward_kernel, layer, layer + 1), out_s...  77.7 us
    pallas_call x1, Pallas kernels, stack_layers(): pl.pallas_call(functools.partial(stack_kernel, len(arrays)), grid=(steps,...  22.6 us
    pallas_call x1, Pallas kernels, attention(): pl.pallas_call(attention_kernel, grid=(heads,), out_shape=[jax.ShapeDtype...  14.1 us

profile of v2, /device:TPU:81, one launch (start us, length us, event | category | flops | bytes accessed | tf_op | source)
XLA Modules:
  0.0 559.2 jit_solution(14991195003829986723)
XLA Ops:
  0.6 51.4 %project_0.1 = (bf16[2048,768]{1,0:T(8,128)(2,1)}, bf16[2048,1024]{1,0:T(8,128)(2,1)}, bf16[2048,1024]{1,0:T(8,128)(2,1)}, bf16[2048,1024]{1,0:T(8,128)(2,1)}, bf16[256,2048]{1,0:T(8,128)(2,1)}) custom-call(bf16[256,2048]{1,0:T(8,128)(2,1)} %x_ref.5, f32[2,2048]{1,0:T(2,128)} %gain_ref.9, bf16[2,2048,768]{2,1,0:T(8,128)(2,1)} %w_qkv_hbm.7, ...), custom_call_target="tpu_custom_call" | custom-call | flops 23622320128 | bytes 23068672 | tf_op jit(solution)/shard_map/project_0/pallas_call | solution.py:316
  52.0 14.1 %attention.1 = (bf16[2048,256]{1,0:T(8,128)(2,1)}, f32[2048,256]{1,0:T(8,128)}) custom-call(bf16[2048,768]{1,0:T(8,128)(2,1)} %get-tuple-element.46.qkv_ref.qkv_hbm), custom_call_target="tpu_custom_call" | custom-call | flops 4294967296 | bytes 3145728 | tf_op jit(solution)/shard_map/attention/pallas_call | solution.py:737
  66.2 77.7 %block_output_0.1 = (bf16[256,2048]{1,0:T(8,128)(2,1)}, bf16[256,2048]{1,0:T(8,128)(2,1)}) custom-call(bf16[2048,256]{1,0:T(8,128)(2,1)} %get-tuple-element.47.o_hbm.rest_0_, bf16[2048,1024]{1,0:T(8,128)(2,1)} %get-tuple-element.48.m_hbm, bf16[2,256,2048]{2,1,0:T(8,128)(2,1)} %w_out_hbm.5, bf16[2,1024,2048]{2,1,0:T(8,128)(2,1)} %w_down_hbm.5, ...), custom_call_target="tpu_custom_call" | custom-call | flops 10737418240 | bytes 10485760 | tf_op jit(solution)/shard_map/block_output_0/pallas_call | solution.py:485
  143.9 47.6 %project_1.1 = (bf16[2048,768]{1,0:T(8,128)(2,1)}, bf16[2048,1024]{1,0:T(8,128)(2,1)}, bf16[2048,1024]{1,0:T(8,128)(2,1)}) custom-call(bf16[256,2048]{1,0:T(8,128)(2,1)} %get-tuple-element.49.x_ref.u_hbm, f32[2,2048]{1,0:T(2,128)} %gain_ref.9, bf16[2,2048,768]{2,1,0:T(8,128)(2,1)} %w_qkv_hbm.7, bf16[2,2048,1024]{2,1,0:T(8,128)(2,1)} %w_gate_hbm.7, ...), custom_call_target="tpu_custom_call" | custom-call | flops 23622320128 | bytes 23068672 | tf_op jit(solution)/shard_map/project_1/pallas_call | solution.py:316
  191.5 87.1 %middle_1.1 = (bf16[2048,1024]{1,0:T(8,128)(2,1)}, bf16[2048,1024]{1,0:T(8,128)(2,1)}, bf16[2048,768]{1,0:T(8,128)(2,1)}, bf16[8,256,2048]{2,1,0:T(8,128)(2,1)},...) custom-call(bf16[256,2048]{1,0:T(8,128)(2,1)} %dy_ref.1, bf16[256,2048]{1,0:T(8,128)(2,1)} %get-tuple-element.49.x_ref.u_hbm, ...), custom_call_target="tpu_custom_call" | custom-call | flops 32212254720 | bytes 20971520 | tf_op jit(solution)/shard_map/middle_1/pallas_call | solution.py:927
  278.6 82.1 %block_input_backward_1.1 = (bf16[256,2048]{1,0:T(8,128)(2,1)}, f32[1,2048]{1,0:T(1,128)}, bf16[2048,768]{1,0:T(8,128)(2,1)}, bf16[2048,1024]{1,0:T(8,128)(2,1)}, bf16[2048,1024]{1,0:T(8,128)(2,1)}) custom-call(bf16[2048,768]{1,0:T(8,128)(2,1)} %get-tuple-element.53.dqkv_hbm, bf16[2048,1024]{1,0:T(8,128)(2,1)} %get-tuple-element.54.dgate_hbm, ...), custom_call_target="tpu_custom_call" | custom-call | flops 47244640256 | bytes 23068672 | tf_op jit(solution)/shard_map/block_input_backward_1/pallas_call | solution.py:650
  360.7 86.4 %middle_0.1 = (bf16[2048,1024]{1,0:T(8,128)(2,1)}, bf16[2048,1024]{1,0:T(8,128)(2,1)}, bf16[2048,768]{1,0:T(8,128)(2,1)}, bf16[8,256,2048]{2,1,0:T(8,128)(2,1)},...) custom-call(bf16[256,2048]{1,0:T(8,128)(2,1)} %get-tuple-element.58.dy_hbm.dy_ref, ...), custom_call_target="tpu_custom_call" | custom-call | flops 32212254720 | bytes 20971520 | tf_op jit(solution)/shard_map/middle_0/pallas_call | solution.py:927
  447.1 87.4 %block_input_backward_0.1 = (bf16[256,2048]{1,0:T(8,128)(2,1)}, f32[2,2048]{1,0:T(2,128)}, bf16[2048,768]{1,0:T(8,128)(2,1)}, bf16[2048,1024]{1,0:T(8,128)(2,1)}, bf16[2048,1024]{1,0:T(8,128)(2,1)}) custom-call(bf16[2048,768]{1,0:T(8,128)(2,1)} %get-tuple-element.63.dqkv_hbm, bf16[2048,1024]{1,0:T(8,128)(2,1)} %get-tuple-element.64.dgate_hbm, ...), custom_call_target="tpu_custom_call" | custom-call | flops 47244640256 | bytes 23068672 | tf_op jit(solution)/shard_map/block_input_backward_0/pallas_call | solution.py:650
  534.5 0.0 copy-start
  534.5 0.0 copy-start.1
  534.5 22.6 %stack_layers.1 = (bf16[2,2048,768]{2,1,0:T(8,128)(2,1)}, bf16[2,2048,1024]{2,1,0:T(8,128)(2,1)}, bf16[2,2048,1024]{2,1,0:T(8,128)(2,1)}, bf16[2,256,2048]{2,1,0:T(8,128)(2,1)}, bf16[2,1024,2048]{2,1,0:T(8,128)(2,1)}) custom-call(bf16[2048,768]{1,0:T(8,128)(2,1)} %get-tuple-element.70.refs_0_, bf16[2048,768]{1,0:T(8,128)(2,1)} %get-tuple-element.71.refs_1_, ...), custom_call_target="tpu_custom_call" | custom-call | bytes 67108864 | tf_op jit(solution)/shard_map/stack_layers/pallas_call | solution.py:673
  557.1 0.0 copy-done
  557.1 1.0 copy.19
  558.1 0.0 copy-done.1
  558.1 0.6 copy.20
Async XLA Ops:
  534.5 22.6 %copy-start = (bf16[256,2048]{1,0:T(8,128)(2,1)S(1)}, bf16[256,2048]{1,0:T(8,128)(2,1)}, u32[]{:S(2)}) copy-start(bf16[256,2048]{1,0:T(8,128)(2,1)} %get-tuple-element.92) | copy-start | bytes 3145732
  534.5 23.6 %copy-start.1 = (f32[2,2048]{1,0:T(2,128)S(1)}, f32[2,2048]{1,0:T(2,128)}, u32[]{:S(2)}) copy-start(f32[2,2048]{1,0:T(2,128)} %get-tuple-element.93) | copy-start | bytes 49156

commit v3 on v2

v3 whole, which is shorter than its diff:
```python
import functools

import jax
import jax.numpy as jnp
import numpy as np
from jax import lax
from jax.experimental import pallas as pl
from jax.experimental.pallas import tpu as pltpu
from jax.sharding import PartitionSpec as P

HEAD_DIM = 128
NORM_EPS = 1e-5
ROPE_BASE = 10000.0
SCALE = HEAD_DIM ** -0.5
LOG2E = 1.4426950408889634
VMEM_LIMIT = 64000 * 1024
CORES = 2
N_CHIPS = 4
N_DEVICES = CORES * N_CHIPS
WAYS = 2
BUFFERS = 2
SUBS = 4
Q_ROWS = 256
ROWS_AT_ONCE = 32
FINE = 128
BF16 = jnp.bfloat16
F32 = jnp.float32
ANY = pl.BlockSpec(memory_space=pl.ANY)
VMEM = pl.BlockSpec(memory_space=pltpu.VMEM)
NT = (((1,), (1,)), ((), ()))
TN = (((0,), (0,)), ((), ()))


def height(array):
    return array.shape[0]


def width_of(array):
    return array.shape[1]


def piece_at(idx, size):
    return pl.ds(pl.multiple_of(idx * size, size), size)


def dma_sems(*shape):
    return pltpu.SemaphoreType.DMA(shape)


def dot(lhs, rhs):
    return jnp.dot(lhs, rhs, preferred_element_type=F32)


def dot_nt(lhs, rhs):
    return lax.dot_general(lhs, rhs, NT, preferred_element_type=F32)


def dot_tn(lhs, rhs):
    return lax.dot_general(lhs, rhs, TN, preferred_element_type=F32)


def params(collective_id=None, semantics=None):
    if collective_id is None:
        return pltpu.CompilerParams(vmem_limit_bytes=VMEM_LIMIT, dimension_semantics=semantics)
    return pltpu.CompilerParams(vmem_limit_bytes=VMEM_LIMIT, collective_id=collective_id, has_side_effects=True)


def row_mean(values):
    return jnp.mean(values, axis=-1, keepdims=True)


def row_sum(values):
    return jnp.sum(values, axis=-1, keepdims=True)


def rope_tables(seq_len, fine):
    half_dim = HEAD_DIM // 2
    freqs = np.float32(ROPE_BASE) ** (np.float32(-2.0) * np.arange(half_dim, dtype=np.float32) / np.float32(HEAD_DIM))
    tables = []
    for positions in (np.arange(fine), np.arange(0, seq_len, fine)):
        angles = positions.astype(np.float32)[:, None] * freqs[None, :]
        tables += [np.tile(np.cos(angles), 2).astype(np.float32), np.tile(np.sin(angles), 2).astype(np.float32)]
    return tables


def fill_rope(fine_cos, fine_sin, coarse_cos, coarse_sin, cos_ref, sin_ref):
    fine = height(fine_cos)
    sign = jnp.where(lax.broadcasted_iota(jnp.int32, (1, HEAD_DIM), 1) < HEAD_DIM // 2, -1.0, 1.0)

    def body(idx, carry):
        span = piece_at(idx, fine)
        big_cos, big_sin = coarse_cos[pl.ds(idx, 1)], coarse_sin[pl.ds(idx, 1)]
        cos_ref[span] = big_cos * fine_cos[...] - big_sin * fine_sin[...]
        sin_ref[span] = (big_sin * fine_cos[...] + big_cos * fine_sin[...]) * sign
        return carry

    lax.fori_loop(0, height(cos_ref) // fine, body, 0)


def rotate(values, cos_tab, sin_tab):
    return values * cos_tab + pltpu.roll(values, HEAD_DIM // 2, 1) * sin_tab


def rms_scale(x_f32, gain_row):
    inv_rms = lax.rsqrt(row_mean(x_f32 * x_f32) + NORM_EPS)
    return x_f32 * inv_rms * gain_row


def ring_place():
    me = lax.axis_index('tp')
    chip = me // 2
    core = me % 2
    return me, chip, core


def device_at(chip, core):
    return ((chip + N_CHIPS) % N_CHIPS) * 2 + core


def remote_copy(src, dst, send_sem, recv_sem, peer):
    return pltpu.make_async_remote_copy(
        src_ref=src, dst_ref=dst, send_sem=send_sem, recv_sem=recv_sem, device_id={'tp': peer}, device_id_type=pl.DeviceIdType.MESH
    )


def meet(peers):
    barrier = pltpu.get_barrier_semaphore()
    for peer in peers:
        pl.semaphore_signal(barrier, inc=1, device_id={'tp': peer}, device_id_type=pl.DeviceIdType.MESH)
    pl.semaphore_wait(barrier, len(peers))


OWN_PARTNER, OWN_AHEAD, OWN_BEHIND, FIRST_PARTNER, FIRST_AHEAD, SECOND_PARTNER, THIRD_PARTNER = KINDS = range(7)


class Gather:
    EVERY, EARLY, LATE = range(SUBS), range(SUBS // 2), range(SUBS // 2, SUBS)

    def __init__(self, full, send_sems, recv_sems):
        self.full, self.send_sems, self.recv_sems = full, send_sems, recv_sems
        self.me, chip, core = ring_place()
        turn = 1 - 2 * core
        self.chip, self.core, self.turn = chip, core, turn
        self.partner = device_at(chip, 1 - core)
        self.ahead = device_at(chip + turn, core)
        self.behind = device_at(chip - turn, core)
        self.first = device_at(chip - turn, core)
        self.first_other = device_at(chip + turn, 1 - core)
        self.second = device_at(chip + turn, core)
        self.second_other = device_at(chip - turn, 1 - core)
        self.third = device_at(chip + 2, core)
        self.third_other = device_at(chip + 2, 1 - core)

    def peers(self):
        return self.partner, self.ahead, self.behind

    def piece(self, kind, shard, sub, peer):
        rows = width_of(self.full) // SUBS
        part = self.full.at[shard, pl.ds(sub * rows, rows)]
        return remote_copy(part, part, self.send_sems.at[kind, sub], self.recv_sems.at[shard, sub], peer)

    def send(self, kind, shard, peer, subs=EVERY):
        for sub in subs:
            self.piece(kind, shard, sub, peer).start()

    def sent(self, kind, shard, peer, subs=EVERY):
        for sub in subs:
            self.piece(kind, shard, sub, peer).wait_send()

    def arrived(self, shard, subs=EVERY, pass_on=None):
        for sub in subs:
            self.piece(OWN_PARTNER, shard, sub, self.partner).wait_recv()
            if pass_on is not None:
                self.piece(pass_on, shard, sub, self.partner).start()

    def launch(self, subs=EVERY):
        self.send(OWN_AHEAD, self.me, self.ahead, subs)
        self.send(OWN_PARTNER, self.me, self.partner, subs)

    def turn_back(self):
        self.sent(OWN_AHEAD, self.me, self.ahead, range(SUBS - 1))
        self.send(OWN_BEHIND, self.me, self.behind)

    def pass_ahead(self):
        self.sent(OWN_BEHIND, self.me, self.behind, range(SUBS - 1))
        self.send(FIRST_AHEAD, self.first, self.ahead)

    def launch_both(self):
        self.launch()
        self.send(OWN_BEHIND, self.me, self.behind)

    def pass_piece(self, sub):
        self.piece(OWN_PARTNER, self.first, sub, self.partner).wait_recv()
        self.piece(FIRST_AHEAD, self.first, sub, self.ahead).start()
        self.piece(FIRST_PARTNER, self.first, sub, self.partner).start()
        self.arrived(self.second, (sub,), SECOND_PARTNER)

    def end_piece(self, sub):
        self.arrived(self.third, (sub,), THIRD_PARTNER)

    def events(self, early=False):
        return (
            lambda: None,
            lambda: (self.turn_back(), self.arrived(self.partner)),
            lambda: self.arrived(self.first, pass_on=FIRST_PARTNER),
            lambda: (self.pass_ahead() if early else None, self.arrived(self.first_other)),
            lambda: (None if early else self.pass_ahead(), self.arrived(self.second, pass_on=SECOND_PARTNER)),
            lambda: self.arrived(self.second_other),
            lambda: (self.arrived(self.third, self.EARLY, THIRD_PARTNER), self.arrived(self.third_other, self.EARLY)),
            lambda: (self.arrived(self.third, self.LATE, THIRD_PARTNER), self.arrived(self.third_other, self.LATE)),
        )

    def places(self, step):
        half = width_of(self.full) // 2
        pair = step // 2
        odd = step % BUFFERS
        side = self.turn * (1 - 2 * odd)
        hop = (3 * pair + (pair // 2) * (2 * pair - 5)) % N_CHIPS
        shard = device_at((self.chip + side * hop + N_DEVICES) % N_CHIPS, (self.core + odd) % 2)
        last = step // (N_DEVICES - 2)
        upper = (1 - last) * shard + last * self.third
        lower = (1 - last) * shard + last * self.third_other
        return (upper, last * odd * half), (lower, (1 - last) * half + last * odd * half)

    def finish(self, waited=SUBS - 1):
        self.sent(OWN_PARTNER, self.me, self.partner)
        self.sent(OWN_AHEAD, self.me, self.ahead, range(waited, SUBS))
        self.sent(OWN_BEHIND, self.me, self.behind, range(waited, SUBS))
        self.sent(FIRST_PARTNER, self.first, self.partner)
        self.sent(FIRST_AHEAD, self.first, self.ahead)
        self.sent(SECOND_PARTNER, self.second, self.partner)
        self.sent(THIRD_PARTNER, self.third, self.partner)


def run_at(step, actions):
    for idx, action in enumerate(actions):
        @pl.when(step == idx)
        def _():
            action()


def gather_scratch(tp_size, rows, width):
    return [
        pltpu.VMEM((tp_size, rows, width), BF16),
        dma_sems(len(KINDS), SUBS),
        dma_sems(tp_size, SUBS),
    ]


def half_rows(ref, place, half):
    return ref[place[0], pl.ds(pl.multiple_of(place[1], half), half)]


def both_halves(ref, places, half):
    return jnp.concatenate([half_rows(ref, place, half) for place in places], axis=0)


def table_rows(ref, places, half, rows):
    parts = [ref[pl.ds(pl.multiple_of(shard * rows + row, half), half)] for shard, row in places]
    return jnp.concatenate(parts, axis=0)


class RowWriter:
    def __init__(self, stages, outs, sems, rows):
        self.stages, self.outs, self.sems, self.rows = stages, outs, sems, rows

    def copies(self, slot, places):
        half = self.rows // 2
        items = []
        for idx in range(len(self.outs)):
            for part, (shard, row) in enumerate(places):
                start = pl.multiple_of(shard * self.rows + row, half)
                src = self.stages[idx].at[slot, pl.ds(part * half, half)]
                items.append(pltpu.make_async_copy(src, self.outs[idx].at[pl.ds(start, half)], self.sems.at[idx, slot, part]))
        return items

    def reuse(self, step):
        @pl.when(step >= 2)
        def _():
            for item in self.copies(step % BUFFERS, ((0, 0), (0, 0))):
                item.wait()

    def start(self, step, places):
        for item in self.copies(step % BUFFERS, places):
            item.start()

    def finish(self):
        for slot in range(BUFFERS):
            for item in self.copies(slot, ((0, 0), (0, 0))):
                item.wait()


def project_kernel(layer, first, x_ref, gain_ref, w_qkv_hbm, w_gate_hbm, w_up_hbm, *rest):
    n_out = 4 if first else 3
    n_tables = 4 if first else 2
    tables, rest = rest[:n_tables], rest[n_tables:]
    outs, rest = rest[:n_out], rest[n_out:]
    if first:
        u_ref, cos_out, sin_out, *rest = rest
    stages, rest = rest[:n_out], rest[n_out:]
    cos_ref, sin_ref, weights, full, send_sems, recv_sems, w_sems, out_sems = rest
    rows = width_of(full)
    half = rows // 2
    gather = Gather(full, send_sems, recv_sems)
    loads, spans, start = [], [], 0
    for idx, src in enumerate((w_qkv_hbm, w_gate_hbm, w_up_hbm)):
        spans.append(slice(start, start + src.shape[2]))
        start += src.shape[2]
        loads.append(pltpu.make_async_copy(src.at[layer], weights.at[:, spans[-1]], w_sems.at[idx]))
    if first:
        keep_tables = [pltpu.make_async_copy(cos_ref, cos_out, w_sems.at[3]), pltpu.make_async_copy(sin_ref, sin_out, w_sems.at[4])]
    else:
        loads += [pltpu.make_async_copy(src, dst, w_sems.at[3 + idx]) for idx, (src, dst) in enumerate(zip(tables, (cos_ref, sin_ref)))]
    writer = RowWriter(stages, outs, out_sems, rows)
    if first:
        norm_rows = min(ROWS_AT_ONCE, rows // SUBS)

        def norm(idx, carry):
            span = piece_at(idx, norm_rows)
            normed = rms_scale(x_ref[span].astype(F32), gain_ref[layer:layer + 1]).astype(BF16)
            full[gather.me, span] = normed
            u_ref[span] = normed
            return carry

        for load in loads:
            load.start()
        meet(gather.peers())
        per_piece = rows // SUBS // norm_rows
        for sub in range(SUBS):
            lax.fori_loop(sub * per_piece, (sub + 1) * per_piece, norm, 0)
            gather.launch((sub,))
        fill_rope(*tables, cos_ref, sin_ref)
        for item in keep_tables:
            item.start()
    else:
        own = pltpu.make_async_copy(x_ref, full.at[gather.me], w_sems.at[5])
        own.start()
        meet(gather.peers())
        own.wait()
        gather.launch()
        for load in loads:
            load.start()
    for load in loads:
        load.wait()

    def step_body(step, carry):
        run_at(step, gather.events())
        places = gather.places(step)
        slot = step % BUFFERS
        writer.reuse(step)
        cos_tab, sin_tab = table_rows(cos_ref, places, half, rows), table_rows(sin_ref, places, half, rows)
        product = dot(both_halves(full, places, half), weights[...]).astype(BF16)
        qkv, gate, up = (product[:, span] for span in spans)
        for head in range(width_of(qkv) // HEAD_DIM):
            cols = slice(head * HEAD_DIM, (head + 1) * HEAD_DIM)
            part = qkv[:, cols]
            if head % 3 != 2:
                part = rotate(part.astype(F32), cos_tab, sin_tab).astype(BF16)
            stages[0][slot, :, cols] = part
        stages[1][slot] = gate
        stages[2][slot] = up
        if first:
            stages[3][slot] = (jax.nn.silu(gate.astype(F32)) * up.astype(F32)).astype(BF16)
        writer.start(step, places)
        return carry

    lax.fori_loop(0, N_DEVICES, step_body, 0)
    gather.finish()
    writer.finish()
    if first:
        for item in keep_tables:
            item.wait()


def project(source, norm_gain, w_qkv, w_gate, w_up, tables, layer, tp_size, first):
    rows, width = source.shape
    seq_len = rows * tp_size
    qkv_cols, ff_cols = w_qkv.shape[2], w_gate.shape[2]
    out_cols = [qkv_cols, ff_cols, ff_cols] + ([ff_cols] if first else [])
    total = qkv_cols + 2 * ff_cols
    outs = [jax.ShapeDtypeStruct((seq_len, cols), BF16) for cols in out_cols]
    out_specs = [ANY] * len(outs)
    table = (seq_len, HEAD_DIM)
    if first:
        outs += [jax.ShapeDtypeStruct((rows, width), BF16)] + [jax.ShapeDtypeStruct(table, F32)] * 2
        out_specs += [VMEM, ANY, ANY]
    scratch = [pltpu.VMEM((BUFFERS, rows, cols), BF16) for cols in out_cols]
    scratch += [pltpu.VMEM(table, F32)] * 2
    scratch += [pltpu.VMEM((width, total), BF16)]
    scratch += gather_scratch(tp_size, rows, width)
    scratch += [dma_sems(6), pltpu.SemaphoreType.DMA((len(out_cols), 2, 2))]
    return pl.pallas_call(
        functools.partial(project_kernel, layer, first),
        out_shape=outs,
        in_specs=[VMEM if first else ANY, VMEM] + [ANY] * 3 + [VMEM if first else ANY] * len(tables),
        out_specs=out_specs,
        scratch_shapes=scratch,
        compiler_params=params(collective_id=1 + layer),
        name=f'project_{layer}',
    )(source, norm_gain, w_qkv, w_gate, w_up, *tables)


EACH = 4
PER_STEP = WAYS * EACH
N_BLOCKS = N_CHIPS * PER_STEP
N_PAIRS = (N_BLOCKS - PER_STEP) // 2
SLOTS = 6


def scatter_blocks(peers, load, product, beside, tmp, acc, ring, pair_send, pair_recv, ring_send, ring_recv):
    me, chip, core = ring_place()
    partner = device_at(chip, 1 - core)
    meet(peers or (partner, device_at(chip + 1, core), device_at(chip - 1, core)))

    def dest(step, way):
        return (chip + (step + 1) * (WAYS * way - 1) + N_DEVICES) % N_CHIPS

    def to_partner(block, slot):
        return remote_copy(tmp.at[slot, 1 - core], acc.at[block], pair_send.at[slot], pair_recv.at[block], partner)

    def to_next(block):
        peer = device_at(chip + 1 - 2 * (block % WAYS), core)
        return remote_copy(acc.at[block], ring.at[block], ring_send.at[block], ring_recv.at[block], peer)

    def serve_first(block):
        to_partner(block, block % SLOTS).wait_recv()
        acc[block] = acc[block] + tmp[block % SLOTS, core]
        to_next(block).start()

    def first_body(block, carry):
        load(block)

        @pl.when(block >= SLOTS)
        def _():
            to_partner(block - SLOTS, block % SLOTS).wait_send()

        way = block % WAYS
        product(dest(0, way), way * EACH + block // WAYS, 1, tmp.at[pl.ds(block % SLOTS, 1)])
        to_partner(block, block % SLOTS).start()

        @pl.when(block >= 1)
        def _():
            serve_first(block - 1)

        return carry

    lax.fori_loop(0, PER_STEP, first_body, 0)

    def pair_blocks(pair):
        step, rest = 1 + pair // EACH, pair % EACH
        way, col = rest % WAYS, 2 * (rest // 2)
        block = step * PER_STEP + 2 * col + way
        slot = (PER_STEP + 2 * pair) % SLOTS
        return step, way, col, ((block, slot), (block + 2, slot + 1))

    def body(pair, carry):
        @pl.when(pair < N_PAIRS)
        def _():
            step, way, col, blocks = pair_blocks(pair)
            load(PER_STEP + pair)
            for block, slot in blocks:
                to_partner(block, slot).wait_send()
            product(dest(step, way), way * EACH + col, 2, tmp.at[pl.ds(blocks[0][1], 2)])
            for block, slot in blocks:
                to_partner(block, slot).start()
            beside(pair)

        @pl.when(pair == 0)
        def _():
            serve_first(PER_STEP - 1)

        @pl.when(pair >= 1)
        def _():
            step, way, col, blocks = pair_blocks(pair - 1)
            for block, slot in blocks:
                to_partner(block, slot).wait_recv()
                to_next(block - PER_STEP).wait_recv()
                acc[block] = (acc[block] + tmp[slot, core]) + ring[block - PER_STEP]

                @pl.when(step < N_CHIPS - 1)
                def _():
                    to_next(block).start()

        return carry

    lax.fori_loop(0, N_PAIRS + 1, body, 0)
    for slot in range(SLOTS):
        to_partner(0, slot).wait_send()
    for block in range(N_BLOCKS - PER_STEP):
        to_next(block).wait_send()
    return lambda cols: acc.at[N_BLOCKS - PER_STEP + 2 * (cols % EACH) + cols // EACH]


def scatter_scratch(rows, width):
    cols = width // PER_STEP
    return [
        pltpu.VMEM((SLOTS, 2, rows, cols), F32),
        pltpu.VMEM((N_BLOCKS, rows, cols), F32),
        pltpu.VMEM((N_BLOCKS - PER_STEP, rows, cols), F32),
        dma_sems(SLOTS),
        dma_sems(N_BLOCKS),
        dma_sems(N_BLOCKS - PER_STEP),
        dma_sems(N_BLOCKS - PER_STEP),
    ]


def start_loads(w_load, row_loads_of):
    order = [(block % WAYS) * EACH + block // WAYS for block in range(PER_STEP)]
    for block, cols in enumerate(order):
        for item in w_load(cols):
            item.start()
        if block < 2:
            for item in row_loads_of[block]:
                item.start()
    for items in row_loads_of[2:]:
        for item in items:
            item.start()

    def load(product):
        for idx, cols in enumerate(order):
            @pl.when(product == idx)
            def _():
                for item in w_load(cols) + (row_loads_of[idx] if idx < 2 else []):
                    item.wait()

    return load


def row_loads(pairs, sems, rows, chip):
    def load(order, hop):
        span = pl.ds(pl.multiple_of(((chip + hop) % N_CHIPS) * rows, rows), rows)
        return [pltpu.make_async_copy(src.at[span], dst.at[span], sems.at[idx, order]) for idx, (src, dst) in enumerate(pairs)]

    return [load(order, hop) for order, hop in enumerate((3, 1, 2, 0))]


def forward_kernel(layer, next_gain, o_hbm, m_hbm, w_out_hbm, w_down_hbm, x_ref, gain_ref, y_ref, u_ref, o_all, m_all, w_out, w_down, row_sems, w_sems, *scatter):
    me, chip, core = ring_place()
    rows, width = x_ref.shape
    block_cols = width // PER_STEP
    loads = row_loads(((o_hbm, o_all), (m_hbm, m_all)), row_sems, CORES * rows, chip)

    def w_load(cols):
        span = pl.ds(cols * block_cols, block_cols)
        return [
            pltpu.make_async_copy(src.at[layer, :, span], dst.at[:, span], w_sems.at[idx, cols])
            for idx, (src, dst) in enumerate(((w_out_hbm, w_out), (w_down_hbm, w_down)))
        ]

    load_first = start_loads(w_load, loads)

    def load(product):
        load_first(product)
        for items, at in ((loads[2], PER_STEP), (loads[3], PER_STEP + 2 * EACH)):
            @pl.when(product == at)
            def _():
                for item in items:
                    item.wait()

    def product(dest, cols, n_cols, out):
        span = piece_at(dest, CORES * rows)
        w_span = pl.ds(pl.multiple_of(cols * block_cols, block_cols), n_cols * block_cols)
        total = dot(o_all[span], w_out[:, w_span]) + dot(m_all[span], w_down[:, w_span])
        for idx in range(n_cols):
            for kind in range(CORES):
                out[idx, kind] = total[kind * rows:(kind + 1) * rows, idx * block_cols:(idx + 1) * block_cols]

    result = scatter_blocks(None, load, product, lambda pair: None, *scatter)

    def finish(idx, carry):
        span = piece_at(idx, ROWS_AT_ONCE)
        summed = jnp.concatenate([result(cols)[span] for cols in range(PER_STEP)], axis=1)
        y = (x_ref[span].astype(F32) + summed).astype(BF16)
        y_ref[span] = y
        u_ref[span] = rms_scale(y.astype(F32), gain_ref[next_gain:next_gain + 1]).astype(BF16)
        return carry

    lax.fori_loop(0, rows // ROWS_AT_ONCE, finish, 0)


def block_output(attn_out, hidden, w_out, w_down, x_loc, norm_gain, layer):
    rows, width = x_loc.shape
    seq_len = height(attn_out)
    o_cols, ff_cols = width_of(w_out), width_of(w_down)
    shard = jax.ShapeDtypeStruct((rows, width), BF16)
    return pl.pallas_call(
        functools.partial(forward_kernel, layer, layer + 1),
        out_shape=[shard, shard],
        in_specs=[ANY] * 4 + [VMEM] * 2,
        out_specs=[VMEM] * 2,
        scratch_shapes=[
            pltpu.VMEM((seq_len, o_cols), BF16),
            pltpu.VMEM((seq_len, ff_cols), BF16),
            pltpu.VMEM((o_cols, width), BF16),
            pltpu.VMEM((ff_cols, width), BF16),
            dma_sems(2, N_CHIPS),
            dma_sems(2, PER_STEP),
        ] + scatter_scratch(rows, width),
        compiler_params=params(collective_id=5 + layer),
        name=f'block_output_{layer}',
    )(attn_out, hidden, w_out, w_down, x_loc, norm_gain)


GRAD_ROWS = N_PAIRS // 3


def backward_kernel(layer, dqkv_hbm, dgate_hbm, dup_hbm, w_qkv_hbm, w_gate_hbm, w_up_hbm, u_hbm, x_ref, dy_ref, gain_ref, *rest):
    first_layer = layer == 0
    if first_layer:
        later_gains_ref, *rest = rest
    dx_ref, dgain_ref, *rest = rest
    grads, rest = rest[:3], rest[3:]
    acts, rest = rest[:3], rest[3:]
    weights, rest = rest[:3], rest[3:]
    u_all, stage, row_sems, w_sems, u_sem, stage_sems, *rest = rest
    if first_layer:
        gain_parts, gain_send, gain_recv, *rest = rest
    scatter = rest
    me, chip, core = ring_place()
    rows, width = x_ref.shape
    block_cols = width // PER_STEP
    loads = row_loads(list(zip((dqkv_hbm, dgate_hbm, dup_hbm), acts)), row_sems, CORES * rows, chip)
    u_load = pltpu.make_async_copy(u_hbm, u_all, u_sem)

    def w_load(cols):
        span = pl.ds(cols * block_cols, block_cols)
        return [
            pltpu.make_async_copy(src.at[layer, span], dst.at[span], w_sems.at[idx, cols])
            for idx, (src, dst) in enumerate(zip((w_qkv_hbm, w_gate_hbm, w_up_hbm), weights))
        ]

    load_first = start_loads(w_load, loads)
    u_load.start()

    def load(product):
        load_first(product)

        @pl.when(product == PER_STEP)
        def _():
            for item in loads[2] + loads[3] + [u_load]:
                item.wait()

    def product(dest, cols, n_cols, out):
        span = piece_at(dest, CORES * rows)
        w_span = pl.ds(pl.multiple_of(cols * block_cols, block_cols), n_cols * block_cols)
        total = dot_nt(acts[0][span], weights[0][w_span]) + dot_nt(acts[1][span], weights[1][w_span]) + dot_nt(acts[2][span], weights[2][w_span])
        for idx in range(n_cols):
            for kind in range(CORES):
                out[idx, kind] = total[kind * rows:(kind + 1) * rows, idx * block_cols:(idx + 1) * block_cols]

    grad_rows = width // GRAD_ROWS

    def grad_out(which, part):
        slot = which % BUFFERS
        src = stage.at[slot, :, :width_of(grads[which])]
        return pltpu.make_async_copy(src, grads[which].at[piece_at(part, grad_rows)], stage_sems.at[slot])

    def beside(task):
        part = task // 3
        cols = piece_at(part, grad_rows)
        for turn, which in enumerate((2, 1, 0)):
            @pl.when(task % 3 == turn)
            def _():
                if which == 2:
                    @pl.when(part > 0)
                    def _():
                        grad_out(0, part - 1).wait()
                elif which == 0:
                    grad_out(2, part).wait()
                else:
                    @pl.when(part > 0)
                    def _():
                        grad_out(1, part - 1).wait()
                stage[which % BUFFERS, :, :width_of(grads[which])] = dot_tn(u_all[:, cols], acts[which][...]).astype(BF16)
                grad_out(which, part).start()

    peers = [(me + 1 + idx) % (N_DEVICES) for idx in range(N_DEVICES - 1)] if first_layer else None
    result = scatter_blocks(peers, load, product, beside, *scatter)
    gain_row = gain_ref[layer:layer + 1]
    dgain = gain_parts.at[me, layer:layer + 1] if first_layer else dgain_ref
    dgain[...] = jnp.zeros_like(dgain)

    def row_values(idx):
        span = piece_at(idx, ROWS_AT_ONCE)
        summed = jnp.concatenate([result(cols)[span] for cols in range(PER_STEP)], axis=1)
        x_f32 = x_ref[span].astype(F32)
        inv_rms = lax.rsqrt(row_mean(x_f32 * x_f32) + NORM_EPS)
        return span, summed.astype(BF16).astype(F32), x_f32, inv_rms

    def gain_rows(idx, carry):
        _, d_normed, x_f32, inv_rms = row_values(idx)
        dgain[...] += jnp.sum(d_normed * (x_f32 * inv_rms), axis=0, keepdims=True)
        return carry

    def input_rows(idx, carry):
        span, d_normed, x_f32, inv_rms = row_values(idx)
        scaled = d_normed * gain_row
        mix = row_mean(scaled * x_f32) * (inv_rms * inv_rms * inv_rms)
        dx_ref[span] = (dy_ref[span].astype(F32) + (scaled * inv_rms - x_f32 * mix)).astype(BF16)
        return carry

    lax.fori_loop(0, rows // ROWS_AT_ONCE, gain_rows, 0)
    if first_layer:
        gain_parts[me, 1:] = later_gains_ref[...]
        copies = [remote_copy(gain_parts.at[me], gain_parts.at[me], gain_send.at[idx], gain_recv.at[me], peer) for idx, peer in enumerate(peers)]
        for item in copies:
            item.start()
    lax.fori_loop(0, rows // ROWS_AT_ONCE, input_rows, 0)
    if first_layer:
        for idx, peer in enumerate(peers):
            remote_copy(gain_parts.at[peer], gain_parts.at[peer], gain_send.at[idx], gain_recv.at[peer], peer).wait_recv()
        total = gain_parts[0]
        for idx in range(1, N_DEVICES):
            total = total + gain_parts[idx]
        dgain_ref[...] = total
        for item in copies:
            item.wait_send()
    grad_out(0, GRAD_ROWS - 1).wait()
    grad_out(1, GRAD_ROWS - 1).wait()


def block_input_backward(d_qkv, d_gate, d_up, w_qkv, w_gate, w_up, u_full, x_loc, dy_loc, norm_gain, later_gains, layer):
    rows, width = x_loc.shape
    seq_len = height(d_qkv)
    n_layers = height(norm_gain)
    all_cols = (w_qkv.shape[2], w_gate.shape[2], w_up.shape[2])
    first_layer = layer == 0
    out_shape = [jax.ShapeDtypeStruct((rows, width), BF16), jax.ShapeDtypeStruct((n_layers if first_layer else 1, width), F32)]
    out_shape += [jax.ShapeDtypeStruct((width, cols), BF16) for cols in all_cols]
    scratch = [pltpu.VMEM((seq_len, cols), BF16) for cols in all_cols]
    scratch += [pltpu.VMEM((width, cols), BF16) for cols in all_cols]
    scratch += [pltpu.VMEM((seq_len, width), BF16), pltpu.VMEM((2, width // GRAD_ROWS, max(all_cols)), BF16)]
    scratch += [dma_sems(3, N_CHIPS), dma_sems(3, PER_STEP), pltpu.SemaphoreType.DMA, dma_sems(2)]
    if first_layer:
        scratch += [pltpu.VMEM((N_DEVICES, n_layers, width), F32), dma_sems(N_DEVICES - 1), dma_sems(N_DEVICES)]
    return pl.pallas_call(
        functools.partial(backward_kernel, layer),
        out_shape=out_shape,
        in_specs=[ANY] * 7 + [VMEM] * (4 if first_layer else 3),
        out_specs=[VMEM] * 2 + [ANY] * 3,
        scratch_shapes=scratch + scatter_scratch(rows, width),
        compiler_params=params(collective_id=7 + layer),
        name=f'block_input_backward_{layer}',
    )(d_qkv, d_gate, d_up, w_qkv, w_gate, w_up, u_full, x_loc, dy_loc, norm_gain, *((later_gains,) if first_layer else ()))


COLLECT_SLOTS = 3


def collect_kernel(moves, steps, dy_hbm, attn_hbm, hidden_hbm, *refs):
    ins, refs = refs[:len(moves)], refs[len(moves):]
    n_outs = 1 + max(out for out, _ in moves)
    outs, refs = refs[:n_outs], refs[n_outs:]
    buffers, refs = refs[:len(moves)], refs[len(moves):]
    dy_full, attn_out, hidden, stage, in_sems, out_sems, whole_sems, dy_sems, grad_sems = refs
    o_cols, cols = width_of(attn_out), width_of(dy_full) // steps

    def move(idx, step, back):
        rows = width_of(buffers[idx])
        span = piece_at(step, rows)
        slot = step % COLLECT_SLOTS
        out, layer = moves[idx]
        dst = outs[out].at[span] if layer is None else outs[out].at[layer, span]
        if back:
            return pltpu.make_async_copy(buffers[idx].at[slot], dst, out_sems.at[idx, slot])
        return pltpu.make_async_copy(ins[idx].at[span], buffers[idx].at[slot], in_sems.at[idx, slot])

    def moves_of(step, back):
        return [move(idx, step, back) for idx in range(len(moves))]

    def dy_load(step):
        span = piece_at(step, cols)
        return pltpu.make_async_copy(dy_hbm.at[:, span], dy_full.at[:, span], dy_sems.at[step])

    def grads(step):
        span = piece_at(step, cols)
        slot = step % BUFFERS
        return (
            pltpu.make_async_copy(stage.at[slot, :o_cols], outs[1].at[1, :, span], grad_sems.at[slot, 0]),
            pltpu.make_async_copy(stage.at[slot, o_cols:], outs[2].at[1, :, span], grad_sems.at[slot, 1]),
        )

    whole = [pltpu.make_async_copy(attn_hbm, attn_out, whole_sems.at[0]), pltpu.make_async_copy(hidden_hbm, hidden, whole_sems.at[1])]
    for item in moves_of(0, False) + whole + [dy_load(0)] + moves_of(1, False):
        item.start()
    for step in range(1, steps):
        dy_load(step).start()
    for item in whole:
        item.wait()

    def body(step, carry):
        @pl.when((step >= 1) & (step + 2 <= steps))
        def _():
            @pl.when(step >= COLLECT_SLOTS - 1)
            def _():
                for item in moves_of(step + 1 - COLLECT_SLOTS, True):
                    item.wait()

            for item in moves_of(step + 1, False):
                item.start()

        for item in moves_of(step, False):
            item.wait()
        for item in moves_of(step, True):
            item.start()

        @pl.when(step >= 2)
        def _():
            for item in grads(step - 2):
                item.wait()

        dy_load(step).wait()
        dy_cols = dy_full[:, piece_at(step, cols)]
        slot = step % BUFFERS
        stage[slot, :o_cols] = dot_tn(attn_out[...], dy_cols).astype(BF16)
        stage[slot, o_cols:] = dot_tn(hidden[...], dy_cols).astype(BF16)
        for item in grads(step):
            item.start()
        return carry

    lax.fori_loop(0, steps, body, 0)
    for step in range(steps - COLLECT_SLOTS, steps):
        for item in moves_of(step, True):
            item.wait()
    for item in grads(steps - 2) + grads(steps - 1):
        item.wait()


def collect(grad_x, dy_full, attn_out, hidden, g_out_first, g_down_first, made, steps):
    n_layers = len(made[0])
    assert n_layers == 2
    seq_len, width, o_cols, ff_cols = height(dy_full), width_of(dy_full), width_of(attn_out), width_of(hidden)
    sources = [(grad_x, 0, None), (g_out_first, 1, 0), (g_down_first, 2, 0)]
    sources += [(item, 3 + idx, layer) for idx, layers in enumerate(made) for layer, item in enumerate(layers)]
    moves = [(out, layer) for _, out, layer in sources]
    out_shape = [jax.ShapeDtypeStruct(grad_x.shape, BF16), jax.ShapeDtypeStruct((n_layers, o_cols, width), BF16), jax.ShapeDtypeStruct((n_layers, ff_cols, width), BF16)]
    out_shape += [jax.ShapeDtypeStruct((n_layers,) + layers[0].shape, BF16) for layers in made]
    scratch = [pltpu.VMEM((COLLECT_SLOTS, height(item) // steps, width_of(item)), BF16) for item, _, _ in sources]
    scratch += [pltpu.VMEM(item.shape, BF16) for item in (dy_full, attn_out, hidden)]
    scratch += [
        pltpu.VMEM((2, o_cols + ff_cols, width // steps), BF16),
        pltpu.SemaphoreType.DMA((len(moves), COLLECT_SLOTS)),
        pltpu.SemaphoreType.DMA((len(moves), COLLECT_SLOTS)),
        dma_sems(2),
        dma_sems(steps),
        dma_sems(2, 2),
    ]
    return pl.pallas_call(
        functools.partial(collect_kernel, moves, steps),
        out_shape=out_shape,
        in_specs=[ANY] * (3 + len(moves)),
        out_specs=[ANY] * len(out_shape),
        scratch_shapes=scratch,
        compiler_params=params(),
        name='collect',
    )(dy_full, attn_out, hidden, *[item for item, _, _ in sources])


def causal_tile(size):
    return lax.broadcasted_iota(jnp.int32, (size, size), 0) >= lax.broadcasted_iota(jnp.int32, (size, size), 1)


def masked_scores(query, keys):
    size = height(query)
    q_start = height(keys) - size
    scores = dot_nt(query, keys)
    diagonal = jnp.where(causal_tile(size), scores[:, q_start:], -1e30)
    scores = diagonal if q_start == 0 else jnp.concatenate([scores[:, :q_start], diagonal], axis=1)
    return scores * (SCALE * LOG2E)


def head_cols(head, part, parts):
    return pl.ds(pl.multiple_of((head * parts + part) * HEAD_DIM, HEAD_DIM), HEAD_DIM)


def attend_rows(q_start, head, qkv_ref, o_ref, lse_ref):
    span, seen = slice(q_start, q_start + Q_ROWS), slice(0, q_start + Q_ROWS)
    scores = masked_scores(qkv_ref[span, head_cols(head, 0, 3)], qkv_ref[seen, head_cols(head, 1, 3)])
    row_max = jnp.max(scores, axis=-1, keepdims=True)
    prob = jnp.exp2(scores - row_max)
    norm = row_sum(prob)
    prob = (prob * (1.0 / norm)).astype(BF16)
    o_ref[span, head_cols(head, 0, 1)] = dot(prob, qkv_ref[seen, head_cols(head, 2, 3)]).astype(BF16)
    lse_ref[span, head_cols(head, 0, 1)] = jnp.broadcast_to(row_max + jnp.log2(norm), (Q_ROWS, HEAD_DIM))


def attend_rows_backward(q_start, head, qkv_ref, lse_ref, do_ref, o_ref, cos_ref, sin_ref, dq_ref, dkt_acc, dvt_acc, prob_tmp, ds_tmp):
    span, seen = slice(q_start, q_start + Q_ROWS), slice(0, q_start + Q_ROWS)
    query = qkv_ref[span, head_cols(head, 0, 3)]
    d_out = do_ref[span, head_cols(head, 0, 1)]
    inner = row_sum(d_out.astype(F32) * o_ref[span, head_cols(head, 0, 1)].astype(F32))
    lse = lse_ref[span, head_cols(head, 0, 1)][:, :1]
    for k_start in range(0, q_start + Q_ROWS, Q_ROWS):
        keys = slice(k_start, k_start + Q_ROWS)
        scores = dot_nt(query, qkv_ref[keys, head_cols(head, 1, 3)]) * (SCALE * LOG2E)
        if k_start == q_start:
            scores = jnp.where(causal_tile(Q_ROWS), scores, -1e30)
        prob = jnp.exp2(scores - lse)
        d_prob = dot_nt(d_out, qkv_ref[keys, head_cols(head, 2, 3)]).astype(BF16).astype(F32)
        ds_tmp[:, keys] = (prob * (d_prob - inner) * SCALE).astype(BF16)
        prob_tmp[:, keys] = prob.astype(BF16)
    dvt_acc[head, :, seen] += dot_tn(d_out, prob_tmp[:, seen])
    dkt_acc[head, :, seen] += dot_tn(query, ds_tmp[:, seen])
    d_query = dot(ds_tmp[:, seen], qkv_ref[seen, head_cols(head, 1, 3)]).astype(BF16)
    dq_ref[span, head_cols(head, 0, 3)] = rotate(d_query.astype(F32), cos_ref[span], -sin_ref[span]).astype(BF16)


def attention_kernel(qkv_ref, o_ref, lse_ref):
    for q_start in range(0, height(qkv_ref), Q_ROWS):
        attend_rows(q_start, 0, qkv_ref, o_ref, lse_ref)


def attention(qkv):
    seq_len, cols = qkv.shape
    heads = cols // (3 * HEAD_DIM)
    return pl.pallas_call(
        attention_kernel,
        grid=(heads,),
        out_shape=[jax.ShapeDtypeStruct((seq_len, heads * HEAD_DIM), BF16), jax.ShapeDtypeStruct((seq_len, heads * HEAD_DIM), F32)],
        in_specs=[pl.BlockSpec((seq_len, 3 * HEAD_DIM), lambda h: (0, h))],
        out_specs=[pl.BlockSpec((seq_len, HEAD_DIM), lambda h: (0, h))] * 2,
        compiler_params=params(semantics=('arbitrary',)),
        name='attention',
    )(qkv)


def middle_kernel(layer, with_forward, dy_hbm, u_hbm, w_out_hbm, w_down_hbm, gate_hbm, up_hbm, cos_hbm, sin_hbm, qkv_hbm, *rest):
    if not with_forward:
        (o_hbm, lse_hbm), rest = rest[:2], rest[2:]
    (dgate_hbm, dup_hbm, dqkv_hbm, u_full_hbm), rest = rest[:4], rest[4:]
    if with_forward:
        (dy_full_hbm, o_hbm, hidden_hbm), rest = rest[:3], rest[3:]
    else:
        (g_out_hbm, g_down_hbm), rest = rest[:2], rest[2:]
    (dgate_stage, dup_stage, gate_in, up_in, weights, qkv, o_all, lse, hidden, d_attn, dqkv, dk_acc, dv_acc, prob_tmp, ds_tmp, grad_stage, cos_ref, sin_ref), rest = rest[:18], rest[18:]
    dy_full, dy_send, dy_recv, u_full, u_send, u_recv, load_sems, out_sems, in_sems, u_sems, dqkv_sem, grad_sems = rest
    rows = width_of(dy_full)
    half = rows // 2
    seq_len = height(qkv)
    n_heads = width_of(o_all) // HEAD_DIM
    o_cols = width_of(o_all)
    gather = Gather(dy_full, dy_send, dy_recv)
    u_gather = Gather(u_full, u_send, u_recv)
    me = gather.me
    own_dy = pltpu.make_async_copy(dy_hbm, dy_full.at[me], load_sems.at[0])
    own_u = pltpu.make_async_copy(u_hbm, u_full.at[me], load_sems.at[1])
    w_loads = [
        pltpu.make_async_copy(w_out_hbm.at[layer], weights.at[:o_cols], load_sems.at[2]),
        pltpu.make_async_copy(w_down_hbm.at[layer], weights.at[o_cols:], load_sems.at[3]),
    ]
    loads = [
        pltpu.make_async_copy(src, dst, load_sems.at[4 + idx])
        for idx, (src, dst) in enumerate([(qkv_hbm, qkv), (cos_hbm, cos_ref), (sin_hbm, sin_ref)] + ([] if with_forward else [(o_hbm, o_all), (lse_hbm, lse)]))
    ]
    writer = RowWriter((dgate_stage, dup_stage), (dgate_hbm, dup_hbm), out_sems, rows)
    own_dy.start()
    meet(gather.peers())
    own_dy.wait()
    gather.launch()
    for item in w_loads + loads + [own_u]:
        item.start()
    dk_acc[...] = jnp.zeros_like(dk_acc)
    dv_acc[...] = jnp.zeros_like(dv_acc)
    for item in w_loads:
        item.wait()

    def both_heads(function, q_start, *args):
        def body(head, carry):
            function(q_start, head, *args)
            return carry

        lax.fori_loop(0, n_heads, body, 0)

    def attend(index):
        run_at(index, [functools.partial(both_heads, attend_rows, q_start, qkv, o_all, lse) for q_start in range(0, seq_len, Q_ROWS)])

    def attend_backward(index):
        refs = (qkv, lse, d_attn, o_all, cos_ref, sin_ref, dqkv, dk_acc, dv_acc, prob_tmp, ds_tmp)
        run_at(index, [functools.partial(both_heads, attend_rows_backward, q_start, *refs) for q_start in range(0, seq_len, Q_ROWS)])

    def finish_keys_values():
        def body(idx, carry):
            span = piece_at(idx, Q_ROWS)
            for head in range(n_heads):
                d_keys = dk_acc[head, :, span].T.astype(BF16).astype(F32)
                dqkv[span, head_cols(head, 1, 3)] = rotate(d_keys, cos_ref[span], -sin_ref[span]).astype(BF16)
                dqkv[span, head_cols(head, 2, 3)] = dv_acc[head, :, span].T.astype(BF16)
            return carry

        lax.fori_loop(0, seq_len // Q_ROWS, body, 0)
        keep_dqkv.start()

    keep_dqkv = pltpu.make_async_copy(dqkv, dqkv_hbm, dqkv_sem)

    def dy_rows(step):
        run_at(step, gather.events(early=True))

        @pl.when(step == N_DEVICES - 2)
        def _():
            own_u.wait()
            u_gather.launch_both()
            keep_u(me)

        places = gather.places(step)
        slot = step % BUFFERS
        fetch = []
        for idx, (src, dst) in enumerate(((gate_hbm, gate_in), (up_hbm, up_in))):
            for part, (shard, row) in enumerate(places):
                here = pl.ds(pl.multiple_of(shard * rows + row, half), half)
                fetch.append(pltpu.make_async_copy(src.at[here], dst.at[pl.ds(part * half, half)], in_sems.at[idx, part]))
        for item in fetch:
            item.start()
        writer.reuse(step)
        product = dot_nt(both_halves(dy_full, places, half), weights[...]).astype(BF16)
        d_hidden = product[:, o_cols:].astype(F32)
        for item in fetch:
            item.wait()
        gate, up = gate_in[...].astype(F32), up_in[...].astype(F32)
        sig = jax.nn.sigmoid(gate)
        act = gate * sig
        hidden_rows = (act * up).astype(BF16)
        for part, (shard, row) in enumerate(places):
            here = pl.ds(pl.multiple_of(shard * rows + row, half), half)
            d_attn[here] = product[part * half:(part + 1) * half, :o_cols]
            hidden[here] = hidden_rows[part * half:(part + 1) * half]
        dgate_stage[slot] = (d_hidden * up * (sig + act * (1.0 - sig))).astype(BF16)
        dup_stage[slot] = (d_hidden * act).astype(BF16)
        writer.start(step, places)

    def wait_loads(step):
        @pl.when(step == 0)
        def _():
            for item in loads:
                item.wait()

    def dy_step_forward(step, carry):
        dy_rows(step)
        wait_loads(step)
        attend(seq_len // Q_ROWS - 1 - step)
        return carry

    def dy_step_backward(step, carry):
        @pl.when(step < N_DEVICES)
        def _():
            dy_rows(step)

        wait_loads(step)
        after = step // (N_DEVICES)
        turn = (1 - after) * (step // 2) + after * (step - 5)
        upper, lower = gather.places(turn)
        shard = upper[0] + (turn // 7) * (lower[0] - upper[0])

        @pl.when(step == 10)
        def _():
            u_gather.pass_piece(0)

        @pl.when(step == 12)
        def _():
            u_gather.pass_piece(1)

        @pl.when((step == 0) | (step == 3) | (step == 5) | (step >= N_DEVICES))
        def _():
            attend_backward(shard * rows // Q_ROWS)

        return carry

    def keep_u(shard):
        pltpu.make_async_copy(u_full.at[shard], u_full_hbm.at[shard], u_sems.at[shard]).start()

    if with_forward:
        lax.fori_loop(0, N_DEVICES, dy_step_forward, 0)
    else:
        lax.fori_loop(0, N_DEVICES + 5, dy_step_backward, 0)

    def grad_copies(step):
        slot = step % BUFFERS
        cols = piece_at(step, grad_cols)
        return (
            pltpu.make_async_copy(grad_stage.at[slot, :o_cols], g_out_hbm.at[:, cols], grad_sems.at[slot, 0]),
            pltpu.make_async_copy(grad_stage.at[slot, o_cols:], g_down_hbm.at[:, cols], grad_sems.at[slot, 1]),
        )

    grad_cols = dy_full.shape[2] // (N_DEVICES)
    first_parts, last_parts = u_gather.pass_piece, u_gather.end_piece
    if with_forward:
        u_at = {1: [0], 2: [1], 4: [2], 7: [3]}
    else:
        u_at = {1: [2], 4: [3], 6: [4], 7: [5]}

    def u_event(at):
        for part in u_at.get(at, ()):
            first_parts(part) if part < SUBS else last_parts(part - SUBS)
        if at == 2 and not with_forward:
            finish_keys_values()

    u_events = [functools.partial(u_event, at) for at in range(N_DEVICES)]
    last_part = max(part for parts in u_at.values() for part in parts) + 1

    def u_step(step, carry):
        run_at(step, u_events)
        if with_forward:
            attend_backward(seq_len // Q_ROWS - 1 - step)
            return carry

        @pl.when(step >= 2)
        def _():
            for item in grad_copies(step - 2):
                item.wait()

        cols = piece_at(step, grad_cols)
        dy_cols = dy_full[:, :, cols].reshape(seq_len, grad_cols)
        slot = step % BUFFERS
        grad_stage[slot, :o_cols] = dot_tn(o_all[...], dy_cols).astype(BF16)
        grad_stage[slot, o_cols:] = dot_tn(hidden[...], dy_cols).astype(BF16)
        for item in grad_copies(step):
            item.start()
        return carry

    if with_forward:
        keeps = [pltpu.make_async_copy(src, dst, grad_sems.at[0, idx]) for idx, (src, dst) in enumerate(((o_all, o_hbm), (hidden, hidden_hbm)))]
        keeps += [pltpu.make_async_copy(dy_full, dy_full_hbm, grad_sems.at[1, 0])]
        for item in keeps:
            item.start()
    lax.fori_loop(0, N_DEVICES, u_step, 0)
    if with_forward:
        finish_keys_values()
    for shard in (u_gather.partner, u_gather.first_other, u_gather.second_other):
        u_gather.arrived(shard)
        keep_u(shard)
    for shard in (u_gather.first, u_gather.second):
        keep_u(shard)
    for part in range(last_part, 2 * SUBS):
        last_parts(part - SUBS)
    keep_u(u_gather.third)
    u_gather.arrived(u_gather.third_other)
    keep_u(u_gather.third_other)
    for item in keeps if with_forward else grad_copies(N_DEVICES - 2) + grad_copies(N_DEVICES - 1):
        item.wait()
    gather.finish()
    u_gather.finish(0)
    writer.finish()
    keep_dqkv.wait()
    for shard in range(N_DEVICES):
        pltpu.make_async_copy(u_full.at[shard], u_full_hbm.at[shard], u_sems.at[shard]).wait()


def middle(dy_loc, u_loc, w_out, w_down, gate_act, up_act, tables, qkv, attended, layer, tp_size):
    rows, width = dy_loc.shape
    seq_len = rows * tp_size
    o_cols, ff_cols, qkv_cols = width_of(w_out), width_of(w_down), width_of(qkv)
    n_heads = o_cols // HEAD_DIM
    total = o_cols + ff_cols
    outs = [(seq_len, ff_cols), (seq_len, ff_cols), (seq_len, qkv_cols), (tp_size, rows, width)]
    outs += [(o_cols, width), (ff_cols, width)] if attended else [(tp_size, rows, width), (seq_len, o_cols), (seq_len, ff_cols)]
    scratch = [pltpu.VMEM((2, rows, ff_cols), BF16)] * 2
    scratch += [pltpu.VMEM((rows, ff_cols), BF16)] * 2
    scratch += [
        pltpu.VMEM((total, width), BF16),
        pltpu.VMEM((seq_len, qkv_cols), BF16),
        pltpu.VMEM((seq_len, o_cols), BF16),
        pltpu.VMEM((seq_len, o_cols), F32),
        pltpu.VMEM((seq_len, ff_cols), BF16),
        pltpu.VMEM((seq_len, o_cols), BF16),
        pltpu.VMEM((seq_len, qkv_cols), BF16),
        pltpu.VMEM((n_heads, HEAD_DIM, seq_len), F32),
        pltpu.VMEM((n_heads, HEAD_DIM, seq_len), F32),
        pltpu.VMEM((Q_ROWS, seq_len), BF16),
        pltpu.VMEM((Q_ROWS, seq_len), BF16),
        pltpu.VMEM((2, total, width // (N_DEVICES)), BF16),
    ]
    scratch += [pltpu.VMEM(table.shape, F32) for table in tables]
    scratch += gather_scratch(tp_size, rows, width) + gather_scratch(tp_size, rows, width)
    scratch += [
        dma_sems(9),
        dma_sems(2, 2, 2),
        dma_sems(2, 2),
        dma_sems(tp_size),
        pltpu.SemaphoreType.DMA,
        dma_sems(2, 2),
    ]
    return pl.pallas_call(
        functools.partial(middle_kernel, layer, not attended),
        out_shape=[jax.ShapeDtypeStruct(shape, BF16) for shape in outs],
        in_specs=[ANY] * (9 + len(attended)),
        out_specs=[ANY] * len(outs),
        scratch_shapes=scratch,
        compiler_params=params(collective_id=3 + layer),
        name=f'middle_{layer}',
    )(dy_loc, u_loc, w_out, w_down, gate_act, up_act, *tables, qkv, *attended)


def solution(mesh):
    tp_size = mesh.shape['tp']
    assert tp_size == N_DEVICES
    row_spec = P(('dp', 'tp'), None)
    col_spec = P(None, None, 'tp')
    inner_spec = P(None, 'tp', None)

    def device_program(x_loc, dy_loc, norm_gain, w_qkv, w_out, w_gate, w_up, w_down):
        n_layers = height(w_qkv)
        seq_len = height(x_loc) * tp_size
        tables = tuple(jnp.asarray(table) for table in rope_tables(seq_len, FINE))
        x_cur, source = x_loc, x_loc
        saved = []
        for layer in range(n_layers):
            first, last = layer == 0, layer == n_layers - 1
            qkv, gate_act, up_act, *more = project(source, norm_gain, w_qkv, w_gate, w_up, tables, layer, tp_size, first)
            u_loc = more[1] if first else source
            tables = more[2:] if first else tables
            if last:
                saved.append((x_cur, u_loc, qkv, gate_act, up_act, ()))
            else:
                attended = attention(qkv)
                saved.append((x_cur, u_loc, qkv, gate_act, up_act, tuple(attended)))
                x_cur, source = block_output(attended[0], more[0], w_out, w_down, x_cur, norm_gain, layer)
        grad_cur = dy_loc
        grads, gains = [None] * n_layers, ()
        for layer in reversed(range(n_layers)):
            x_cur, u_loc, qkv, gate_act, up_act, attended = saved[layer]
            d_gate, d_up, d_qkv, u_full, *more = middle(grad_cur, u_loc, w_out, w_down, gate_act, up_act, tables, qkv, attended, layer, tp_size)
            u_full = u_full.reshape(seq_len, u_full.shape[2])
            later_gains = jnp.concatenate(gains, axis=0) if gains else None
            grad_cur, gain_grad, g_qkv, g_gate, g_up = block_input_backward(
                d_qkv, d_gate, d_up, w_qkv, w_gate, w_up, u_full, x_cur, grad_cur, norm_gain, later_gains, layer
            )
            grads[layer] = (g_qkv, g_gate, g_up)
            if layer == n_layers - 1:
                dy_full, attn_out, hidden = more
            gains = (gain_grad,) + gains
        grad_x, g_out, g_down, g_qkv, g_gate, g_up = collect(grad_cur, dy_full.reshape(seq_len, -1), attn_out, hidden, *more, list(zip(*grads)), 8)
        return (grad_x, gains[0], g_qkv, g_out, g_gate, g_up, g_down)

    return jax.shard_map(
        device_program,
        mesh=mesh,
        in_specs=(row_spec, row_spec, P(None, None), col_spec, inner_spec, col_spec, col_spec, inner_spec),
        out_specs=(row_spec, P('dp', None), P('dp', None, 'tp'), P('dp', 'tp', None), P('dp', None, 'tp'), P('dp', None, 'tp'), P('dp', 'tp', None)),
        check_vma=False,
    )
```

time: 567 us -> 551 us (0.972)
  Pallas kernels: 556 us -> 541 us
    pallas_call x2, Pallas kernels: 174 us -> 156 us  [middle(): pl.pallas_call(functools.partial(middle_kernel, layer, not attended), out...]
where the time goes in v3:
time: 551 us; the launch traced here: 543 us
  Pallas kernels  541 us (98%)
    pallas_call x2, Pallas kernels, block_input_backward(): pl.pallas_call(functools.partial(backward_kernel, layer), out_shape=out_s...  169 us
    pallas_call x2, Pallas kernels, middle(): pl.pallas_call(functools.partial(middle_kernel, layer, not attended), out...  156 us
    pallas_call x2, Pallas kernels, project(): pl.pallas_call(functools.partial(project_kernel, layer, first), out_shape...  96.6 us
    pallas_call x1, Pallas kernels, block_output(): pl.pallas_call(functools.partial(forward_kernel, layer, layer + 1), out_s...  78.3 us
    pallas_call x1, Pallas kernels, collect(): pl.pallas_call(functools.partial(collect_kernel, moves, steps), out_shape...  27.7 us
    pallas_call x1, Pallas kernels, attention(): pl.pallas_call(attention_kernel, grid=(heads,), out_shape=[jax.ShapeDtype...  14.2 us

profile of v3, /device:TPU:81, one launch (start us, length us, event | category | flops | bytes accessed | tf_op | source)
XLA Modules:
  0.0 542.8 jit_solution(16910887604976097448)
XLA Ops:
  0.6 50.6 %project_0.1 = (bf16[2048,768]{1,0:T(8,128)(2,1)}, bf16[2048,1024]{1,0:T(8,128)(2,1)}, bf16[2048,1024]{1,0:T(8,128)(2,1)}, bf16[2048,1024]{1,0:T(8,128)(2,1)}, b...) custom-call(bf16[256,2048]{1,0:T(8,128)(2,1)} %x_ref.5, f32[2,2048]{1,0:T(2,128)} %gain_ref.9, ...), custom_call_target="tpu_custom_call" | custom-call | tf_op jit(solution)/shard_map/project_0/pallas_call | solution.py:392
  51.2 14.2 %attention.1 = (bf16[2048,256]{1,0:T(8,128)(2,1)}, f32[2048,256]{1,0:T(8,128)}) custom-call(bf16[2048,768]{1,0:T(8,128)(2,1)} %get-tuple-element.50.qkv_ref.qkv_hbm), custom_call_target="tpu_custom_call" | custom-call | tf_op jit(solution)/shard_map/attention/pallas_call | solution.py:916
  65.4 78.3 %block_output_0.1 = (bf16[256,2048]{1,0:T(8,128)(2,1)}, bf16[256,2048]{1,0:T(8,128)(2,1)}) custom-call(bf16[2048,256]{1,0:T(8,128)(2,1)} %get-tuple-element.51.o_hbm.rest_0_, bf16[2048,1024]{1,0:T(8,128)(2,1)} %get-tuple-element.52.m_hbm, bf16[2,256,2048]{2,1,0:T(8,128)(2,1)} %w_out_hbm.5, bf16[2,1024,2048]{2,1,0:T(8,128)(2,1)} %w_down_hbm.5, ...), custom_call_target="tpu_custom_call" | custom-call | tf_op jit(solution)/shard_map/block_output_0/pallas_call | solution.py:586
  143.7 46.0 %project_1.1 = (bf16[2048,768]{1,0:T(8,128)(2,1)}, bf16[2048,1024]{1,0:T(8,128)(2,1)}, bf16[2048,1024]{1,0:T(8,128)(2,1)}) custom-call(bf16[256,2048]{1,0:T(8,128)(2,1)} %get-tuple-element.53.x_ref.u_hbm, f32[2,2048]{1,0:T(2,128)} %gain_ref.9, bf16[2,2048,768]{2,1,0:T(8,128)(2,1)} %w_qkv_hbm.7, bf16[2,2048,1024]{2,1,0:T(8,128)(2,1)} %w_gate_hbm.7, ...), custom_call_target="tpu_custom_call" | custom-call | tf_op jit(solution)/shard_map/project_1/pallas_call | solution.py:392
  189.7 77.1 %middle_1.1 = (bf16[2048,1024]{1,0:T(8,128)(2,1)}, bf16[2048,1024]{1,0:T(8,128)(2,1)}, bf16[2048,768]{1,0:T(8,128)(2,1)}, bf16[8,256,2048]{2,1,0:T(8,128)(2,1)},...) custom-call(bf16[256,2048]{1,0:T(8,128)(2,1)} %dy_ref.1, ...), custom_call_target="tpu_custom_call" | custom-call | tf_op jit(solution)/shard_map/middle_1/pallas_call | solution.py:1181
  266.9 82.5 %block_input_backward_1.1 = (bf16[256,2048]{1,0:T(8,128)(2,1)}, f32[1,2048]{1,0:T(1,128)}, bf16[2048,768]{1,0:T(8,128)(2,1)}, bf16[2048,1024]{1,0:T(8,128)(2,1)}, bf16[2048,1024]{1,0:T(8,128)(2,1)}) custom-call(bf16[2048,768]{1,0:T(8,128)(2,1)} %get-tuple-element.62.dqkv_hbm, bf16[2048,1024]{1,0:T(8,128)(2,1)} %get-tuple-element.63.dgate_hbm, ...), custom_call_target="tpu_custom_call" | custom-call | tf_op jit(solution)/shard_map/block_input_backward_1/pallas_call | solution.py:736
  349.4 78.4 %middle_0.1 = (bf16[2048,1024]{1,0:T(8,128)(2,1)}, bf16[2048,1024]{1,0:T(8,128)(2,1)}, bf16[2048,768]{1,0:T(8,128)(2,1)}, bf16[8,256,2048]{2,1,0:T(8,128)(2,1)},...) custom-call(bf16[256,2048]{1,0:T(8,128)(2,1)} %get-tuple-element.67.dy_hbm.dy_ref, ...), custom_call_target="tpu_custom_call" | custom-call | tf_op jit(solution)/shard_map/middle_0/pallas_call | solution.py:1181
  427.8 86.2 %block_input_backward_0.1 = (bf16[256,2048]{1,0:T(8,128)(2,1)}, f32[2,2048]{1,0:T(2,128)}, bf16[2048,768]{1,0:T(8,128)(2,1)}, bf16[2048,1024]{1,0:T(8,128)(2,1)}, bf16[2048,1024]{1,0:T(8,128)(2,1)}) custom-call(bf16[2048,768]{1,0:T(8,128)(2,1)} %get-tuple-element.72.dqkv_hbm, bf16[2048,1024]{1,0:T(8,128)(2,1)} %get-tuple-element.73.dgate_hbm, ...), custom_call_target="tpu_custom_call" | custom-call | tf_op jit(solution)/shard_map/block_input_backward_0/pallas_call | solution.py:736
  514.0 0.0 copy-start
  514.0 27.7 %collect.1 = (bf16[256,2048]{1,0:T(8,128)(2,1)}, bf16[2,256,2048]{2,1,0:T(8,128)(2,1)}, bf16[2,1024,2048]{2,1,0:T(8,128)(2,1)}, bf16[2,2048,768]{2,1,0:T(8,128)(...) custom-call(bf16[2048,2048]{1,0:T(8,128)(2,1)} %bitcast.4, ...), custom_call_target="tpu_custom_call" | custom-call | tf_op jit(solution)/shard_map/collect/pallas_call | solution.py:848
  541.7 0.0 copy-done
  541.7 0.6 copy.20
Async XLA Ops:
  514.0 27.7 %copy-start = (f32[2,2048]{1,0:T(2,128)S(1)}, f32[2,2048]{1,0:T(2,128)}, u32[]{:S(2)}) copy-start(f32[2,2048]{1,0:T(2,128)} %get-tuple-element.101) | copy-start | bytes 49156

commit v4 on v3

--- a/solution.py
+++ b/solution.py
@@ -43,6 +43,10 @@
     return pl.ds(pl.multiple_of(idx * size, size), size)
 
 
+def loop(count, body):
+    lax.fori_loop(0, count, body, 0)
+
+
 def dma_sems(*shape):
     return pltpu.SemaphoreType.DMA(shape)
 
@@ -94,7 +98,7 @@
         sin_ref[span] = (big_sin * fine_cos[...] + big_cos * fine_sin[...]) * sign
         return carry
 
-    lax.fori_loop(0, height(cos_ref) // fine, body, 0)
+    loop(height(cos_ref) // fine, body)
 
 
 def rotate(values, cos_tab, sin_tab):
@@ -290,58 +294,18 @@
                 item.wait()
 
 
-def project_kernel(layer, first, x_ref, gain_ref, w_qkv_hbm, w_gate_hbm, w_up_hbm, *rest):
-    n_out = 4 if first else 3
-    n_tables = 4 if first else 2
-    tables, rest = rest[:n_tables], rest[n_tables:]
-    outs, rest = rest[:n_out], rest[n_out:]
-    if first:
-        u_ref, cos_out, sin_out, *rest = rest
-    stages, rest = rest[:n_out], rest[n_out:]
-    cos_ref, sin_ref, weights, full, send_sems, recv_sems, w_sems, out_sems = rest
-    rows = width_of(full)
-    half = rows // 2
-    gather = Gather(full, send_sems, recv_sems)
+def project_loads(layer, sources, weights, sems):
     loads, spans, start = [], [], 0
-    for idx, src in enumerate((w_qkv_hbm, w_gate_hbm, w_up_hbm)):
-        spans.append(slice(start, start + src.shape[2]))
-        start += src.shape[2]
-        loads.append(pltpu.make_async_copy(src.at[layer], weights.at[:, spans[-1]], w_sems.at[idx]))
-    if first:
-        keep_tables = [pltpu.make_async_copy(cos_ref, cos_out, w_sems.at[3]), pltpu.make_async_copy(sin_ref, sin_out, w_sems.at[4])]
-    else:
-        loads += [pltpu.make_async_copy(src, dst, w_sems.at[3 + idx]) for idx, (src, dst) in enumerate(zip(tables, (cos_ref, sin_ref)))]
-    writer = RowWriter(stages, outs, out_sems, rows)
-    if first:
-        norm_rows = min(ROWS_AT_ONCE, rows // SUBS)
-
-        def norm(idx, carry):
-            span = piece_at(idx, norm_rows)
-            normed = rms_scale(x_ref[span].astype(F32), gain_ref[layer:layer + 1]).astype(BF16)
-            full[gather.me, span] = normed
-            u_ref[span] = normed
-            return carry
-
-        for load in loads:
-            load.start()
-        meet(gather.peers())
-        per_piece = rows // SUBS // norm_rows
-        for sub in range(SUBS):
-            lax.fori_loop(sub * per_piece, (sub + 1) * per_piece, norm, 0)
-            gather.launch((sub,))
-        fill_rope(*tables, cos_ref, sin_ref)
-        for item in keep_tables:
-            item.start()
-    else:
-        own = pltpu.make_async_copy(x_ref, full.at[gather.me], w_sems.at[5])
-        own.start()
-        meet(gather.peers())
-        own.wait()
-        gather.launch()
-        for load in loads:
-            load.start()
-    for load in loads:
-        load.wait()
+    for idx, src in enumerate(sources):
+        spans.append(slice(start, start + src.shape[-1]))
+        start += src.shape[-1]
+        loads.append(pltpu.make_async_copy(src.at[layer], weights.at[:, spans[-1]], sems.at[idx]))
+    return loads, spans
+
+
+def project_steps(gather, weights, spans, stages, writer, cos_ref, sin_ref, with_hidden):
+    rows = width_of(gather.full)
+    half = rows // CORES
 
     def step_body(step, carry):
         run_at(step, gather.events())
@@ -349,7 +313,7 @@
         slot = step % BUFFERS
         writer.reuse(step)
         cos_tab, sin_tab = table_rows(cos_ref, places, half, rows), table_rows(sin_ref, places, half, rows)
-        product = dot(both_halves(full, places, half), weights[...]).astype(BF16)
+        product = dot(both_halves(gather.full, places, half), weights[...]).astype(BF16)
         qkv, gate, up = (product[:, span] for span in spans)
         for head in range(width_of(qkv) // HEAD_DIM):
             cols = slice(head * HEAD_DIM, (head + 1) * HEAD_DIM)
@@ -359,45 +323,73 @@
             stages[0][slot, :, cols] = part
         stages[1][slot] = gate
         stages[2][slot] = up
-        if first:
+        if with_hidden:
             stages[3][slot] = (jax.nn.silu(gate.astype(F32)) * up.astype(F32)).astype(BF16)
         writer.start(step, places)
         return carry
 
-    lax.fori_loop(0, N_DEVICES, step_body, 0)
+    loop(N_DEVICES, step_body)
     gather.finish()
     writer.finish()
-    if first:
-        for item in keep_tables:
-            item.wait()
-
-
-def project(source, norm_gain, w_qkv, w_gate, w_up, tables, layer, tp_size, first):
-    rows, width = source.shape
+
+
+def project_kernel(layer, x_ref, gain_ref, w_qkv_hbm, w_gate_hbm, w_up_hbm, *rest):
+    tables, rest = rest[:4], rest[4:]
+    outs, rest = rest[:4], rest[4:]
+    u_ref, cos_out, sin_out, *rest = rest
+    stages, rest = rest[:4], rest[4:]
+    cos_ref, sin_ref, weights, full, send_sems, recv_sems, w_sems, table_sems, out_sems = rest
+    rows = width_of(full)
+    gather = Gather(full, send_sems, recv_sems)
+    loads, spans = project_loads(layer, (w_qkv_hbm, w_gate_hbm, w_up_hbm), weights, w_sems)
+    keep_tables = [pltpu.make_async_copy(cos_ref, cos_out, table_sems.at[0]), pltpu.make_async_copy(sin_ref, sin_out, table_sems.at[1])]
+    norm_rows = min(ROWS_AT_ONCE, rows // SUBS)
+
+    def norm(idx, carry):
+        span = piece_at(idx, norm_rows)
+        normed = rms_scale(x_ref[span].astype(F32), gain_ref[layer:layer + 1]).astype(BF16)
+        full[gather.me, span] = normed
+        u_ref[span] = normed
+        return carry
+
+    for load in loads:
+        load.start()
+    meet(gather.peers())
+    per_piece = rows // SUBS // norm_rows
+    for sub in range(SUBS):
+        lax.fori_loop(sub * per_piece, (sub + 1) * per_piece, norm, 0)
+        gather.launch((sub,))
+    fill_rope(*tables, cos_ref, sin_ref)
+    for item in keep_tables:
+        item.start()
+    for load in loads:
+        load.wait()
+    project_steps(gather, weights, spans, stages, RowWriter(stages, outs, out_sems, rows), cos_ref, sin_ref, True)
+    for item in keep_tables:
+        item.wait()
+
+
+def project(x_loc, norm_gain, w_qkv, w_gate, w_up, tables, layer, tp_size):
+    rows, width = x_loc.shape
     seq_len = rows * tp_size
-    qkv_cols, ff_cols = w_qkv.shape[2], w_gate.shape[2]
-    out_cols = [qkv_cols, ff_cols, ff_cols] + ([ff_cols] if first else [])
-    total = qkv_cols + 2 * ff_cols
+    out_cols = [item.shape[-1] for item in (w_qkv, w_gate, w_up, w_up)]
+    table = (seq_len, HEAD_DIM)
     outs = [jax.ShapeDtypeStruct((seq_len, cols), BF16) for cols in out_cols]
-    out_specs = [ANY] * len(outs)
-    table = (seq_len, HEAD_DIM)
-    if first:
-        outs += [jax.ShapeDtypeStruct((rows, width), BF16)] + [jax.ShapeDtypeStruct(table, F32)] * 2
-        out_specs += [VMEM, ANY, ANY]
+    outs += [jax.ShapeDtypeStruct((rows, width), BF16)] + [jax.ShapeDtypeStruct(table, F32)] * 2
     scratch = [pltpu.VMEM((BUFFERS, rows, cols), BF16) for cols in out_cols]
     scratch += [pltpu.VMEM(table, F32)] * 2
-    scratch += [pltpu.VMEM((width, total), BF16)]
+    scratch += [pltpu.VMEM((width, sum(out_cols[:3])), BF16)]
     scratch += gather_scratch(tp_size, rows, width)
-    scratch += [dma_sems(6), pltpu.SemaphoreType.DMA((len(out_cols), 2, 2))]
+    scratch += [dma_sems(3), dma_sems(2), dma_sems(len(out_cols), BUFFERS, CORES)]
     return pl.pallas_call(
-        functools.partial(project_kernel, layer, first),
+        functools.partial(project_kernel, layer),
         out_shape=outs,
-        in_specs=[VMEM if first else ANY, VMEM] + [ANY] * 3 + [VMEM if first else ANY] * len(tables),
-        out_specs=out_specs,
+        in_specs=[VMEM] * 2 + [ANY] * 3 + [VMEM] * len(tables),
+        out_specs=[ANY] * len(out_cols) + [VMEM, ANY, ANY],
         scratch_shapes=scratch,
         compiler_params=params(collective_id=1 + layer),
         name=f'project_{layer}',
-    )(source, norm_gain, w_qkv, w_gate, w_up, *tables)
+    )(x_loc, norm_gain, w_qkv, w_gate, w_up, *tables)
 
 
 EACH = 4
@@ -407,7 +399,7 @@
 SLOTS = 6
 
 
-def scatter_blocks(peers, load, product, beside, tmp, acc, ring, pair_send, pair_recv, ring_send, ring_recv):
+def scatter_blocks(peers, load, early, product, beside, tmp, acc, ring, pair_send, pair_recv, ring_send, ring_recv):
     me, chip, core = ring_place()
     partner = device_at(chip, 1 - core)
     meet(peers or (partner, device_at(chip + 1, core), device_at(chip - 1, core)))
@@ -429,6 +421,7 @@
 
     def first_body(block, carry):
         load(block)
+        early(block)
 
         @pl.when(block >= SLOTS)
         def _():
@@ -444,7 +437,7 @@
 
         return carry
 
-    lax.fori_loop(0, PER_STEP, first_body, 0)
+    loop(PER_STEP, first_body)
 
     def pair_blocks(pair):
         step, rest = 1 + pair // EACH, pair % EACH
@@ -483,7 +476,7 @@
 
         return carry
 
-    lax.fori_loop(0, N_PAIRS + 1, body, 0)
+    loop(N_PAIRS + 1, body)
     for slot in range(SLOTS):
         to_partner(0, slot).wait_send()
     for block in range(N_BLOCKS - PER_STEP):
@@ -504,24 +497,20 @@
     ]
 
 
-def start_loads(w_load, row_loads_of):
+def start_loads(w_load, row_loads_of, later):
     order = [(block % WAYS) * EACH + block // WAYS for block in range(PER_STEP)]
-    for block, cols in enumerate(order):
-        for item in w_load(cols):
-            item.start()
-        if block < 2:
-            for item in row_loads_of[block]:
-                item.start()
-    for items in row_loads_of[2:]:
-        for item in items:
-            item.start()
+    needed = [w_load(cols) + (row_loads_of[idx] if idx < WAYS else []) for idx, cols in enumerate(order)]
+    for item in needed[0] + needed[1]:
+        item.start()
 
     def load(product):
-        for idx, cols in enumerate(order):
+        for idx in range(PER_STEP):
             @pl.when(product == idx)
             def _():
-                for item in w_load(cols) + (row_loads_of[idx] if idx < 2 else []):
+                for item in needed[idx]:
                     item.wait()
+                for item in (needed[idx + WAYS] if idx + WAYS < PER_STEP else []) + later.get(idx, []):
+                    item.start()
 
     return load
 
@@ -534,11 +523,21 @@
     return [load(order, hop) for order, hop in enumerate((3, 1, 2, 0))]
 
 
-def forward_kernel(layer, next_gain, o_hbm, m_hbm, w_out_hbm, w_down_hbm, x_ref, gain_ref, y_ref, u_ref, o_all, m_all, w_out, w_down, row_sems, w_sems, *scatter):
+def block_kernel(layer, qkv_hbm, m_hbm, w_out_hbm, w_down_hbm, x_ref, gain_ref, w_qkv_hbm, w_gate_hbm, w_up_hbm, cos_hbm, sin_hbm, *rest):
+    y_ref, u_ref, o_hbm, lse_hbm, *rest = rest
+    outs, rest = rest[:3], rest[3:]
+    stages, rest = rest[:3], rest[3:]
+    qkv, o_all, lse, m_all, w_out, w_down, weights, cos_ref, sin_ref, row_sems, w_sems, load_sems, out_sems = rest[:13]
+    (full, send_sems, recv_sems), scatter = rest[13:16], rest[16:]
     me, chip, core = ring_place()
     rows, width = x_ref.shape
     block_cols = width // PER_STEP
-    loads = row_loads(((o_hbm, o_all), (m_hbm, m_all)), row_sems, CORES * rows, chip)
+    loads = row_loads(((m_hbm, m_all),), row_sems, CORES * rows, chip)
+    gather = Gather(full, send_sems, recv_sems)
+    qkv_load = pltpu.make_async_copy(qkv_hbm, qkv, load_sems.at[3])
+    keeps = [pltpu.make_async_copy(o_all, o_hbm, load_sems.at[4]), pltpu.make_async_copy(lse, lse_hbm, load_sems.at[5])]
+    next_loads, spans = project_loads(layer + 1, (w_qkv_hbm, w_gate_hbm, w_up_hbm), weights, load_sems)
+    next_loads += [pltpu.make_async_copy(src, dst, load_sems.at[6 + idx]) for idx, (src, dst) in enumerate(((cos_hbm, cos_ref), (sin_hbm, sin_ref)))]
 
     def w_load(cols):
         span = pl.ds(cols * block_cols, block_cols)
@@ -547,15 +546,41 @@
             for idx, (src, dst) in enumerate(((w_out_hbm, w_out), (w_down_hbm, w_down)))
         ]
 
-    load_first = start_loads(w_load, loads)
+    qkv_load.start()
+    qkv_load.wait()
+    load_first = start_loads(w_load, loads, {4: loads[2], 6: loads[3]})
 
     def load(product):
         load_first(product)
-        for items, at in ((loads[2], PER_STEP), (loads[3], PER_STEP + 2 * EACH)):
+        for items, at in ((loads[2], PER_STEP), (loads[3], PER_STEP + WAYS * EACH)):
             @pl.when(product == at)
             def _():
                 for item in items:
                     item.wait()
+
+        @pl.when(product == PER_STEP)
+        def _():
+            for item in keeps + next_loads:
+                item.start()
+
+    def attend(index):
+        def head_rows(q_start):
+            def body(head, carry):
+                attend_rows(q_start, head, qkv, o_all, lse)
+                return carry
+
+            loop(width_of(o_all) // HEAD_DIM, body)
+
+        run_at(index, [functools.partial(head_rows, q_start) for q_start in range(0, height(qkv), Q_ROWS)])
+
+    def early(block):
+        turn = block - block // 4 * 2 - block // 6
+        dest = (chip + 3 + 2 * turn + turn // 2 * 3) % N_CHIPS
+        per_chip = CORES * rows // Q_ROWS
+
+        @pl.when((block == 0) | (block == 1) | (block == 4) | (block == 6))
+        def _():
+            lax.fori_loop(0, per_chip, lambda idx, carry: (attend(dest * per_chip + idx), carry)[1], 0)
 
     def product(dest, cols, n_cols, out):
         span = piece_at(dest, CORES * rows)
@@ -565,40 +590,58 @@
             for kind in range(CORES):
                 out[idx, kind] = total[kind * rows:(kind + 1) * rows, idx * block_cols:(idx + 1) * block_cols]
 
-    result = scatter_blocks(None, load, product, lambda pair: None, *scatter)
+    result = scatter_blocks(gather.peers(), load, early, product, lambda pair: None, *scatter)
+    norm_rows = min(ROWS_AT_ONCE, rows // SUBS)
 
     def finish(idx, carry):
-        span = piece_at(idx, ROWS_AT_ONCE)
+        span = piece_at(idx, norm_rows)
         summed = jnp.concatenate([result(cols)[span] for cols in range(PER_STEP)], axis=1)
         y = (x_ref[span].astype(F32) + summed).astype(BF16)
+        normed = rms_scale(y.astype(F32), gain_ref[layer + 1:layer + 2]).astype(BF16)
         y_ref[span] = y
-        u_ref[span] = rms_scale(y.astype(F32), gain_ref[next_gain:next_gain + 1]).astype(BF16)
+        u_ref[span] = normed
+        full[me, span] = normed
         return carry
 
-    lax.fori_loop(0, rows // ROWS_AT_ONCE, finish, 0)
-
-
-def block_output(attn_out, hidden, w_out, w_down, x_loc, norm_gain, layer):
+    per_piece = rows // SUBS // norm_rows
+    for sub in range(SUBS):
+        lax.fori_loop(sub * per_piece, (sub + 1) * per_piece, finish, 0)
+        gather.launch((sub,))
+    for item in next_loads:
+        item.wait()
+    project_steps(gather, weights, spans, stages, RowWriter(stages, outs, out_sems, rows), cos_ref, sin_ref, False)
+    for item in keeps:
+        item.wait()
+
+
+def block_rest(qkv, hidden, w_out, w_down, x_loc, norm_gain, w_qkv, w_gate, w_up, tables, layer, tp_size):
     rows, width = x_loc.shape
-    seq_len = height(attn_out)
+    seq_len = height(qkv)
     o_cols, ff_cols = width_of(w_out), width_of(w_down)
-    shard = jax.ShapeDtypeStruct((rows, width), BF16)
+    out_cols = [item.shape[-1] for item in (w_qkv, w_gate, w_up)]
+    outs = [((rows, width), BF16), ((rows, width), BF16), ((seq_len, o_cols), BF16), ((seq_len, o_cols), F32)]
+    outs += [((seq_len, cols), BF16) for cols in out_cols]
+    scratch = [pltpu.VMEM((BUFFERS, rows, cols), BF16) for cols in out_cols]
+    scratch += [
+        pltpu.VMEM(qkv.shape, BF16),
+        pltpu.VMEM((seq_len, o_cols), BF16),
+        pltpu.VMEM((seq_len, o_cols), F32),
+        pltpu.VMEM((seq_len, ff_cols), BF16),
+        pltpu.VMEM((o_cols, width), BF16),
+        pltpu.VMEM((ff_cols, width), BF16),
+        pltpu.VMEM((width, sum(out_cols)), BF16),
+    ]
+    scratch += [pltpu.VMEM(table.shape, F32) for table in tables]
+    scratch += [dma_sems(1, N_CHIPS), dma_sems(CORES, PER_STEP), dma_sems(8), dma_sems(len(out_cols), BUFFERS, CORES)]
     return pl.pallas_call(
-        functools.partial(forward_kernel, layer, layer + 1),
-        out_shape=[shard, shard],
-        in_specs=[ANY] * 4 + [VMEM] * 2,
-        out_specs=[VMEM] * 2,
-        scratch_shapes=[
-            pltpu.VMEM((seq_len, o_cols), BF16),
-            pltpu.VMEM((seq_len, ff_cols), BF16),
-            pltpu.VMEM((o_cols, width), BF16),
-            pltpu.VMEM((ff_cols, width), BF16),
-            dma_sems(2, N_CHIPS),
-            dma_sems(2, PER_STEP),
-        ] + scatter_scratch(rows, width),
+        functools.partial(block_kernel, layer),
+        out_shape=[jax.ShapeDtypeStruct(*item) for item in outs],
+        in_specs=[ANY] * 4 + [VMEM] * 2 + [ANY] * 5,
+        out_specs=[VMEM] * 2 + [ANY] * 5,
+        scratch_shapes=scratch + gather_scratch(tp_size, rows, width) + scatter_scratch(rows, width),
         compiler_params=params(collective_id=5 + layer),
-        name=f'block_output_{layer}',
-    )(attn_out, hidden, w_out, w_down, x_loc, norm_gain)
+        name=f'block_rest_{layer}',
+    )(qkv, hidden, w_out, w_down, x_loc, norm_gain, w_qkv, w_gate, w_up, *tables)
 
 
 GRAD_ROWS = N_PAIRS // 3
@@ -629,8 +672,7 @@
             for idx, (src, dst) in enumerate(zip((w_qkv_hbm, w_gate_hbm, w_up_hbm), weights))
         ]
 
-    load_first = start_loads(w_load, loads)
-    u_load.start()
+    load_first = start_loads(w_load, loads, {2: loads[2], 3: loads[3], 4: [u_load]})
 
     def load(product):
         load_first(product)
@@ -675,7 +717,7 @@
                 grad_out(which, part).start()
 
     peers = [(me + 1 + idx) % (N_DEVICES) for idx in range(N_DEVICES - 1)] if first_layer else None
-    result = scatter_blocks(peers, load, product, beside, *scatter)
+    result = scatter_blocks(peers, load, lambda block: None, product, beside, *scatter)
     gain_row = gain_ref[layer:layer + 1]
     dgain = gain_parts.at[me, layer:layer + 1] if first_layer else dgain_ref
     dgain[...] = jnp.zeros_like(dgain)
@@ -699,13 +741,17 @@
         dx_ref[span] = (dy_ref[span].astype(F32) + (scaled * inv_rms - x_f32 * mix)).astype(BF16)
         return carry
 
-    lax.fori_loop(0, rows // ROWS_AT_ONCE, gain_rows, 0)
+    def both_rows(idx, carry):
+        gain_rows(idx, carry)
+        return input_rows(idx, carry)
+
     if first_layer:
+        loop(rows // ROWS_AT_ONCE, gain_rows)
         gain_parts[me, 1:] = later_gains_ref[...]
         copies = [remote_copy(gain_parts.at[me], gain_parts.at[me], gain_send.at[idx], gain_recv.at[me], peer) for idx, peer in enumerate(peers)]
         for item in copies:
             item.start()
-    lax.fori_loop(0, rows // ROWS_AT_ONCE, input_rows, 0)
+    loop(rows // ROWS_AT_ONCE, input_rows if first_layer else both_rows)
     if first_layer:
         for idx, peer in enumerate(peers):
             remote_copy(gain_parts.at[peer], gain_parts.at[peer], gain_send.at[idx], gain_recv.at[peer], peer).wait_recv()
@@ -818,7 +864,7 @@
             item.start()
         return carry
 
-    lax.fori_loop(0, steps, body, 0)
+    loop(steps, body)
     for step in range(steps - COLLECT_SLOTS, steps):
         for item in moves_of(step, True):
             item.wait()
@@ -903,25 +949,6 @@
     dkt_acc[head, :, seen] += dot_tn(query, ds_tmp[:, seen])
     d_query = dot(ds_tmp[:, seen], qkv_ref[seen, head_cols(head, 1, 3)]).astype(BF16)
     dq_ref[span, head_cols(head, 0, 3)] = rotate(d_query.astype(F32), cos_ref[span], -sin_ref[span]).astype(BF16)
-
-
-def attention_kernel(qkv_ref, o_ref, lse_ref):
-    for q_start in range(0, height(qkv_ref), Q_ROWS):
-        attend_rows(q_start, 0, qkv_ref, o_ref, lse_ref)
-
-
-def attention(qkv):
-    seq_len, cols = qkv.shape
-    heads = cols // (3 * HEAD_DIM)
-    return pl.pallas_call(
-        attention_kernel,
-        grid=(heads,),
-        out_shape=[jax.ShapeDtypeStruct((seq_len, heads * HEAD_DIM), BF16), jax.ShapeDtypeStruct((seq_len, heads * HEAD_DIM), F32)],
-        in_specs=[pl.BlockSpec((seq_len, 3 * HEAD_DIM), lambda h: (0, h))],
-        out_specs=[pl.BlockSpec((seq_len, HEAD_DIM), lambda h: (0, h))] * 2,
-        compiler_params=params(semantics=('arbitrary',)),
-        name='attention',
-    )(qkv)
 
 
 def middle_kernel(layer, with_forward, dy_hbm, u_hbm, w_out_hbm, w_down_hbm, gate_hbm, up_hbm, cos_hbm, sin_hbm, qkv_hbm, *rest):
@@ -969,7 +996,7 @@
             function(q_start, head, *args)
             return carry
 
-        lax.fori_loop(0, n_heads, body, 0)
+        loop(n_heads, body)
 
     def attend(index):
         run_at(index, [functools.partial(both_heads, attend_rows, q_start, qkv, o_all, lse) for q_start in range(0, seq_len, Q_ROWS)])
@@ -987,7 +1014,7 @@
                 dqkv[span, head_cols(head, 2, 3)] = dv_acc[head, :, span].T.astype(BF16)
             return carry
 
-        lax.fori_loop(0, seq_len // Q_ROWS, body, 0)
+        loop(seq_len // Q_ROWS, body)
         keep_dqkv.start()
 
     keep_dqkv = pltpu.make_async_copy(dqkv, dqkv_hbm, dqkv_sem)
@@ -1068,9 +1095,9 @@
         pltpu.make_async_copy(u_full.at[shard], u_full_hbm.at[shard], u_sems.at[shard]).start()
 
     if with_forward:
-        lax.fori_loop(0, N_DEVICES, dy_step_forward, 0)
+        loop(N_DEVICES, dy_step_forward)
     else:
-        lax.fori_loop(0, N_DEVICES + 5, dy_step_backward, 0)
+        loop(N_DEVICES + 5, dy_step_backward)
 
     def grad_copies(step):
         slot = step % BUFFERS
@@ -1121,7 +1148,7 @@
         keeps += [pltpu.make_async_copy(dy_full, dy_full_hbm, grad_sems.at[1, 0])]
         for item in keeps:
             item.start()
-    lax.fori_loop(0, N_DEVICES, u_step, 0)
+    loop(N_DEVICES, u_step)
     if with_forward:
         finish_keys_values()
     for shard in (u_gather.partner, u_gather.first_other, u_gather.second_other):
@@ -1200,19 +1227,10 @@
         n_layers = height(w_qkv)
         seq_len = height(x_loc) * tp_size
         tables = tuple(jnp.asarray(table) for table in rope_tables(seq_len, FINE))
-        x_cur, source = x_loc, x_loc
-        saved = []
-        for layer in range(n_layers):
-            first, last = layer == 0, layer == n_layers - 1
-            qkv, gate_act, up_act, *more = project(source, norm_gain, w_qkv, w_gate, w_up, tables, layer, tp_size, first)
-            u_loc = more[1] if first else source
-            tables = more[2:] if first else tables
-            if last:
-                saved.append((x_cur, u_loc, qkv, gate_act, up_act, ()))
-            else:
-                attended = attention(qkv)
-                saved.append((x_cur, u_loc, qkv, gate_act, up_act, tuple(attended)))
-                x_cur, source = block_output(attended[0], more[0], w_out, w_down, x_cur, norm_gain, layer)
+        assert n_layers == 2
+        qkv, gate_act, up_act, hidden, u_loc, *tables = project(x_loc, norm_gain, w_qkv, w_gate, w_up, tables, 0, tp_size)
+        y_loc, u_next, attn_out, lse, *projected = block_rest(qkv, hidden, w_out, w_down, x_loc, norm_gain, w_qkv, w_gate, w_up, tables, 0, tp_size)
+        saved = ((x_loc, u_loc, qkv, gate_act, up_act, (attn_out, lse)), (y_loc, u_next, *projected, ()))
         grad_cur = dy_loc
         grads, gains = [None] * n_layers, ()
         for layer in reversed(range(n_layers)):

time: 551 us -> 541 us (0.982)
  Pallas kernels: 541 us -> 531 us
    pallas_call x4 -> x2, Pallas kernels: 189 us -> 183 us  [the longest x1 132 us: block_rest(): pl.pallas_call(functools.partial(block_kernel, layer), out_shape=[jax.Sha...]
where the time goes in v4:
time: 541 us; the launch traced here: 533 us
  Pallas kernels  531 us (98%)
    pallas_call x2, Pallas kernels, block_input_backward(): pl.pallas_call(functools.partial(backward_kernel, layer), out_shape=out_s...  163 us
    pallas_call x2, Pallas kernels, middle(): pl.pallas_call(functools.partial(middle_kernel, layer, not attended), out...  157 us
    pallas_call x1, Pallas kernels, block_rest(): pl.pallas_call(functools.partial(block_kernel, layer), out_shape=[jax.Sha...  132 us
    pallas_call x1, Pallas kernels, project(): pl.pallas_call(functools.partial(project_kernel, layer), out_shape=outs,...  50.6 us
    pallas_call x1, Pallas kernels, collect(): pl.pallas_call(functools.partial(collect_kernel, moves, steps), out_shape...  27.7 us

profile of v4, /device:TPU:81, one launch (start us, length us, event | category | flops | bytes accessed | tf_op | source)
XLA Modules:
  0.0 532.8 jit_solution(11524148906698695391)
XLA Ops:
  0.6 50.6 %project_0.1 = (bf16[2048,768]{1,0:T(8,128)(2,1)}, bf16[2048,1024]{1,0:T(8,128)(2,1)}, bf16[2048,1024]{1,0:T(8,128)(2,1)}, bf16[2048,1024]{1,0:T(8,128)(2,1)}, b...) custom-call(bf16[256,2048]{1,0:T(8,128)(2,1)} %x_ref.5, f32[2,2048]{1,0:T(2,128)} %gain_ref.7, ...), custom_call_target="tpu_custom_call" | custom-call | tf_op jit(solution)/shard_map/project_0/pallas_call | solution.py:384
  51.2 132.1 %block_rest_0.1 = (bf16[256,2048]{1,0:T(8,128)(2,1)}, bf16[256,2048]{1,0:T(8,128)(2,1)}, bf16[2048,256]{1,0:T(8,128)(2,1)}, f32[2048,256]{1,0:T(8,128)}, bf16[20...) custom-call(bf16[2048,768]{1,0:T(8,128)(2,1)} %get-tuple-element.50.qkv_hbm, ...), custom_call_target="tpu_custom_call" | custom-call | tf_op jit(solution)/shard_map/block_rest_0/pallas_call | solution.py:636
  183.3 77.5 %middle_1.1 = (bf16[2048,1024]{1,0:T(8,128)(2,1)}, bf16[2048,1024]{1,0:T(8,128)(2,1)}, bf16[2048,768]{1,0:T(8,128)(2,1)}, bf16[8,256,2048]{2,1,0:T(8,128)(2,1)},...) custom-call(bf16[256,2048]{1,0:T(8,128)(2,1)} %dy_ref.1, ...), custom_call_target="tpu_custom_call" | custom-call | tf_op jit(solution)/shard_map/middle_1/pallas_call | solution.py:1208
  260.8 78.6 %block_input_backward_1.1 = (bf16[256,2048]{1,0:T(8,128)(2,1)}, f32[1,2048]{1,0:T(1,128)}, bf16[2048,768]{1,0:T(8,128)(2,1)}, bf16[2048,1024]{1,0:T(8,128)(2,1)}, bf16[2048,1024]{1,0:T(8,128)(2,1)}) custom-call(bf16[2048,768]{1,0:T(8,128)(2,1)} %get-tuple-element.61.dqkv_hbm, bf16[2048,1024]{1,0:T(8,128)(2,1)} %get-tuple-element.62.dgate_hbm, ...), custom_call_target="tpu_custom_call" | custom-call | tf_op jit(solution)/shard_map/block_input_backward_1/pallas_call | solution.py:782
  339.4 79.9 %middle_0.1 = (bf16[2048,1024]{1,0:T(8,128)(2,1)}, bf16[2048,1024]{1,0:T(8,128)(2,1)}, bf16[2048,768]{1,0:T(8,128)(2,1)}, bf16[8,256,2048]{2,1,0:T(8,128)(2,1)},...) custom-call(bf16[256,2048]{1,0:T(8,128)(2,1)} %get-tuple-element.66.dy_hbm.dy_ref, ...), custom_call_target="tpu_custom_call" | custom-call | tf_op jit(solution)/shard_map/middle_0/pallas_call | solution.py:1208
  419.4 84.7 %block_input_backward_0.1 = (bf16[256,2048]{1,0:T(8,128)(2,1)}, f32[2,2048]{1,0:T(2,128)}, bf16[2048,768]{1,0:T(8,128)(2,1)}, bf16[2048,1024]{1,0:T(8,128)(2,1)}, bf16[2048,1024]{1,0:T(8,128)(2,1)}) custom-call(bf16[2048,768]{1,0:T(8,128)(2,1)} %get-tuple-element.72.dqkv_hbm, bf16[2048,1024]{1,0:T(8,128)(2,1)} %get-tuple-element.73.dgate_hbm, ...), custom_call_target="tpu_custom_call" | custom-call | tf_op jit(solution)/shard_map/block_input_backward_0/pallas_call | solution.py:782
  504.1 0.0 copy-start
  504.1 27.7 %collect.1 = (bf16[256,2048]{1,0:T(8,128)(2,1)}, bf16[2,256,2048]{2,1,0:T(8,128)(2,1)}, bf16[2,1024,2048]{2,1,0:T(8,128)(2,1)}, bf16[2,2048,768]{2,1,0:T(8,128)(...) custom-call(bf16[2048,2048]{1,0:T(8,128)(2,1)} %bitcast.4, ...), custom_call_target="tpu_custom_call" | custom-call | tf_op jit(solution)/shard_map/collect/pallas_call | solution.py:894
  531.8 0.0 copy-done
  531.8 0.6 copy.20
Async XLA Ops:
  504.1 27.7 %copy-start = (f32[2,2048]{1,0:T(2,128)S(1)}, f32[2,2048]{1,0:T(2,128)}, u32[]{:S(2)}) copy-start(f32[2,2048]{1,0:T(2,128)} %get-tuple-element.101) | copy-start | bytes 49156

commit v5 on v4

--- a/solution.py
+++ b/solution.py
@@ -336,20 +336,22 @@
 def project_kernel(layer, x_ref, gain_ref, w_qkv_hbm, w_gate_hbm, w_up_hbm, *rest):
     tables, rest = rest[:4], rest[4:]
     outs, rest = rest[:4], rest[4:]
-    u_ref, cos_out, sin_out, *rest = rest
+    u_hbm, cos_out, sin_out, *rest = rest
     stages, rest = rest[:4], rest[4:]
-    cos_ref, sin_ref, weights, full, send_sems, recv_sems, w_sems, table_sems, out_sems = rest
+    cos_ref, sin_ref, weights, full, send_sems, recv_sems, w_sems, keep_sems, out_sems = rest
     rows = width_of(full)
     gather = Gather(full, send_sems, recv_sems)
     loads, spans = project_loads(layer, (w_qkv_hbm, w_gate_hbm, w_up_hbm), weights, w_sems)
-    keep_tables = [pltpu.make_async_copy(cos_ref, cos_out, table_sems.at[0]), pltpu.make_async_copy(sin_ref, sin_out, table_sems.at[1])]
+    keeps = [
+        pltpu.make_async_copy(src, dst, keep_sems.at[idx])
+        for idx, (src, dst) in enumerate(((cos_ref, cos_out), (sin_ref, sin_out), (full.at[gather.me], u_hbm)))
+    ]
     norm_rows = min(ROWS_AT_ONCE, rows // SUBS)
 
     def norm(idx, carry):
         span = piece_at(idx, norm_rows)
         normed = rms_scale(x_ref[span].astype(F32), gain_ref[layer:layer + 1]).astype(BF16)
         full[gather.me, span] = normed
-        u_ref[span] = normed
         return carry
 
     for load in loads:
@@ -360,12 +362,12 @@
         lax.fori_loop(sub * per_piece, (sub + 1) * per_piece, norm, 0)
         gather.launch((sub,))
     fill_rope(*tables, cos_ref, sin_ref)
-    for item in keep_tables:
+    for item in keeps:
         item.start()
     for load in loads:
         load.wait()
     project_steps(gather, weights, spans, stages, RowWriter(stages, outs, out_sems, rows), cos_ref, sin_ref, True)
-    for item in keep_tables:
+    for item in keeps:
         item.wait()
 
 
@@ -380,12 +382,12 @@
     scratch += [pltpu.VMEM(table, F32)] * 2
     scratch += [pltpu.VMEM((width, sum(out_cols[:3])), BF16)]
     scratch += gather_scratch(tp_size, rows, width)
-    scratch += [dma_sems(3), dma_sems(2), dma_sems(len(out_cols), BUFFERS, CORES)]
+    scratch += [dma_sems(3), dma_sems(3), dma_sems(len(out_cols), BUFFERS, CORES)]
     return pl.pallas_call(
         functools.partial(project_kernel, layer),
         out_shape=outs,
         in_specs=[VMEM] * 2 + [ANY] * 3 + [VMEM] * len(tables),
-        out_specs=[ANY] * len(out_cols) + [VMEM, ANY, ANY],
+        out_specs=[ANY] * len(outs),
         scratch_shapes=scratch,
         compiler_params=params(collective_id=1 + layer),
         name=f'project_{layer}',
@@ -523,21 +525,24 @@
     return [load(order, hop) for order, hop in enumerate((3, 1, 2, 0))]
 
 
-def block_kernel(layer, qkv_hbm, m_hbm, w_out_hbm, w_down_hbm, x_ref, gain_ref, w_qkv_hbm, w_gate_hbm, w_up_hbm, cos_hbm, sin_hbm, *rest):
-    y_ref, u_ref, o_hbm, lse_hbm, *rest = rest
+def block_kernel(layer, qkv_hbm, m_hbm, w_out_hbm, w_down_hbm, x_hbm, gain_ref, w_qkv_hbm, w_gate_hbm, w_up_hbm, cos_hbm, sin_hbm, *rest):
+    y_hbm, u_hbm, o_hbm, lse_hbm, *rest = rest
     outs, rest = rest[:3], rest[3:]
-    stages, rest = rest[:3], rest[3:]
+    stages, (x_ref, y_ref, *rest) = rest[:3], rest[3:]
     qkv, o_all, lse, m_all, w_out, w_down, weights, cos_ref, sin_ref, row_sems, w_sems, load_sems, out_sems = rest[:13]
     (full, send_sems, recv_sems), scatter = rest[13:16], rest[16:]
     me, chip, core = ring_place()
-    rows, width = x_ref.shape
+    rows, width = x_hbm.shape
     block_cols = width // PER_STEP
     loads = row_loads(((m_hbm, m_all),), row_sems, CORES * rows, chip)
     gather = Gather(full, send_sems, recv_sems)
-    qkv_load = pltpu.make_async_copy(qkv_hbm, qkv, load_sems.at[3])
-    keeps = [pltpu.make_async_copy(o_all, o_hbm, load_sems.at[4]), pltpu.make_async_copy(lse, lse_hbm, load_sems.at[5])]
+    qkv_load, x_load, *keeps = [
+        pltpu.make_async_copy(src, dst, load_sems.at[3 + idx])
+        for idx, (src, dst) in enumerate(((qkv_hbm, qkv), (x_hbm, x_ref), (o_all, o_hbm), (lse, lse_hbm), (y_ref, y_hbm), (full.at[me], u_hbm)))
+    ]
+    keeps, keeps_after = keeps[:2], keeps[2:]
     next_loads, spans = project_loads(layer + 1, (w_qkv_hbm, w_gate_hbm, w_up_hbm), weights, load_sems)
-    next_loads += [pltpu.make_async_copy(src, dst, load_sems.at[6 + idx]) for idx, (src, dst) in enumerate(((cos_hbm, cos_ref), (sin_hbm, sin_ref)))]
+    next_loads += [pltpu.make_async_copy(src, dst, load_sems.at[9 + idx]) for idx, (src, dst) in enumerate(((cos_hbm, cos_ref), (sin_hbm, sin_ref)))]
 
     def w_load(cols):
         span = pl.ds(cols * block_cols, block_cols)
@@ -560,7 +565,7 @@
 
         @pl.when(product == PER_STEP)
         def _():
-            for item in keeps + next_loads:
+            for item in [x_load] + keeps + next_loads:
                 item.start()
 
     def attend(index):
@@ -580,7 +585,11 @@
 
         @pl.when((block == 0) | (block == 1) | (block == 4) | (block == 6))
         def _():
-            lax.fori_loop(0, per_chip, lambda idx, carry: (attend(dest * per_chip + idx), carry)[1], 0)
+            def body(idx, carry):
+                attend(dest * per_chip + idx)
+                return carry
+
+            loop(per_chip, body)
 
     def product(dest, cols, n_cols, out):
         span = piece_at(dest, CORES * rows)
@@ -592,6 +601,7 @@
 
     result = scatter_blocks(gather.peers(), load, early, product, lambda pair: None, *scatter)
     norm_rows = min(ROWS_AT_ONCE, rows // SUBS)
+    x_load.wait()
 
     def finish(idx, carry):
         span = piece_at(idx, norm_rows)
@@ -599,7 +609,6 @@
         y = (x_ref[span].astype(F32) + summed).astype(BF16)
         normed = rms_scale(y.astype(F32), gain_ref[layer + 1:layer + 2]).astype(BF16)
         y_ref[span] = y
-        u_ref[span] = normed
         full[me, span] = normed
         return carry
 
@@ -607,10 +616,12 @@
     for sub in range(SUBS):
         lax.fori_loop(sub * per_piece, (sub + 1) * per_piece, finish, 0)
         gather.launch((sub,))
+    for item in keeps_after:
+        item.start()
     for item in next_loads:
         item.wait()
     project_steps(gather, weights, spans, stages, RowWriter(stages, outs, out_sems, rows), cos_ref, sin_ref, False)
-    for item in keeps:
+    for item in keeps + keeps_after:
         item.wait()
 
 
@@ -622,6 +633,7 @@
     outs = [((rows, width), BF16), ((rows, width), BF16), ((seq_len, o_cols), BF16), ((seq_len, o_cols), F32)]
     outs += [((seq_len, cols), BF16) for cols in out_cols]
     scratch = [pltpu.VMEM((BUFFERS, rows, cols), BF16) for cols in out_cols]
+    scratch += [pltpu.VMEM((rows, width), BF16)] * 2
     scratch += [
         pltpu.VMEM(qkv.shape, BF16),
         pltpu.VMEM((seq_len, o_cols), BF16),
@@ -632,12 +644,12 @@
         pltpu.VMEM((width, sum(out_cols)), BF16),
     ]
     scratch += [pltpu.VMEM(table.shape, F32) for table in tables]
-    scratch += [dma_sems(1, N_CHIPS), dma_sems(CORES, PER_STEP), dma_sems(8), dma_sems(len(out_cols), BUFFERS, CORES)]
+    scratch += [dma_sems(1, N_CHIPS), dma_sems(CORES, PER_STEP), dma_sems(11), dma_sems(len(out_cols), BUFFERS, CORES)]
     return pl.pallas_call(
         functools.partial(block_kernel, layer),
         out_shape=[jax.ShapeDtypeStruct(*item) for item in outs],
-        in_specs=[ANY] * 4 + [VMEM] * 2 + [ANY] * 5,
-        out_specs=[VMEM] * 2 + [ANY] * 5,
+        in_specs=[ANY] * 5 + [VMEM] + [ANY] * 5,
+        out_specs=[ANY] * len(outs),
         scratch_shapes=scratch + gather_scratch(tp_size, rows, width) + scatter_scratch(rows, width),
         compiler_params=params(collective_id=5 + layer),
         name=f'block_rest_{layer}',
@@ -647,7 +659,7 @@
 GRAD_ROWS = N_PAIRS // 3
 
 
-def backward_kernel(layer, dqkv_hbm, dgate_hbm, dup_hbm, w_qkv_hbm, w_gate_hbm, w_up_hbm, u_hbm, x_ref, dy_ref, gain_ref, *rest):
+def backward_kernel(layer, dqkv_hbm, dgate_hbm, dup_hbm, w_qkv_hbm, w_gate_hbm, w_up_hbm, u_hbm, x_hbm, dy_hbm, gain_ref, *rest):
     first_layer = layer == 0
     if first_layer:
         later_gains_ref, *rest = rest
@@ -655,15 +667,16 @@
     grads, rest = rest[:3], rest[3:]
     acts, rest = rest[:3], rest[3:]
     weights, rest = rest[:3], rest[3:]
-    u_all, stage, row_sems, w_sems, u_sem, stage_sems, *rest = rest
+    u_all, x_ref, dy_ref, stage, row_sems, w_sems, u_sem, x_sem, dy_sem, stage_sems, *rest = rest
     if first_layer:
         gain_parts, gain_send, gain_recv, *rest = rest
     scatter = rest
     me, chip, core = ring_place()
-    rows, width = x_ref.shape
+    rows, width = x_hbm.shape
     block_cols = width // PER_STEP
     loads = row_loads(list(zip((dqkv_hbm, dgate_hbm, dup_hbm), acts)), row_sems, CORES * rows, chip)
     u_load = pltpu.make_async_copy(u_hbm, u_all, u_sem)
+    x_loads = [pltpu.make_async_copy(x_hbm, x_ref, x_sem), pltpu.make_async_copy(dy_hbm, dy_ref, dy_sem)]
 
     def w_load(cols):
         span = pl.ds(cols * block_cols, block_cols)
@@ -672,14 +685,14 @@
             for idx, (src, dst) in enumerate(zip((w_qkv_hbm, w_gate_hbm, w_up_hbm), weights))
         ]
 
-    load_first = start_loads(w_load, loads, {2: loads[2], 3: loads[3], 4: [u_load]})
+    load_first = start_loads(w_load, loads, {2: loads[2], 3: loads[3], 4: [u_load] + x_loads})
 
     def load(product):
         load_first(product)
 
         @pl.when(product == PER_STEP)
         def _():
-            for item in loads[2] + loads[3] + [u_load]:
+            for item in loads[2] + loads[3] + [u_load] + x_loads:
                 item.wait()
 
     def product(dest, cols, n_cols, out):
@@ -775,14 +788,14 @@
     out_shape += [jax.ShapeDtypeStruct((width, cols), BF16) for cols in all_cols]
     scratch = [pltpu.VMEM((seq_len, cols), BF16) for cols in all_cols]
     scratch += [pltpu.VMEM((width, cols), BF16) for cols in all_cols]
-    scratch += [pltpu.VMEM((seq_len, width), BF16), pltpu.VMEM((2, width // GRAD_ROWS, max(all_cols)), BF16)]
-    scratch += [dma_sems(3, N_CHIPS), dma_sems(3, PER_STEP), pltpu.SemaphoreType.DMA, dma_sems(2)]
+    scratch += [pltpu.VMEM((seq_len, width), BF16)] + [pltpu.VMEM((rows, width), BF16)] * 2 + [pltpu.VMEM((BUFFERS, width // GRAD_ROWS, max(all_cols)), BF16)]
+    scratch += [dma_sems(3, N_CHIPS), dma_sems(3, PER_STEP)] + [pltpu.SemaphoreType.DMA] * 3 + [dma_sems(BUFFERS)]
     if first_layer:
         scratch += [pltpu.VMEM((N_DEVICES, n_layers, width), F32), dma_sems(N_DEVICES - 1), dma_sems(N_DEVICES)]
     return pl.pallas_call(
         functools.partial(backward_kernel, layer),
         out_shape=out_shape,
-        in_specs=[ANY] * 7 + [VMEM] * (4 if first_layer else 3),
+        in_specs=[ANY] * 9 + [VMEM] * (2 if first_layer else 1),
         out_specs=[VMEM] * 2 + [ANY] * 3,
         scratch_shapes=scratch + scatter_scratch(rows, width),
         compiler_params=params(collective_id=7 + layer),
@@ -790,7 +803,7 @@
     )(d_qkv, d_gate, d_up, w_qkv, w_gate, w_up, u_full, x_loc, dy_loc, norm_gain, *((later_gains,) if first_layer else ()))
 
 
-COLLECT_SLOTS = 3
+COLLECT_SLOTS = 4
 
 
 def collect_kernel(moves, steps, dy_hbm, attn_hbm, hidden_hbm, *refs):
@@ -827,7 +840,7 @@
         )
 
     whole = [pltpu.make_async_copy(attn_hbm, attn_out, whole_sems.at[0]), pltpu.make_async_copy(hidden_hbm, hidden, whole_sems.at[1])]
-    for item in moves_of(0, False) + whole + [dy_load(0)] + moves_of(1, False):
+    for item in moves_of(0, False) + whole + [dy_load(0)] + moves_of(1, False) + moves_of(2, False):
         item.start()
     for step in range(1, steps):
         dy_load(step).start()
@@ -835,14 +848,14 @@
         item.wait()
 
     def body(step, carry):
-        @pl.when((step >= 1) & (step + 2 <= steps))
-        def _():
-            @pl.when(step >= COLLECT_SLOTS - 1)
+        @pl.when((step >= 1) & (step + 2 < steps))
+        def _():
+            @pl.when(step >= BUFFERS)
             def _():
-                for item in moves_of(step + 1 - COLLECT_SLOTS, True):
+                for item in moves_of(step - BUFFERS, True):
                     item.wait()
 
-            for item in moves_of(step + 1, False):
+            for item in moves_of(step + 2, False):
                 item.start()
 
         for item in moves_of(step, False):

time: 541 us -> 537 us (level)
  no operation moved by 1% of the time
where the time goes in v5:
time: 537 us; the launch traced here: 528 us
  Pallas kernels  526 us (98%)
    pallas_call x2, Pallas kernels, block_input_backward(): pl.pallas_call(functools.partial(backward_kernel, layer), out_shape=out_s...  162 us
    pallas_call x2, Pallas kernels, middle(): pl.pallas_call(functools.partial(middle_kernel, layer, not attended), out...  157 us
    pallas_call x1, Pallas kernels, block_rest(): pl.pallas_call(functools.partial(block_kernel, layer), out_shape=[jax.Sha...  130 us
    pallas_call x1, Pallas kernels, project(): pl.pallas_call(functools.partial(project_kernel, layer), out_shape=outs,...  49.6 us
    pallas_call x1, Pallas kernels, collect(): pl.pallas_call(functools.partial(collect_kernel, moves, steps), out_shape...  27.3 us

profile of v5, /device:TPU:81, one launch (start us, length us, event | category | flops | bytes accessed | tf_op | source)
XLA Modules:
  0.0 528.1 jit_solution(9726105230512775016)
XLA Ops:
  0.6 49.6 %project_0.1 = (bf16[2048,768]{1,0:T(8,128)(2,1)}, bf16[2048,1024]{1,0:T(8,128)(2,1)}, bf16[2048,1024]{1,0:T(8,128)(2,1)}, bf16[2048,1024]{1,0:T(8,128)(2,1)}, b...) custom-call(bf16[256,2048]{1,0:T(8,128)(2,1)} %x_hbm.3, f32[2,2048]{1,0:T(2,128)} %gain_ref.7, ...), custom_call_target="tpu_custom_call" | custom-call | tf_op jit(solution)/shard_map/project_0/pallas_call | solution.py:386
  50.2 130.3 %block_rest_0.1 = (bf16[256,2048]{1,0:T(8,128)(2,1)}, bf16[256,2048]{1,0:T(8,128)(2,1)}, bf16[2048,256]{1,0:T(8,128)(2,1)}, f32[2048,256]{1,0:T(8,128)}, bf16[20...) custom-call(bf16[2048,768]{1,0:T(8,128)(2,1)} %get-tuple-element.50.qkv_hbm, ...), custom_call_target="tpu_custom_call" | custom-call | tf_op jit(solution)/shard_map/block_rest_0/pallas_call | solution.py:648
  180.5 77.5 %middle_1.1 = (bf16[2048,1024]{1,0:T(8,128)(2,1)}, bf16[2048,1024]{1,0:T(8,128)(2,1)}, bf16[2048,768]{1,0:T(8,128)(2,1)}, bf16[8,256,2048]{2,1,0:T(8,128)(2,1)},...) custom-call(bf16[256,2048]{1,0:T(8,128)(2,1)} %dy_hbm.3, ...), custom_call_target="tpu_custom_call" | custom-call | tf_op jit(solution)/shard_map/middle_1/pallas_call | solution.py:1221
  258.1 77.8 %block_input_backward_1.1 = (bf16[256,2048]{1,0:T(8,128)(2,1)}, f32[1,2048]{1,0:T(1,128)}, bf16[2048,768]{1,0:T(8,128)(2,1)}, bf16[2048,1024]{1,0:T(8,128)(2,1)}, bf16[2048,1024]{1,0:T(8,128)(2,1)}) custom-call(bf16[2048,768]{1,0:T(8,128)(2,1)} %get-tuple-element.61.dqkv_hbm, bf16[2048,1024]{1,0:T(8,128)(2,1)} %get-tuple-element.62.dgate_hbm, ...), custom_call_target="tpu_custom_call" | custom-call | tf_op jit(solution)/shard_map/block_input_backward_1/pallas_call | solution.py:795
  335.8 79.9 %middle_0.1 = (bf16[2048,1024]{1,0:T(8,128)(2,1)}, bf16[2048,1024]{1,0:T(8,128)(2,1)}, bf16[2048,768]{1,0:T(8,128)(2,1)}, bf16[8,256,2048]{2,1,0:T(8,128)(2,1)},...) custom-call(bf16[256,2048]{1,0:T(8,128)(2,1)} %get-tuple-element.66.dy_hbm, ...), custom_call_target="tpu_custom_call" | custom-call | tf_op jit(solution)/shard_map/middle_0/pallas_call | solution.py:1221
  415.8 83.9 %block_input_backward_0.1 = (bf16[256,2048]{1,0:T(8,128)(2,1)}, f32[2,2048]{1,0:T(2,128)}, bf16[2048,768]{1,0:T(8,128)(2,1)}, bf16[2048,1024]{1,0:T(8,128)(2,1)}, bf16[2048,1024]{1,0:T(8,128)(2,1)}) custom-call(bf16[2048,768]{1,0:T(8,128)(2,1)} %get-tuple-element.72.dqkv_hbm, bf16[2048,1024]{1,0:T(8,128)(2,1)} %get-tuple-element.73.dgate_hbm, ...), custom_call_target="tpu_custom_call" | custom-call | tf_op jit(solution)/shard_map/block_input_backward_0/pallas_call | solution.py:795
  499.7 0.0 copy-start
  499.7 27.3 %collect.1 = (bf16[256,2048]{1,0:T(8,128)(2,1)}, bf16[2,256,2048]{2,1,0:T(8,128)(2,1)}, bf16[2,1024,2048]{2,1,0:T(8,128)(2,1)}, bf16[2,2048,768]{2,1,0:T(8,128)(...) custom-call(bf16[2048,2048]{1,0:T(8,128)(2,1)} %bitcast.4, ...), custom_call_target="tpu_custom_call" | custom-call | tf_op jit(solution)/shard_map/collect/pallas_call | solution.py:907
  527.0 0.0 copy-done
  527.0 0.6 copy.20
Async XLA Ops:
  499.7 27.3 %copy-start = (f32[2,2048]{1,0:T(2,128)S(1)}, f32[2,2048]{1,0:T(2,128)}, u32[]{:S(2)}) copy-start(f32[2,2048]{1,0:T(2,128)} %get-tuple-element.101) | copy-start | bytes 49156

commit v6 on v5

--- a/solution.py
+++ b/solution.py
@@ -21,7 +21,7 @@
 BUFFERS = 2
 SUBS = 4
 Q_ROWS = 256
-ROWS_AT_ONCE = 32
+ROWS_AT_ONCE = 64
 FINE = 128
 BF16 = jnp.bfloat16
 F32 = jnp.float32

time: 537 us -> 536 us (level)
  no operation moved by 1% of the time
where the time goes in v6:
time: 536 us; the launch traced here: 527 us
  Pallas kernels  526 us (98%)
    pallas_call x2, Pallas kernels, block_input_backward(): pl.pallas_call(functools.partial(backward_kernel, layer), out_shape=out_s...  161 us
    pallas_call x2, Pallas kernels, middle(): pl.pallas_call(functools.partial(middle_kernel, layer, not attended), out...  157 us
    pallas_call x1, Pallas kernels, block_rest(): pl.pallas_call(functools.partial(block_kernel, layer), out_shape=[jax.Sha...  130 us
    pallas_call x1, Pallas kernels, project(): pl.pallas_call(functools.partial(project_kernel, layer), out_shape=outs,...  49.5 us
    pallas_call x1, Pallas kernels, collect(): pl.pallas_call(functools.partial(collect_kernel, moves, steps), out_shape...  27.3 us

profile of v6, /device:TPU:81, one launch (start us, length us, event | category | flops | bytes accessed | tf_op | source)
XLA Modules:
  0.0 527.4 jit_solution(5904426436972246757)
XLA Ops:
  0.6 49.5 %project_0.1 = (bf16[2048,768]{1,0:T(8,128)(2,1)}, bf16[2048,1024]{1,0:T(8,128)(2,1)}, bf16[2048,1024]{1,0:T(8,128)(2,1)}, bf16[2048,1024]{1,0:T(8,128)(2,1)}, b...) custom-call(bf16[256,2048]{1,0:T(8,128)(2,1)} %x_hbm.3, f32[2,2048]{1,0:T(2,128)} %gain_ref.7, ...), custom_call_target="tpu_custom_call" | custom-call | tf_op jit(solution)/shard_map/project_0/pallas_call | solution.py:386
  50.1 130.3 %block_rest_0.1 = (bf16[256,2048]{1,0:T(8,128)(2,1)}, bf16[256,2048]{1,0:T(8,128)(2,1)}, bf16[2048,256]{1,0:T(8,128)(2,1)}, f32[2048,256]{1,0:T(8,128)}, bf16[20...) custom-call(bf16[2048,768]{1,0:T(8,128)(2,1)} %get-tuple-element.50.qkv_hbm, ...), custom_call_target="tpu_custom_call" | custom-call | tf_op jit(solution)/shard_map/block_rest_0/pallas_call | solution.py:648
  180.4 77.5 %middle_1.1 = (bf16[2048,1024]{1,0:T(8,128)(2,1)}, bf16[2048,1024]{1,0:T(8,128)(2,1)}, bf16[2048,768]{1,0:T(8,128)(2,1)}, bf16[8,256,2048]{2,1,0:T(8,128)(2,1)},...) custom-call(bf16[256,2048]{1,0:T(8,128)(2,1)} %dy_hbm.3, ...), custom_call_target="tpu_custom_call" | custom-call | tf_op jit(solution)/shard_map/middle_1/pallas_call | solution.py:1221
  257.9 77.7 %block_input_backward_1.1 = (bf16[256,2048]{1,0:T(8,128)(2,1)}, f32[1,2048]{1,0:T(1,128)}, bf16[2048,768]{1,0:T(8,128)(2,1)}, bf16[2048,1024]{1,0:T(8,128)(2,1)}, bf16[2048,1024]{1,0:T(8,128)(2,1)}) custom-call(bf16[2048,768]{1,0:T(8,128)(2,1)} %get-tuple-element.61.dqkv_hbm, bf16[2048,1024]{1,0:T(8,128)(2,1)} %get-tuple-element.62.dgate_hbm, ...), custom_call_target="tpu_custom_call" | custom-call | tf_op jit(solution)/shard_map/block_input_backward_1/pallas_call | solution.py:795
  335.6 79.9 %middle_0.1 = (bf16[2048,1024]{1,0:T(8,128)(2,1)}, bf16[2048,1024]{1,0:T(8,128)(2,1)}, bf16[2048,768]{1,0:T(8,128)(2,1)}, bf16[8,256,2048]{2,1,0:T(8,128)(2,1)},...) custom-call(bf16[256,2048]{1,0:T(8,128)(2,1)} %get-tuple-element.66.dy_hbm, ...), custom_call_target="tpu_custom_call" | custom-call | tf_op jit(solution)/shard_map/middle_0/pallas_call | solution.py:1221
  415.6 83.5 %block_input_backward_0.1 = (bf16[256,2048]{1,0:T(8,128)(2,1)}, f32[2,2048]{1,0:T(2,128)}, bf16[2048,768]{1,0:T(8,128)(2,1)}, bf16[2048,1024]{1,0:T(8,128)(2,1)}, bf16[2048,1024]{1,0:T(8,128)(2,1)}) custom-call(bf16[2048,768]{1,0:T(8,128)(2,1)} %get-tuple-element.72.dqkv_hbm, bf16[2048,1024]{1,0:T(8,128)(2,1)} %get-tuple-element.73.dgate_hbm, ...), custom_call_target="tpu_custom_call" | custom-call | tf_op jit(solution)/shard_map/block_input_backward_0/pallas_call | solution.py:795
  499.1 0.0 copy-start
  499.1 27.3 %collect.1 = (bf16[256,2048]{1,0:T(8,128)(2,1)}, bf16[2,256,2048]{2,1,0:T(8,128)(2,1)}, bf16[2,1024,2048]{2,1,0:T(8,128)(2,1)}, bf16[2,2048,768]{2,1,0:T(8,128)(...) custom-call(bf16[2048,2048]{1,0:T(8,128)(2,1)} %bitcast.4, ...), custom_call_target="tpu_custom_call" | custom-call | tf_op jit(solution)/shard_map/collect/pallas_call | solution.py:907
  526.4 0.0 copy-done
  526.4 0.6 copy.20
Async XLA Ops:
  499.1 27.3 %copy-start = (f32[2,2048]{1,0:T(2,128)S(1)}, f32[2,2048]{1,0:T(2,128)}, u32[]{:S(2)}) copy-start(f32[2,2048]{1,0:T(2,128)} %get-tuple-element.101) | copy-start | bytes 49156
